TPU v7x, 32 devices: a whole 2x2x4 slice. The times are simulated.
32 devices in a mesh: gx: 16 (over z, y, core), gy: 2 (over x).
Axes of the slice: x: 2, y: 2, z: 4, core: 2. Of those that a mesh axis runs over, the one named last changes fastest.
Arguments:
- solution_vector: float32 [3, 256, 32, 128], P(None, 'gx', 'gy'), may hold values from -1 to 3, as said below
- insulator_marker: int32 [256, 32, 128], P('gx', 'gy'), may hold values 0 or 1
- electrode_marker: int32 [256, 32, 128], P('gx', 'gy'), may hold values 0 or 1
- impurity_zone_index: int32 [64, 8, 32], P('gx', 'gy'), may hold values from 0 to 3
- conductivity_category: int32 [64, 8, 32], P('gx', 'gy'), may hold values from 0 to 3
- warmth_rise: float32 [64, 8, 32], P('gx', 'gy'), may hold values from 0 to 2
Outputs:
- new_state: float32 [3, 256, 32, 128], P(None, 'gx', 'gy')
- new_temperature: float32 [64, 8, 32], P('gx', 'gy')
Inputs may be any that keep to these rules, and one draw needn't show every extreme that they name: `solution_vector`: channel 0 is the potential; channels 1 and 2 are the electron and hole densities, which are positive.
All inputs are finite; a program needn't handle non-finite values. No bound on the sum of `insulator_marker` or of `electrode_marker` on one device may be relied on, other than what follows from the above.
Results may differ from a plain program's by a relative error of at most 0.0003.
Values sent between devices are 32-bit elements; how exact they have to be, the bound alone decides.
No kernel may reach another device: no remote copies, remote signals or barrier semaphores. Data moves between devices by JAX's collectives and lax.ppermute only.
A program may use at most 64 MiB of HBM per device.

v0:
```python
import jax
import jax.numpy as jnp
from jax import lax
from jax.sharding import PartitionSpec as P

COARSEN_RATIO = 4
NEWTON = 3
SWEEPS = 3


poisson_scale = 2.0
charge_scale = 4.0
clock_offset = 24.0
contact_bias = 0.25
heat_gain = 1.0
sink_rate = 0.3
speed_falloff = 0.5
dope_table = (-2.0, -0.5, 0.5, 2.0)
conduct_table = (0.5, 1.0, 2.0, 4.0)


def extended(block, sides, width):
    for axis, dim in sides:
        count = lax.axis_size(axis)
        forward = [(i, i + 1) for i in range(count - 1)]
        backward = [(target, source) for source, target in forward]
        low = lax.ppermute(
            lax.slice_in_dim(block, block.shape[dim] - width, None, axis=dim), axis, forward
        )
        high = lax.ppermute(lax.slice_in_dim(block, 0, width, axis=dim), axis, backward)
        block = jnp.concatenate([low, block, high], axis=dim)
    return block


def bernoulli(value):
    tiny = jnp.abs(value) < 0.0001
    safe = jnp.where(tiny, 1.0, jnp.expm1(value))
    return jnp.where(tiny, 1.0 - 0.5 * value, value / safe)


def bernoulli_slope(value):
    tiny = jnp.abs(value) < 0.05
    safe = jnp.where(tiny, 1.0, jnp.expm1(value))
    exact = (safe - value * jnp.exp(value)) / (safe * safe)
    series = -0.5 + value / 6.0 - value * value * value / 180.0
    return jnp.where(tiny, series, exact)


def neighbours(framed_array):
    return [
        framed_array[..., 2:, 1:-1, 1:-1],
        framed_array[..., :-2, 1:-1, 1:-1],
        framed_array[..., 1:-1, 2:, 1:-1],
        framed_array[..., 1:-1, :-2, 1:-1],
        framed_array[..., 1:-1, 1:-1, 2:],
        framed_array[..., 1:-1, 1:-1, :-2],
    ]


def centre(framed_array):
    return framed_array[..., 1:-1, 1:-1, 1:-1]


def lookup(labels, table):
    result = jnp.zeros(labels.shape, jnp.float32)
    for level, amount in enumerate(table):
        result = result + jnp.where(labels == level, amount, 0.0)
    return result


def refine_warmth(coarse):
    lattice_span = coarse.shape
    spread = jnp.broadcast_to(
        coarse[:, None, :, None, :, None],
        (
            lattice_span[0],
            COARSEN_RATIO,
            lattice_span[1],
            COARSEN_RATIO,
            lattice_span[2],
            COARSEN_RATIO,
        ),
    )
    return spread.reshape(
        lattice_span[0] * COARSEN_RATIO,
        lattice_span[1] * COARSEN_RATIO,
        lattice_span[2] * COARSEN_RATIO,
    )


def restrict(fine):
    lattice_span = fine.shape
    blocks = fine.reshape(
        lattice_span[0] // COARSEN_RATIO,
        COARSEN_RATIO,
        lattice_span[1] // COARSEN_RATIO,
        COARSEN_RATIO,
        lattice_span[2] // COARSEN_RATIO,
        COARSEN_RATIO,
    )
    return jnp.mean(blocks, axis=(1, 3, 5))


def relax_weight(framed_array, warming_input, caloric_transfer):
    total = sum(neighbours(framed_array))
    return (warming_input + caloric_transfer * total) / (sink_rate + 6.0 * caloric_transfer)


def framed_layers(array):
    widths = [(0, 0)] * (array.ndim - 1) + [(1, 1)]
    return jnp.pad(array, widths)


def linearized_correction(
    framed_array,
    permittivity_framed,
    interior_frame_mask,
    impurity_profile,
    electrode_active,
    species_drift_speed,
):
    voltage_field = centre(framed_array[0])
    negative_density = centre(framed_array[1])
    positive_density = centre(framed_array[2])
    eps_here = centre(permittivity_framed)
    lap_sum = jnp.zeros_like(voltage_field)
    face_sum = jnp.zeros_like(voltage_field)
    negative_current = jnp.zeros_like(voltage_field)
    positive_current = jnp.zeros_like(voltage_field)
    negative_gradient = jnp.zeros_like(voltage_field)
    positive_gradient = jnp.zeros_like(voltage_field)
    backward_scharfetter = jnp.zeros_like(voltage_field)
    forward_scharfetter = jnp.zeros_like(voltage_field)
    ohmic_dissipation = jnp.zeros_like(voltage_field)
    parts = zip(
        neighbours(framed_array[0]),
        neighbours(framed_array[1]),
        neighbours(framed_array[2]),
        neighbours(permittivity_framed),
        neighbours(interior_frame_mask),
    )
    for pot_near, elec_near, hole_near, eps_near, weight in parts:
        drop = pot_near - voltage_field
        plus = bernoulli(drop)
        minus = bernoulli(-drop)
        slope_plus = bernoulli_slope(drop)
        slope_minus = bernoulli_slope(-drop)
        face = weight * 0.5 * (eps_here + eps_near)
        lap_sum = lap_sum + face * drop
        face_sum = face_sum + face
        elec_flow = weight * (elec_near * plus - negative_density * minus)
        hole_flow = weight * (hole_near * minus - positive_density * plus)
        negative_current = negative_current + elec_flow
        positive_current = positive_current + hole_flow
        ohmic_dissipation = ohmic_dissipation + (elec_flow - hole_flow) * (elec_flow - hole_flow)
        negative_gradient = negative_gradient + weight * (
            -elec_near * slope_plus - negative_density * slope_minus
        )
        positive_gradient = positive_gradient + weight * (
            hole_near * slope_minus + positive_density * slope_plus
        )
        backward_scharfetter = backward_scharfetter + weight * minus
        forward_scharfetter = forward_scharfetter + weight * plus
    denom = negative_density + positive_density + 2.0
    annihilation_rate = (negative_density * positive_density - 1.0) / denom
    negative_generation = (positive_density + 1.0) * (positive_density + 1.0) / (denom * denom)
    positive_generation = (negative_density + 1.0) * (negative_density + 1.0) / (denom * denom)
    res_psi = poisson_scale * lap_sum + charge_scale * (
        positive_density - negative_density + impurity_profile
    )
    negative_mismatch = species_drift_speed * negative_current - annihilation_rate
    positive_mismatch = species_drift_speed * positive_current - annihilation_rate
    blank_array = jnp.zeros_like(voltage_field)
    unit_array = jnp.ones_like(voltage_field)
    res_psi = jnp.where(electrode_active, voltage_field - contact_bias * impurity_profile, res_psi)
    negative_mismatch = jnp.where(electrode_active, negative_density - 1.0, negative_mismatch)
    positive_mismatch = jnp.where(electrode_active, positive_density - 1.0, positive_mismatch)
    mat_aa = jnp.where(electrode_active, unit_array, -poisson_scale * face_sum)
    mat_ab = jnp.where(electrode_active, blank_array, -charge_scale * unit_array)
    mat_ac = jnp.where(electrode_active, blank_array, charge_scale * unit_array)
    jacobian_entry_second_first = jnp.where(
        electrode_active, blank_array, species_drift_speed * negative_gradient
    )
    jacobian_entry_second_second = jnp.where(
        electrode_active,
        unit_array,
        -species_drift_speed * backward_scharfetter - negative_generation - clock_offset,
    )
    mat_bc = jnp.where(electrode_active, blank_array, -positive_generation)
    jacobian_entry_third_first = jnp.where(
        electrode_active, blank_array, species_drift_speed * positive_gradient
    )
    mat_cb = jnp.where(electrode_active, blank_array, -negative_generation)
    jacobian_entry_third_third = jnp.where(
        electrode_active,
        unit_array,
        -species_drift_speed * forward_scharfetter - positive_generation - clock_offset,
    )
    cof_aa = jacobian_entry_second_second * jacobian_entry_third_third - mat_bc * mat_cb
    cof_ab = (
        mat_bc * jacobian_entry_third_first
        - jacobian_entry_second_first * jacobian_entry_third_third
    )
    cof_ac = (
        jacobian_entry_second_first * mat_cb
        - jacobian_entry_second_second * jacobian_entry_third_first
    )
    determ = mat_aa * cof_aa + mat_ab * cof_ab + mat_ac * cof_ac
    step_psi = (
        cof_aa * res_psi
        + (mat_ac * mat_cb - mat_ab * jacobian_entry_third_third) * negative_mismatch
        + (mat_ab * mat_bc - mat_ac * jacobian_entry_second_second) * positive_mismatch
    ) / determ
    step_n = (
        cof_ab * res_psi
        + (mat_aa * jacobian_entry_third_third - mat_ac * jacobian_entry_third_first)
        * negative_mismatch
        + (mat_ac * jacobian_entry_second_first - mat_aa * mat_bc) * positive_mismatch
    ) / determ
    step_p = (
        cof_ac * res_psi
        + (mat_ab * jacobian_entry_third_first - mat_aa * mat_cb) * negative_mismatch
        + (mat_aa * jacobian_entry_second_second - mat_ab * jacobian_entry_second_first)
        * positive_mismatch
    ) / determ
    new_pot = voltage_field - step_psi
    new_elec = negative_density * jnp.exp(-step_n / negative_density)
    new_hole = positive_density * jnp.exp(-step_p / positive_density)
    warming_field = (
        0.5 * species_drift_speed * ohmic_dissipation / (negative_density + positive_density)
    )
    return (jnp.stack([new_pot, new_elec, new_hole], 0), warming_field)


def inside(count, position, devices):
    first = position * count - 1 + jnp.arange(count + 2, dtype=jnp.int32)
    return ((first >= 0) & (first < count * devices)).astype(jnp.float32)


def inside_wide(count, position, devices, margin):
    first = position * count - margin + jnp.arange(count + 2 * margin, dtype=jnp.int32)
    return ((first >= 0) & (first < count * devices)).astype(jnp.float32)


def per_device(
    solution_vector,
    insulator_marker,
    electrode_marker,
    impurity_zone_index,
    conductivity_category,
    warmth_rise,
):
    rows_x = solution_vector.shape[1]
    rows_y = solution_vector.shape[2]
    depth = solution_vector.shape[3]
    eps = jnp.where(insulator_marker == 1, 0.4, 1.0).astype(jnp.float32)
    valid_x = inside(rows_x, lax.axis_index("gx"), lax.axis_size("gx"))
    valid_y = inside(rows_y, lax.axis_index("gy"), lax.axis_size("gy"))
    valid_z = jnp.pad(jnp.ones((depth,), jnp.float32), 1)
    interior_frame_mask = valid_x[:, None, None] * valid_y[None, :, None] * valid_z[None, None, :]
    impurity_profile = refine_warmth(lookup(impurity_zone_index, dope_table))
    caloric_transfer = lookup(conductivity_category, conduct_table)
    electrode_active = electrode_marker == 1
    cells_x = warmth_rise.shape[0]
    cells_y = warmth_rise.shape[1]
    cell_mask_x = inside_wide(cells_x, lax.axis_index("gx"), lax.axis_size("gx"), SWEEPS)
    cell_mask_y = inside_wide(cells_y, lax.axis_index("gy"), lax.axis_size("gy"), SWEEPS)
    cell_mask = cell_mask_x[:, None, None] * cell_mask_y[None, :, None]
    for newton_step in range(NEWTON):
        pointwise_warmth = warmth_rise
        species_drift_speed = 1.0 / (1.0 + speed_falloff * refine_warmth(pointwise_warmth))
        stacked = jnp.concatenate([solution_vector, eps[None]], 0)
        padded_all = framed_layers(extended(stacked, (("gx", 1), ("gy", 2)), 1))
        framed_array = padded_all[:3]
        permittivity_framed = padded_all[3]
        solution_vector, warming_field = linearized_correction(
            framed_array,
            permittivity_framed,
            interior_frame_mask,
            impurity_profile,
            electrode_active,
            species_drift_speed,
        )
        warming_input = heat_gain * restrict(warming_field)
        packed = jnp.stack([warmth_rise, warming_input, caloric_transfer], 0)
        widened = extended(packed, (("gx", 1), ("gy", 2)), SWEEPS)
        temp_wide = widened[0]
        source_wide = widened[1]
        cond_wide = widened[2]
        mask_wide = cell_mask
        for sweep in range(SWEEPS):
            source_wide = source_wide[1:-1, 1:-1]
            cond_wide = cond_wide[1:-1, 1:-1]
            mask_wide = mask_wide[1:-1, 1:-1]
            temp_wide = relax_weight(framed_layers(temp_wide), source_wide, cond_wide) * mask_wide
        warmth_rise = temp_wide
    return (solution_vector, warmth_rise)


def solution(mesh):
    placed = (
        P(None, "gx", "gy", None),
        P("gx", "gy", None),
        P("gx", "gy", None),
        P("gx", "gy", None),
        P("gx", "gy", None),
        P("gx", "gy", None),
    )
    return jax.shard_map(
        per_device,
        mesh=mesh,
        in_specs=placed,
        out_specs=(P(None, "gx", "gy", None), P("gx", "gy", None)),
        check_vma=False,
    )
```

profile of v0, /device:TPU:9, one launch (start us, length us, event | category | flops | bytes accessed | tf_op | source)
XLA Modules:
  0.0 162.6 jit_solution(13985735775680334527)
XLA Ops:
  2.3 2.6 %collective-permute-start.1 = (f32[4,1,16,128]{3,2,1,0:T(8,128)S(1)}, f32[4,1,16,128]{3,2,1,0:T(8,128)S(1)}, u32[]{:S(2)}, u32[]{:S(2)}) collective-permute-start(f32[4,1,16,128]{3,2,1,0:T(8,128)S(1)} %get-tuple-element.119), channel_id=1, source_target_pairs={{2,0},{4,2},{6,4},{8,6},{10,8},{12,10},{14,12},{16,14},{18,16},{20... | collective-permute-start | bytes 98312 | tf_op jit(solution)/shard_map/ppermute | solution.py:30
  4.9 3.0 %collective-permute-start = (f32[4,1,16,128]{3,2,1,0:T(8,128)S(1)}, f32[4,1,16,128]{3,2,1,0:T(8,128)S(1)}, u32[]{:S(2)}, u32[]{:S(2)}) collective-permute-start(f32[4,1,16,128]{3,2,1,0:T(8,128)S(1)} %get-tuple-element.118), channel_id=1, source_target_pairs={{0,2},{2,4},{4,6},{6,8},{8,10},{10,12},{12,14},{14,16},{16,18},{18... | collective-permute-start | bytes 98312 | tf_op jit(solution)/shard_map/ppermute | solution.py:27
  13.0 4.0 %collective-permute-start.2 = (f32[4,18,1,128]{3,2,1,0:T(1,128)S(1)}, f32[4,18,1,128]{3,2,1,0:T(1,128)S(1)}, u32[]{:S(2)}, u32[]{:S(2)}) collective-permute-start(f32[4,18,1,128]{3,2,1,0:T(1,128)S(1)} %get-tuple-element.112), channel_id=1, source_target_pairs={{0,1},{2,3},{4,5},{6,7},{8,9},{10,11},{12,13},{14,15},{16,17},{18,... | collective-permute-start | bytes 110600 | tf_op jit(solution)/shard_map/ppermute | solution.py:27
  17.1 2.6 %broadcast_in_dim.152 = f32[4,4,4,4,32,4]{5,4,3,2,1,0:T(8,128)} broadcast(f32[4,4,32]{2,1,0:T(4,128)S(1)} %add_divide_fusion.5), dimensions={0,2,4} | broadcast | bytes 133120 | tf_op jit(solution)/shard_map/broadcast_in_dim | solution.py:73
  19.7 4.9 %div.577 = f32[16,16,128]{2,1,0:T(8,128)S(1)} reshape(f32[4,4,4,4,32,4]{5,4,3,2,1,0:T(8,128)} %broadcast_in_dim.152) | data formatting | bytes 262144 | tf_op jit(solution)/shard_map/div | solution.py:271
  24.5 2.6 %broadcast_in_dim.158 = f32[4,4,4,4,32,4]{5,4,3,2,1,0:T(8,128)} broadcast(f32[4,4,32]{2,1,0:T(4,128)S(1)} %select_add_fusion), dimensions={0,2,4} | broadcast | bytes 133120 | tf_op jit(solution)/shard_map/broadcast_in_dim | solution.py:73
  27.1 4.9 %reshape.181 = f32[16,16,128]{2,1,0:T(8,128)S(1)} reshape(f32[4,4,4,4,32,4]{5,4,3,2,1,0:T(8,128)} %broadcast_in_dim.158) | data formatting | bytes 262144 | tf_op jit(solution)/shard_map/reshape | solution.py:84
  32.7 2.7 %multiply_divide_fusion.6 = (f32[16,16,128]{2,1,0:T(8,128)S(1)}, f32[16,16,128]{2,1,0:T(8,128)S(1)}, f32[16,16,128]{2,1,0:T(8,128)S(1)}, f32[16,16,128]{2,1,0:T(...) fusion(f32[16,16,128]{2,1,0:T(8,128)S(1)} %div.577, ...), kind=kLoop, calls=%fused_computation.707 | loop fusion | flops 5406720 | bytes 6160384 | tf_op jit(solution)/shard_map/div | solution.py:230
  35.4 5.7 %reshape.182 = f32[4,4,4,4,32,4]{5,4,3,2,1,0:T(8,128)} reshape(f32[16,16,128]{2,1,0:T(8,128)S(1)} %get-tuple-element.59) | data formatting | bytes 262144 | tf_op jit(solution)/shard_map/reshape | solution.py:93
  41.1 2.6 %reduce_sum.27 = f32[4,4,32]{2,1,0:T(4,128)S(1)} reduce(f32[4,4,4,4,32,4]{5,4,3,2,1,0:T(8,128)} %reshape.182, f32[]{:T(128)} %constant.150.clone.1), dimensions={1,3,5}, to_apply=%region_0.1 | reduce | flops 32256 | bytes 133124 | tf_op jit(solution)/shard_map/reduce_sum | solution.py:101
  43.7 3.7 %collective-permute-start.9 = (f32[3,3,4,32]{3,2,1,0:T(4,128)S(1)}, f32[3,3,4,32]{3,2,1,0:T(4,128)S(1)}, u32[]{:S(2)}, u32[]{:S(2)}) collective-permute-start(f32[3,3,4,32]{3,2,1,0:T(4,128)S(1)} %get-tuple-element.146), channel_id=1, source_target_pairs={{2,0},{4,2},{6,4},{8,6},{10,8},{12,10},{14,12},{16,14},{18,16},{20... | collective-permute-start | bytes 13832 | tf_op jit(solution)/shard_map/ppermute | solution.py:30
  49.4 4.5 %fusion.383 = (f32[1,16,16,128]{3,2,1,0:T(8,128)S(1)}, f32[16,16,128]{2,1,0:T(8,128)S(1)}, f32[16,16,128]{2,1,0:T(8,128)S(1)}, f32[16,16,128]{2,1,0:T(8,128)S(1)...) fusion(f32[18,18,130]{2,1,0:T(8,128)S(1)} %get-tuple-element.10, ...), kind=kLoop, calls=%fused_computation.747 | loop fusion | flops 14647296 | bytes 7897088 | tf_op jit(solution)/shard_map/stack | solution.py:232
  55.7 4.0 %collective-permute-start.10 = (f32[3,10,3,32]{3,2,1,0:T(4,128)S(1)}, f32[3,10,3,32]{3,2,1,0:T(4,128)S(1)}, u32[]{:S(2)}, u32[]{:S(2)}) collective-permute-start(f32[3,10,3,32]{3,2,1,0:T(4,128)S(1)} %get-tuple-element.139), channel_id=1, source_target_pairs={{0,1},{2,3},{4,5},{6,7},{8,9},{10,11},{12,13},{14,15},{16,17},{18,... | collective-permute-start | bytes 34568 | tf_op jit(solution)/shard_map/ppermute | solution.py:27
  59.7 3.0 %collective-permute-start.5 = (f32[4,1,16,128]{3,2,1,0:T(8,128)S(1)}, f32[4,1,16,128]{3,2,1,0:T(8,128)S(1)}, u32[]{:S(2)}, u32[]{:S(2)}) collective-permute-start(f32[4,1,16,128]{3,2,1,0:T(8,128)S(1)} %get-tuple-element.117), channel_id=1, source_target_pairs={{2,0},{4,2},{6,4},{8,6},{10,8},{12,10},{14,12},{16,14},{18,16},{20... | collective-permute-start | bytes 98312 | tf_op jit(solution)/shard_map/ppermute | solution.py:30
  68.8 4.2 %collective-permute-start.6 = (f32[4,18,1,128]{3,2,1,0:T(1,128)S(1)}, f32[4,18,1,128]{3,2,1,0:T(1,128)S(1)}, u32[]{:S(2)}, u32[]{:S(2)}) collective-permute-start(f32[4,18,1,128]{3,2,1,0:T(1,128)S(1)} %get-tuple-element.110), channel_id=1, source_target_pairs={{0,1},{2,3},{4,5},{6,7},{8,9},{10,11},{12,13},{14,15},{16,17},{18,... | collective-permute-start | bytes 110600 | tf_op jit(solution)/shard_map/ppermute | solution.py:27
  73.1 2.6 %broadcast_in_dim.160 = f32[4,4,4,4,32,4]{5,4,3,2,1,0:T(8,128)} broadcast(f32[4,4,32]{2,1,0:T(4,128)S(1)} %get-tuple-element.57), dimensions={0,2,4} | broadcast | bytes 133120 | tf_op jit(solution)/shard_map/broadcast_in_dim | solution.py:73
  75.6 4.9 %div.641 = f32[16,16,128]{2,1,0:T(8,128)S(1)} reshape(f32[4,4,4,4,32,4]{5,4,3,2,1,0:T(8,128)} %broadcast_in_dim.160) | data formatting | bytes 262144 | tf_op jit(solution)/shard_map/div | solution.py:271
  81.5 3.5 %fusion.382 = (f32[1,16,16,128]{3,2,1,0:T(8,128)S(1)}, f32[16,16,128]{2,1,0:T(8,128)S(1)}, f32[16,16,128]{2,1,0:T(8,128)S(1)}, f32[16,16,128]{2,1,0:T(8,128)S(1)...) fusion(pred[16,16,128]{2,1,0:T(8,128)(4,1)S(1)} %get-tuple-elem, ...), kind=kLoop, calls=%fused_computation.746 | loop fusion | flops 16187392 | bytes 7766016 | tf_op jit(solution)/shard_map/stack | solution.py:232
  85.7 6.5 %reshape.183 = f32[4,4,4,4,32,4]{5,4,3,2,1,0:T(8,128)} reshape(f32[16,16,128]{2,1,0:T(8,128)} %multiply_divide_fusion.3) | data formatting | bytes 262144 | tf_op jit(solution)/shard_map/reshape | solution.py:93
  92.2 2.6 %reduce_sum.28 = f32[4,4,32]{2,1,0:T(4,128)S(1)} reduce(f32[4,4,4,4,32,4]{5,4,3,2,1,0:T(8,128)} %reshape.183, f32[]{:T(128)} %constant.150.clone.1), dimensions={1,3,5}, to_apply=%region_1.2 | reduce | flops 32256 | bytes 133124 | tf_op jit(solution)/shard_map/reduce_sum | solution.py:101
  94.9 6.0 %collective-permute-start.17 = (f32[3,3,4,32]{3,2,1,0:T(4,128)S(1)}, f32[3,3,4,32]{3,2,1,0:T(4,128)S(1)}, u32[]{:S(2)}, u32[]{:S(2)}) collective-permute-start(f32[3,3,4,32]{3,2,1,0:T(4,128)S(1)} %get-tuple-element.144), channel_id=1, source_target_pairs={{2,0},{4,2},{6,4},{8,6},{10,8},{12,10},{14,12},{16,14},{18,16},{20... | collective-permute-start | bytes 13832 | tf_op jit(solution)/shard_map/ppermute | solution.py:30
  105.3 4.0 %collective-permute-start.18 = (f32[3,10,3,32]{3,2,1,0:T(4,128)S(1)}, f32[3,10,3,32]{3,2,1,0:T(4,128)S(1)}, u32[]{:S(2)}, u32[]{:S(2)}) collective-permute-start(f32[3,10,3,32]{3,2,1,0:T(4,128)S(1)} %get-tuple-element.137), channel_id=1, source_target_pairs={{0,1},{2,3},{4,5},{6,7},{8,9},{10,11},{12,13},{14,15},{16,17},{18,... | collective-permute-start | bytes 34568 | tf_op jit(solution)/shard_map/ppermute | solution.py:27
  109.3 5.4 %collective-permute-start.13 = (f32[4,1,16,128]{3,2,1,0:T(8,128)S(1)}, f32[4,1,16,128]{3,2,1,0:T(8,128)S(1)}, u32[]{:S(2)}, u32[]{:S(2)}) collective-permute-start(f32[4,1,16,128]{3,2,1,0:T(8,128)S(1)} %get-tuple-element.115), channel_id=1, source_target_pairs={{2,0},{4,2},{6,4},{8,6},{10,8},{12,10},{14,12},{16,14},{18,16},{20... | collective-permute-start | bytes 98312 | tf_op jit(solution)/shard_map/ppermute | solution.py:30
  119.2 4.2 %collective-permute-start.14 = (f32[4,18,1,128]{3,2,1,0:T(1,128)S(1)}, f32[4,18,1,128]{3,2,1,0:T(1,128)S(1)}, u32[]{:S(2)}, u32[]{:S(2)}) collective-permute-start(f32[4,18,1,128]{3,2,1,0:T(1,128)S(1)} %get-tuple-element.108), channel_id=1, source_target_pairs={{0,1},{2,3},{4,5},{6,7},{8,9},{10,11},{12,13},{14,15},{16,17},{18,... | collective-permute-start | bytes 110600 | tf_op jit(solution)/shard_map/ppermute | solution.py:27
  123.5 2.6 %broadcast_in_dim.161 = f32[4,4,4,4,32,4]{5,4,3,2,1,0:T(8,128)} broadcast(f32[4,4,32]{2,1,0:T(4,128)S(1)} %get-tuple-element.55), dimensions={0,2,4} | broadcast | bytes 133120 | tf_op jit(solution)/shard_map/broadcast_in_dim | solution.py:73
  126.1 4.9 %div.705 = f32[16,16,128]{2,1,0:T(8,128)S(1)} reshape(f32[4,4,4,4,32,4]{5,4,3,2,1,0:T(8,128)} %broadcast_in_dim.161) | data formatting | bytes 262144 | tf_op jit(solution)/shard_map/div | solution.py:271
  131.7 2.7 %multiply_divide_fusion = (f32[16,16,128]{2,1,0:T(8,128)S(1)}, f32[16,16,128]{2,1,0:T(8,128)S(1)}, f32[16,16,128]{2,1,0:T(8,128)S(1)}, f32[16,16,128]{2,1,0:T(8,...) fusion(f32[16,16,128]{2,1,0:T(8,128)S(1)} %div.705, ...), kind=kLoop, calls=%fused_computation.633 | loop fusion | flops 5406720 | bytes 6160384 | tf_op jit(solution)/shard_map/div | solution.py:230
  134.4 5.7 %reshape.184 = f32[4,4,4,4,32,4]{5,4,3,2,1,0:T(8,128)} reshape(f32[16,16,128]{2,1,0:T(8,128)S(1)} %get-tuple-element.2) | data formatting | bytes 262144 | tf_op jit(solution)/shard_map/reshape | solution.py:93
  140.0 2.6 %reduce_sum.29 = f32[4,4,32]{2,1,0:T(4,128)S(1)} reduce(f32[4,4,4,4,32,4]{5,4,3,2,1,0:T(8,128)} %reshape.184, f32[]{:T(128)} %constant.150.clone.1), dimensions={1,3,5}, to_apply=%region_2.3 | reduce | flops 32256 | bytes 133124 | tf_op jit(solution)/shard_map/reduce_sum | solution.py:101
  142.7 5.5 %collective-permute-start.21 = (f32[3,3,4,32]{3,2,1,0:T(4,128)S(1)}, f32[3,3,4,32]{3,2,1,0:T(4,128)S(1)}, u32[]{:S(2)}, u32[]{:S(2)}) collective-permute-start(f32[3,3,4,32]{3,2,1,0:T(4,128)S(1)} %get-tuple-element.142), channel_id=1, source_target_pairs={{2,0},{4,2},{6,4},{8,6},{10,8},{12,10},{14,12},{16,14},{18,16},{20... | collective-permute-start | bytes 13832 | tf_op jit(solution)/shard_map/ppermute | solution.py:30
  150.1 4.5 %fusion.381 = (f32[1,16,16,128]{3,2,1,0:T(8,128)S(1)}, f32[16,16,128]{2,1,0:T(8,128)S(1)}, f32[16,16,128]{2,1,0:T(8,128)S(1)}, f32[16,16,128]{2,1,0:T(8,128)S(1)...) fusion(pred[16,16,128]{2,1,0:T(8,128)(4,1)S(1)} %get-tuple-elem, ...), kind=kLoop, calls=%fused_computation.745 | loop fusion | flops 14614528 | bytes 7766016 | tf_op jit(solution)/shard_map/stack | solution.py:232
  156.3 4.0 %collective-permute-start.22 = (f32[3,10,3,32]{3,2,1,0:T(4,128)S(1)}, f32[3,10,3,32]{3,2,1,0:T(4,128)S(1)}, u32[]{:S(2)}, u32[]{:S(2)}) collective-permute-start(f32[3,10,3,32]{3,2,1,0:T(4,128)S(1)} %get-tuple-element.135), channel_id=1, source_target_pairs={{0,1},{2,3},{4,5},{6,7},{8,9},{10,11},{12,13},{14,15},{16,17},{18,... | collective-permute-start | bytes 34568 | tf_op jit(solution)/shard_map/ppermute | solution.py:27
  (106 shorter events, 34.5 us)
Async XLA Ops:
  2.3 8.3 %collective-permute-start.1 = (f32[4,1,16,128]{3,2,1,0:T(8,128)S(1)}, f32[4,1,16,128]{3,2,1,0:T(8,128)S(1)}, u32[]{:S(2)}, u32[]{:S(2)}) collective-permute-start(f32[4,1,16,128]{3,2,1,0:T(8,128)S(1)} %get-tuple-element.119), channel_id=1, source_target_pairs={{2,0},{4,2},{6,4},{8,6},{10,8},{12,10},{14,12},{16,14},{18,16},{20... | collective-permute-start | bytes 98312 | tf_op jit(solution)/shard_map/ppermute | solution.py:30
  4.9 5.7 %collective-permute-start = (f32[4,1,16,128]{3,2,1,0:T(8,128)S(1)}, f32[4,1,16,128]{3,2,1,0:T(8,128)S(1)}, u32[]{:S(2)}, u32[]{:S(2)}) collective-permute-start(f32[4,1,16,128]{3,2,1,0:T(8,128)S(1)} %get-tuple-element.118), channel_id=1, source_target_pairs={{0,2},{2,4},{4,6},{6,8},{8,10},{10,12},{12,14},{14,16},{16,18},{18... | collective-permute-start | bytes 98312 | tf_op jit(solution)/shard_map/ppermute | solution.py:27
  11.7 20.3 %collective-permute-start.3 = (f32[4,18,1,128]{3,2,1,0:T(1,128)S(1)}, f32[4,18,1,128]{3,2,1,0:T(1,128)S(1)}, u32[]{:S(2)}, u32[]{:S(2)}) collective-permute-start(f32[4,18,1,128]{3,2,1,0:T(1,128)S(1)} %get-tuple-element.113), channel_id=1, source_target_pairs={{1,0},{3,2},{5,4},{7,6},{9,8},{11,10},{13,12},{15,14},{17,16},{19,... | collective-permute-start | bytes 110600 | tf_op jit(solution)/shard_map/ppermute | solution.py:30
  13.0 19.0 %collective-permute-start.2 = (f32[4,18,1,128]{3,2,1,0:T(1,128)S(1)}, f32[4,18,1,128]{3,2,1,0:T(1,128)S(1)}, u32[]{:S(2)}, u32[]{:S(2)}) collective-permute-start(f32[4,18,1,128]{3,2,1,0:T(1,128)S(1)} %get-tuple-element.112), channel_id=1, source_target_pairs={{0,1},{2,3},{4,5},{6,7},{8,9},{10,11},{12,13},{14,15},{16,17},{18,... | collective-permute-start | bytes 110600 | tf_op jit(solution)/shard_map/ppermute | solution.py:27
  27.1 4.9 %copy-start = (f32[3,16,16,128]{3,2,1,0:T(8,128)S(1)}, f32[3,16,16,128]{3,2,1,0:T(8,128)}, u32[]{:S(2)}) copy-start(f32[3,16,16,128]{3,2,1,0:T(8,128)} %param.6) | copy-start | bytes 1179652
  41.1 2.6 %copy-start.1 = (f32[4,4,32]{2,1,0:T(4,128)S(1)}, f32[4,4,32]{2,1,0:T(4,128)}, u32[]{:S(2)}) copy-start(f32[4,4,32]{2,1,0:T(4,128)} %param.11) | copy-start | bytes 6148
  43.7 10.5 %collective-permute-start.9 = (f32[3,3,4,32]{3,2,1,0:T(4,128)S(1)}, f32[3,3,4,32]{3,2,1,0:T(4,128)S(1)}, u32[]{:S(2)}, u32[]{:S(2)}) collective-permute-start(f32[3,3,4,32]{3,2,1,0:T(4,128)S(1)} %get-tuple-element.146), channel_id=1, source_target_pairs={{2,0},{4,2},{6,4},{8,6},{10,8},{12,10},{14,12},{16,14},{18,16},{20... | collective-permute-start | bytes 13832 | tf_op jit(solution)/shard_map/ppermute | solution.py:30
  47.5 6.8 %collective-permute-start.8 = (f32[3,3,4,32]{3,2,1,0:T(4,128)S(1)}, f32[3,3,4,32]{3,2,1,0:T(4,128)S(1)}, u32[]{:S(2)}, u32[]{:S(2)}) collective-permute-start(f32[3,3,4,32]{3,2,1,0:T(4,128)S(1)} %get-tuple-element.145), channel_id=1, source_target_pairs={{0,2},{2,4},{4,6},{6,8},{8,10},{10,12},{12,14},{14,16},{16,18},{18... | collective-permute-start | bytes 13832 | tf_op jit(solution)/shard_map/ppermute | solution.py:27
  54.4 10.9 %collective-permute-start.11 = (f32[3,10,3,32]{3,2,1,0:T(4,128)S(1)}, f32[3,10,3,32]{3,2,1,0:T(4,128)S(1)}, u32[]{:S(2)}, u32[]{:S(2)}) collective-permute-start(f32[3,10,3,32]{3,2,1,0:T(4,128)S(1)} %get-tuple-element.140), channel_id=1, source_target_pairs={{1,0},{3,2},{5,4},{7,6},{9,8},{11,10},{13,12},{15,14},{17,16},{19,... | collective-permute-start | bytes 34568 | tf_op jit(solution)/shard_map/ppermute | solution.py:30
  55.7 9.6 %collective-permute-start.10 = (f32[3,10,3,32]{3,2,1,0:T(4,128)S(1)}, f32[3,10,3,32]{3,2,1,0:T(4,128)S(1)}, u32[]{:S(2)}, u32[]{:S(2)}) collective-permute-start(f32[3,10,3,32]{3,2,1,0:T(4,128)S(1)} %get-tuple-element.139), channel_id=1, source_target_pairs={{0,1},{2,3},{4,5},{6,7},{8,9},{10,11},{12,13},{14,15},{16,17},{18,... | collective-permute-start | bytes 34568 | tf_op jit(solution)/shard_map/ppermute | solution.py:27
  59.7 5.9 %collective-permute-start.5 = (f32[4,1,16,128]{3,2,1,0:T(8,128)S(1)}, f32[4,1,16,128]{3,2,1,0:T(8,128)S(1)}, u32[]{:S(2)}, u32[]{:S(2)}) collective-permute-start(f32[4,1,16,128]{3,2,1,0:T(8,128)S(1)} %get-tuple-element.117), channel_id=1, source_target_pairs={{2,0},{4,2},{6,4},{8,6},{10,8},{12,10},{14,12},{16,14},{18,16},{20... | collective-permute-start | bytes 98312 | tf_op jit(solution)/shard_map/ppermute | solution.py:30
  62.7 4.7 %collective-permute-start.4 = (f32[4,1,16,128]{3,2,1,0:T(8,128)S(1)}, f32[4,1,16,128]{3,2,1,0:T(8,128)S(1)}, u32[]{:S(2)}, u32[]{:S(2)}) collective-permute-start(f32[4,1,16,128]{3,2,1,0:T(8,128)S(1)} %get-tuple-element.116), channel_id=1, source_target_pairs={{0,2},{2,4},{4,6},{6,8},{8,10},{10,12},{12,14},{14,16},{16,18},{18... | collective-permute-start | bytes 98312 | tf_op jit(solution)/shard_map/ppermute | solution.py:27
  67.5 13.0 %collective-permute-start.7 = (f32[4,18,1,128]{3,2,1,0:T(1,128)S(1)}, f32[4,18,1,128]{3,2,1,0:T(1,128)S(1)}, u32[]{:S(2)}, u32[]{:S(2)}) collective-permute-start(f32[4,18,1,128]{3,2,1,0:T(1,128)S(1)} %get-tuple-element.111), channel_id=1, source_target_pairs={{1,0},{3,2},{5,4},{7,6},{9,8},{11,10},{13,12},{15,14},{17,16},{19,... | collective-permute-start | bytes 110600 | tf_op jit(solution)/shard_map/ppermute | solution.py:30
  68.8 11.7 %collective-permute-start.6 = (f32[4,18,1,128]{3,2,1,0:T(1,128)S(1)}, f32[4,18,1,128]{3,2,1,0:T(1,128)S(1)}, u32[]{:S(2)}, u32[]{:S(2)}) collective-permute-start(f32[4,18,1,128]{3,2,1,0:T(1,128)S(1)} %get-tuple-element.110), channel_id=1, source_target_pairs={{0,1},{2,3},{4,5},{6,7},{8,9},{10,11},{12,13},{14,15},{16,17},{18,... | collective-permute-start | bytes 110600 | tf_op jit(solution)/shard_map/ppermute | solution.py:27
  94.9 8.3 %collective-permute-start.17 = (f32[3,3,4,32]{3,2,1,0:T(4,128)S(1)}, f32[3,3,4,32]{3,2,1,0:T(4,128)S(1)}, u32[]{:S(2)}, u32[]{:S(2)}) collective-permute-start(f32[3,3,4,32]{3,2,1,0:T(4,128)S(1)} %get-tuple-element.144), channel_id=1, source_target_pairs={{2,0},{4,2},{6,4},{8,6},{10,8},{12,10},{14,12},{16,14},{18,16},{20... | collective-permute-start | bytes 13832 | tf_op jit(solution)/shard_map/ppermute | solution.py:30
  100.9 3.1 %collective-permute-start.16 = (f32[3,3,4,32]{3,2,1,0:T(4,128)S(1)}, f32[3,3,4,32]{3,2,1,0:T(4,128)S(1)}, u32[]{:S(2)}, u32[]{:S(2)}) collective-permute-start(f32[3,3,4,32]{3,2,1,0:T(4,128)S(1)} %get-tuple-element.143), channel_id=1, source_target_pairs={{0,2},{2,4},{4,6},{6,8},{8,10},{10,12},{12,14},{14,16},{16,18},{18... | collective-permute-start | bytes 13832 | tf_op jit(solution)/shard_map/ppermute | solution.py:27
  104.0 12.6 %collective-permute-start.19 = (f32[3,10,3,32]{3,2,1,0:T(4,128)S(1)}, f32[3,10,3,32]{3,2,1,0:T(4,128)S(1)}, u32[]{:S(2)}, u32[]{:S(2)}) collective-permute-start(f32[3,10,3,32]{3,2,1,0:T(4,128)S(1)} %get-tuple-element.138), channel_id=1, source_target_pairs={{1,0},{3,2},{5,4},{7,6},{9,8},{11,10},{13,12},{15,14},{17,16},{19,... | collective-permute-start | bytes 34568 | tf_op jit(solution)/shard_map/ppermute | solution.py:30
  105.3 11.3 %collective-permute-start.18 = (f32[3,10,3,32]{3,2,1,0:T(4,128)S(1)}, f32[3,10,3,32]{3,2,1,0:T(4,128)S(1)}, u32[]{:S(2)}, u32[]{:S(2)}) collective-permute-start(f32[3,10,3,32]{3,2,1,0:T(4,128)S(1)} %get-tuple-element.137), channel_id=1, source_target_pairs={{0,1},{2,3},{4,5},{6,7},{8,9},{10,11},{12,13},{14,15},{16,17},{18,... | collective-permute-start | bytes 34568 | tf_op jit(solution)/shard_map/ppermute | solution.py:27
  109.3 7.6 %collective-permute-start.13 = (f32[4,1,16,128]{3,2,1,0:T(8,128)S(1)}, f32[4,1,16,128]{3,2,1,0:T(8,128)S(1)}, u32[]{:S(2)}, u32[]{:S(2)}) collective-permute-start(f32[4,1,16,128]{3,2,1,0:T(8,128)S(1)} %get-tuple-element.115), channel_id=1, source_target_pairs={{2,0},{4,2},{6,4},{8,6},{10,8},{12,10},{14,12},{16,14},{18,16},{20... | collective-permute-start | bytes 98312 | tf_op jit(solution)/shard_map/ppermute | solution.py:30
  114.7 3.1 %collective-permute-start.12 = (f32[4,1,16,128]{3,2,1,0:T(8,128)S(1)}, f32[4,1,16,128]{3,2,1,0:T(8,128)S(1)}, u32[]{:S(2)}, u32[]{:S(2)}) collective-permute-start(f32[4,1,16,128]{3,2,1,0:T(8,128)S(1)} %get-tuple-element.114), channel_id=1, source_target_pairs={{0,2},{2,4},{4,6},{6,8},{8,10},{10,12},{12,14},{14,16},{16,18},{18... | collective-permute-start | bytes 98312 | tf_op jit(solution)/shard_map/ppermute | solution.py:27
  117.9 13.0 %collective-permute-start.15 = (f32[4,18,1,128]{3,2,1,0:T(1,128)S(1)}, f32[4,18,1,128]{3,2,1,0:T(1,128)S(1)}, u32[]{:S(2)}, u32[]{:S(2)}) collective-permute-start(f32[4,18,1,128]{3,2,1,0:T(1,128)S(1)} %get-tuple-element.109), channel_id=1, source_target_pairs={{1,0},{3,2},{5,4},{7,6},{9,8},{11,10},{13,12},{15,14},{17,16},{19,... | collective-permute-start | bytes 110600 | tf_op jit(solution)/shard_map/ppermute | solution.py:30
  119.2 11.7 %collective-permute-start.14 = (f32[4,18,1,128]{3,2,1,0:T(1,128)S(1)}, f32[4,18,1,128]{3,2,1,0:T(1,128)S(1)}, u32[]{:S(2)}, u32[]{:S(2)}) collective-permute-start(f32[4,18,1,128]{3,2,1,0:T(1,128)S(1)} %get-tuple-element.108), channel_id=1, source_target_pairs={{0,1},{2,3},{4,5},{6,7},{8,9},{10,11},{12,13},{14,15},{16,17},{18,... | collective-permute-start | bytes 110600 | tf_op jit(solution)/shard_map/ppermute | solution.py:27
  142.7 12.2 %collective-permute-start.21 = (f32[3,3,4,32]{3,2,1,0:T(4,128)S(1)}, f32[3,3,4,32]{3,2,1,0:T(4,128)S(1)}, u32[]{:S(2)}, u32[]{:S(2)}) collective-permute-start(f32[3,3,4,32]{3,2,1,0:T(4,128)S(1)} %get-tuple-element.142), channel_id=1, source_target_pairs={{2,0},{4,2},{6,4},{8,6},{10,8},{12,10},{14,12},{16,14},{18,16},{20... | collective-permute-start | bytes 13832 | tf_op jit(solution)/shard_map/ppermute | solution.py:30
  148.2 6.7 %collective-permute-start.20 = (f32[3,3,4,32]{3,2,1,0:T(4,128)S(1)}, f32[3,3,4,32]{3,2,1,0:T(4,128)S(1)}, u32[]{:S(2)}, u32[]{:S(2)}) collective-permute-start(f32[3,3,4,32]{3,2,1,0:T(4,128)S(1)} %get-tuple-element.141), channel_id=1, source_target_pairs={{0,2},{2,4},{4,6},{6,8},{8,10},{10,12},{12,14},{14,16},{16,18},{18... | collective-permute-start | bytes 13832 | tf_op jit(solution)/shard_map/ppermute | solution.py:27
  155.0 6.1 %collective-permute-start.23 = (f32[3,10,3,32]{3,2,1,0:T(4,128)S(1)}, f32[3,10,3,32]{3,2,1,0:T(4,128)S(1)}, u32[]{:S(2)}, u32[]{:S(2)}) collective-permute-start(f32[3,10,3,32]{3,2,1,0:T(4,128)S(1)} %get-tuple-element.136), channel_id=1, source_target_pairs={{1,0},{3,2},{5,4},{7,6},{9,8},{11,10},{13,12},{15,14},{17,16},{19,... | collective-permute-start | bytes 34568 | tf_op jit(solution)/shard_map/ppermute | solution.py:30
  156.3 5.3 %collective-permute-start.22 = (f32[3,10,3,32]{3,2,1,0:T(4,128)S(1)}, f32[3,10,3,32]{3,2,1,0:T(4,128)S(1)}, u32[]{:S(2)}, u32[]{:S(2)}) collective-permute-start(f32[3,10,3,32]{3,2,1,0:T(4,128)S(1)} %get-tuple-element.135), channel_id=1, source_target_pairs={{0,1},{2,3},{4,5},{6,7},{8,9},{10,11},{12,13},{14,15},{16,17},{18,... | collective-permute-start | bytes 34568 | tf_op jit(solution)/shard_map/ppermute | solution.py:27
where the time goes:
time: 166 us; the launch traced here: 163 us
  starting transfers between devices  71.5 us (43%)
  local copies, waits for them, and re-layouts  49.8 us (30%)
  other arithmetic  36 us (22%)
  waiting for transfers between devices  3.92 us (2%)
    ppermute x12, starting transfers between devices, extended(): lax.ppermute(lax.slice_in_dim(block, block.shape[dim] - width, None, axis...  37.6 us
    ppermute x12, starting transfers between devices, extended(): lax.ppermute(lax.slice_in_dim(block, 0, width, axis=dim), axis, backward)  33.9 us
    reshape x3, local copies, waits for them, and re-layouts, restrict(): fine.reshape(lattice_span[0] // COARSEN_RATIO, COARSEN_RATIO, lattice_spa...  17.8 us
    div x3, local copies, waits for them, and re-layouts, per_device(): 1.0 / (1.0 + speed_falloff * refine_warmth(pointwise_warmth))  14.6 us
    another operation x7, other arithmetic, linearized_correction(): return (jnp.stack([new_pot, new_elec, new_hole], 0), warming_field)  14.2 us
    broadcast_in_dim x4, local copies, waits for them, and re-layouts, refine_warmth(): jnp.broadcast_to(coarse[:, None, :, None, :, None], (lattice_span[0], COA...  10.3 us
    reduce_sum x3, other arithmetic, restrict(): return jnp.mean(blocks, axis=(1, 3, 5))  7.86 us
    div x3, other arithmetic, linearized_correction(): 0.5 * species_drift_speed * ohmic_dissipation  6.22 us
  transfers between devices with their start and end apart: 24, of which 4 were waited for; matrix products, arithmetic and copies ran while one was open for 27% of the time, Pallas kernels for 0%

commit v1 on v0

v1 whole, which is shorter than its diff:
```python
import jax
import jax.numpy as jnp
from jax import lax
from jax.experimental import pallas as pl
from jax.experimental.pallas import tpu as pltpu
from jax.sharding import PartitionSpec as P

R = 4
NEWTON = 3
SWEEPS = 3

POISSON = 2.0
CHARGE = 4.0
SHIFT = 24.0
BIAS = 0.25
GAIN = 1.0
SINK = 0.3
DROP = 0.5
DOPING = (-2.0, -0.5, 0.5, 2.0)
CONDUCT = (0.5, 1.0, 2.0, 4.0)

F32 = jnp.float32


def phases(count):
    out = []
    for start in (0, 1):
        pairs = []
        for i in range(start, count - 1, 2):
            pairs += [(i, i + 1), (i + 1, i)]
        if pairs:
            out.append(pairs)
    return out


def both(pairs_x, pairs_y, count_y):
    return [(i * count_y + j, k * count_y + m) for i, k in pairs_x for j, m in pairs_y]


def lookup(labels, table):
    value = jnp.full(labels.shape, table[0], F32)
    for level in range(1, len(table)):
        value = jnp.where(labels == level, table[level], value)
    return value


def face(here, there, weight=None):
    psi_i, n_i, p_i, e_i = here
    psi_j, n_j, p_j, e_j = there
    d = psi_j - psi_i
    small = jnp.abs(d) < 0.25
    r = 1.0 / jnp.where(small, 1.0, jnp.exp(d) - 1.0)
    q = d * d
    b = jnp.where(
        small, (1.0 - 0.5 * d) + q * (1 / 12 - q * (1 / 720 - q * (1 / 30240))), d * r
    )
    bm = b + d
    s = jnp.where(small, -0.5 + d * (1 / 6 - q * (1 / 180 - q * (1 / 5040))), r * (1.0 - bm))
    e = 0.5 * (e_i + e_j)
    if weight is None:
        gn = n_i + (n_i - n_j) * s
        gp = (p_i - p_j) * s - p_j
    else:
        b = b * weight
        bm = b + d * weight
        s = s * weight
        e = e * weight
        gn = n_i * weight + (n_i - n_j) * s
        gp = (p_i - p_j) * s - p_j * weight
    fe = n_j * b - n_i * bm
    fh = p_j * bm - p_i * b
    j = fe - fh
    return e * d, e, fe, fh, gn, gp, b, bm, j * j


def add_here(acc, f):
    lap, es, fe, fh, gn, gp, b, bm, h = f
    return [x + y for x, y in zip(acc, (lap, es, fe, fh, gn, gp, b, bm, h))]


def add_there(acc, f):
    lap, es, fe, fh, gn, gp, b, bm, h = f
    return [
        acc[0] - lap, acc[1] + es, acc[2] - fe, acc[3] - fh,
        acc[4] + gn, acc[5] + gp, acc[6] + bm, acc[7] + b, acc[8] + h,
    ]


def solve(here, acc, contact, dop, mob):
    psi, n, p, _ = here
    lap, es, fe, fh, gn, gp, fwd, bwd, h = acc
    total = n + p
    rden = 1.0 / (total + 2.0)
    rec = (n * p - 1.0) * rden
    rn = (p + 1.0) * rden
    rn = rn * rn
    rp = (n + 1.0) * rden
    rp = rp * rp
    r0 = POISSON * lap + CHARGE * (p - n + dop)
    r1 = mob * fe - rec
    r2 = mob * fh - rec
    a = -POISSON * es
    b1 = mob * gn
    b2 = -mob * bwd - rn - SHIFT
    g1 = mob * gp
    g3 = -mob * fwd - rp - SHIFT
    caa = b2 * g3 - rp * rn
    cab = -(rp * g1 + b1 * g3)
    cac = -(b1 * rn + b2 * g1)
    rdet = 1.0 / (a * caa + CHARGE * (cac - cab))
    cb1 = CHARGE * b1
    cg1 = CHARGE * g1
    s0 = (caa * r0 + CHARGE * ((g3 - rn) * r1 + (rp - b2) * r2)) * rdet
    s1 = (cab * r0 + (a * g3 - cg1) * r1 + (cb1 + a * rp) * r2) * rdet
    s2 = (cac * r0 + (a * rn - cg1) * r1 + (a * b2 + cb1) * r2) * rdet
    s0 = jnp.where(contact, psi - BIAS * dop, s0)
    s1 = jnp.where(contact, n - 1.0, s1)
    s2 = jnp.where(contact, p - 1.0, s2)
    heat = h / total
    return psi - s0, n * jnp.exp(-s1 / n), p * jnp.exp(-s2 / p), heat


def iota(shape, axis):
    return lax.broadcasted_iota(jnp.int32, shape, axis)


def spread_rows(ref, first, count):
    lanes = ref.shape[-1]
    group = iota((count * R, lanes), 0) // R
    out = jnp.broadcast_to(ref[first : first + 1, :], (count * R, lanes))
    for j in range(1, count):
        out = jnp.where(group == j, ref[first + j : first + j + 1, :], out)
    return out


def make(nx, ny, nz, gx, gy):
    cx, cy = nx // R, ny // R
    cells = cx * cy
    W = SWEEPS
    px, py = phases(gx), phases(gy)
    ux, uy = len(px), len(py)
    ex, ey = cx + 2 * W, -(-(cy + 2 * W) // 8) * 8
    params = pltpu.CompilerParams(vmem_limit_bytes=16 * 1024 * 1024)
    smem = pl.BlockSpec(memory_space=pltpu.SMEM)
    vmem = pl.BlockSpec(memory_space=pltpu.VMEM)

    def call(kernel, outs, scratch, args, cost):
        return pl.pallas_call(
            kernel,
            out_shape=[jax.ShapeDtypeStruct(s, F32) for s in outs],
            in_specs=[smem] + [vmem] * (len(args) - 1),
            out_specs=[vmem] * len(outs),
            scratch_shapes=scratch,
            compiler_params=params,
            cost_estimate=pl.CostEstimate(
                flops=cost, bytes_accessed=0, transcendentals=0
            ),
        )(*args)

    def pick(odd, which, values):
        low_phase_even = 1 - which
        get = lambda k: values[k] if k < len(values) else jnp.zeros_like(values[0])
        return jnp.where(odd, get(1 - low_phase_even), get(low_phase_even))

    def put_sends(info, fields, sends):
        odd_x, odd_y = info[4] > 0.5, info[5] > 0.5
        for f, ref in enumerate(fields):
            low, high = ref[0:ny, :], ref[(nx - 1) * ny : nx * ny, :]
            rows = slice(f * ny, (f + 1) * ny)
            sends[0][rows, :] = jnp.where(odd_x, low, high)
            if ux > 1:
                sends[1][rows, :] = jnp.where(odd_x, high, low)
            low = ref[pl.ds(0, nx, stride=ny), :]
            high = ref[pl.ds(ny - 1, nx, stride=ny), :]
            rows = slice(f * nx, (f + 1) * nx)
            sends[ux][rows, :] = jnp.where(odd_y, low, high)
            if uy > 1:
                sends[ux + 1][rows, :] = jnp.where(odd_y, high, low)

    def pack_kernel(info, state, ins, zone, cat, warm, *rest):
        sends, (dop, cond, temp), eps = rest[: ux + uy], rest[ux + uy : ux + uy + 3], rest[-1]
        eps[...] = jnp.where(ins[...] == 1, 0.4, 1.0)
        put_sends(info, [state.at[0], state.at[1], state.at[2], eps], sends)
        coarse = nz // R
        pickz = (iota((coarse, nz), 1) // R == iota((coarse, nz), 0)).astype(F32)

        def widen(x):
            return jnp.dot(x, pickz, precision=lax.Precision.HIGHEST, preferred_element_type=F32)

        dop[...] = widen(lookup(zone[...], DOPING))
        cond[...] = widen(lookup(cat[...], CONDUCT))
        temp[...] = widen(warm[...])

    def sweeps(info, own, tiles_x, tiles_y, tiles_xy, base, ext):
        odd_x, odd_y = info[4] > 0.5, info[5] > 0.5
        ext[...] = jnp.zeros_like(ext)

        def grab(refs, f, off):
            return [r[off + f * cells : off + (f + 1) * cells, :] for r in refs]

        def place(f, sx, sy, tile):
            xs = {-1: range(cx - W, cx), 0: range(cx), 1: range(W)}[sx]
            ys = {-1: (cy - W, cy, 0), 0: (0, cy, W), 1: (0, W, W + cy)}[sy]
            at = {-1: 0, 0: W, 1: W + cx}[sx]
            for k, x in enumerate(xs):
                ext[f * ex + at + k, ys[2] : ys[2] + ys[1] - ys[0], :] = tile[
                    x * cy + ys[0] : x * cy + ys[1], :
                ]

        for f in range(3):
            place(f, 0, 0, own[f])
            for sx in (-1, 1):
                place(f, sx, 0, pick(odd_x, (sx + 1) // 2, grab(tiles_x, f, base[0])))
            for sy in (-1, 1):
                place(f, 0, sy, pick(odd_y, (sy + 1) // 2, grab(tiles_y, f, base[1])))
            for sx in (-1, 1):
                cols = []
                for row in tiles_xy:
                    cols.append(grab(row, f, 0))
                for sy in (-1, 1):
                    along = [pick(odd_y, (sy + 1) // 2, c) for c in cols]
                    place(f, sx, sy, pick(odd_x, (sx + 1) // 2, along))
        lane = iota((ey, nz), 1)
        has_low, has_high = lane >= R, lane < nz - R
        src = [ext[x] for x in range(ex)]
        tem = [ext[ex + x] for x in range(ex)]
        con = [ext[2 * ex + x] for x in range(ex)]
        inv = [1.0 / (SINK + 6.0 * c) for c in con]
        for s in range(1, W + 1):
            new = list(tem)
            for x in range(s, ex - s):
                t = tem[x]
                total = tem[x - 1] + tem[x + 1]
                total = total + (pltpu.roll(t, 1, 0) + pltpu.roll(t, ey - 1, 0))
                total = total + jnp.where(has_low, pltpu.roll(t, R, 1), 0.0)
                total = total + jnp.where(has_high, pltpu.roll(t, nz - R, 1), 0.0)
                new[x] = (src[x] + con[x] * total) * inv[x]
            tem = new
        return [tem[W + x][W : W + cy, :] for x in range(cx)]

    def newton_kernel(k):
        first, last = k == 0, k == NEWTON - 1

        def kernel(info, state, ins, ele, dop, cond, *rest):
            rest = list(rest)
            take = lambda c: [rest.pop(0) for _ in range(c)]
            got0 = take(ux + uy)
            if first:
                (temp_in,) = take(1)
                got, diag = got0, None
            else:
                got = take(ux + uy)
                diag = [take(uy) for _ in range(ux)]
                (tile,) = take(1)
            (out,) = take(1)
            sends = take(0 if last else ux + uy)
            (tile_out,) = take(1)
            halo, lowf, temp, heat, ext, mobs = take(6)
            odd_x, odd_y = info[4] > 0.5, info[5] > 0.5

            if first:
                temp[...] = temp_in[...]
            else:
                own = [tile[f * cells : (f + 1) * cells, :] for f in range(3)]
                rows = sweeps(info, own, got[:ux], got[ux:], diag, (3 * ny, 3 * nx), ext)
                for x in range(cx):
                    temp[x * cy : (x + 1) * cy, :] = rows[x]
            mobs[...] = 1.0 / (1.0 + DROP * temp[...])

            def side(axis, which, f):
                src = got0 if f == 3 else got
                if axis == 0:
                    return pick(odd_x, which, [r[f * ny : (f + 1) * ny, :] for r in src[:ux]])
                return pick(odd_y, which, [r[f * nx : (f + 1) * nx, :] for r in src[ux:]])

            epsof = lambda marks: jnp.where(marks == 1, 0.4, 1.0)
            row0 = [state[f, pl.ds(0, nx, stride=ny), :] for f in range(3)]
            row0.append(epsof(ins[pl.ds(0, nx, stride=ny), :]))
            below = [side(1, 0, f) for f in range(4)]
            for q, v in enumerate(face(below, row0, info[2])):
                lowf[q] = v
            for f in range(4):
                halo[f] = side(1, 1, f)

            zlane = iota((ny, nz), 1)
            wz = jnp.where(zlane < nz - 1, 1.0, 0.0)
            yrow = iota((ny, nz), 0)
            top = yrow == ny - 1
            bottom = yrow == 0
            wy = jnp.where(top, info[3], 1.0)

            def plane(x):
                rows = slice(x * ny, (x + 1) * ny)
                return [state[0, rows, :], state[1, rows, :], state[2, rows, :], epsof(ins[rows, :])]

            zero = jnp.zeros((ny, nz), F32)
            here = plane(0)
            acc = add_there(
                [zero] * 9, face([side(0, 0, f) for f in range(4)], here, info[0])
            )
            hsum = None
            for x in range(nx):
                if x % R == 0:
                    mob = spread_rows(mobs, (x // R) * cy, cy)
                    dopx = spread_rows(dop, (x // R) * cy, cy)
                if x + 1 < nx:
                    nxt = plane(x + 1)
                    f = face(here, nxt)
                else:
                    nxt = [side(0, 1, f) for f in range(4)]
                    f = face(here, nxt, info[1])
                acc = add_here(acc, f)
                later = add_there([zero] * 9, f)
                f = face(here, [pltpu.roll(v, nz - 1, 1) for v in here], wz)
                acc = add_here(acc, f)
                acc = add_there(acc, [pltpu.roll(v, 1, 1) for v in f])
                up = [
                    jnp.where(top, halo[q, x : x + 1, :], pltpu.roll(v, ny - 1, 0))
                    for q, v in enumerate(here)
                ]
                f = face(here, up, wy)
                acc = add_here(acc, f)
                f = [
                    jnp.where(bottom, lowf[q, x : x + 1, :], pltpu.roll(v, 1, 0))
                    for q, v in enumerate(f)
                ]
                acc = add_there(acc, f)
                contact = ele[slice(x * ny, (x + 1) * ny), :] == 1
                psi, n, p, h = solve(here, acc, contact, dopx, mob)
                rows = slice(x * ny, (x + 1) * ny)
                out[0, rows, :] = psi
                out[1, rows, :] = n
                out[2, rows, :] = p
                hsum = h if x % R == 0 else hsum + h
                if x % R == R - 1:
                    xc = x // R
                    heat[xc * ny : (xc + 1) * ny, :] = hsum
                here, acc = nxt, later

            v = heat[pl.ds(0, cells, stride=R), :]
            for j in range(1, R):
                v = v + heat[pl.ds(j, cells, stride=R), :]
            lane = iota((cells, nz), 1)
            step = 1
            while step < R:
                v = v + jnp.where(
                    lane % (2 * step) < step, pltpu.roll(v, nz - step, 1), pltpu.roll(v, step, 1)
                )
                step *= 2
            source = (GAIN * 0.5 / R**3) * mobs[...] * v
            tile_out[0:cells, :] = source
            tile_out[cells : 2 * cells, :] = temp[...]
            tile_out[2 * cells : 3 * cells, :] = cond[...]
            if not last:
                put_sends(info, [out.at[f] for f in range(3)], sends)
                for k2, s in enumerate(sends):
                    base = 3 * ny if k2 < ux else 3 * nx
                    s[base : base + 3 * cells, :] = tile_out[...]

        return kernel

    def final_kernel(info, *rest):
        rest = list(rest)
        take = lambda c: [rest.pop(0) for _ in range(c)]
        got = take(ux + uy)
        diag = [take(uy) for _ in range(ux)]
        tile, out, ext = take(3)
        own = [tile[f * cells : (f + 1) * cells, :] for f in range(3)]
        rows = sweeps(info, own, got[:ux], got[ux:], diag, (0, 0), ext)
        coarse = nz // R
        sel = (iota((nz, coarse), 0) == R * iota((nz, coarse), 1)).astype(F32)
        for x in range(cx):
            out[x * cy : (x + 1) * cy, :] = jnp.dot(
                rows[x], sel, precision=lax.Precision.HIGHEST, preferred_element_type=F32
            )

    def exchange(sends, tile=None):
        got = []
        for k, pairs in enumerate(px):
            got.append(lax.ppermute(sends[k], "gx", pairs))
        for k, pairs in enumerate(py):
            got.append(lax.ppermute(sends[ux + k], "gy", pairs))
        diag = []
        if tile is not None:
            for a in px:
                for b in py:
                    diag.append(lax.ppermute(tile, ("gx", "gy"), both(a, b, gy)))
        return got, diag

    def per_device(sol, ins, ele, zone, cat, warm):
        state = sol.reshape(3, nx * ny, nz)
        ins = ins.reshape(nx * ny, nz)
        ele = ele.reshape(nx * ny, nz)
        coarse = nz // R
        ix, iy = lax.axis_index("gx"), lax.axis_index("gy")
        info = jnp.stack(
            [ix > 0, ix < gx - 1, iy > 0, iy < gy - 1, ix % 2 == 1, iy % 2 == 1]
        ).astype(F32)
        rows_of = lambda extra: [(extra[0], nz)] * ux + [(extra[1], nz)] * uy
        node = nx * ny * nz
        res = call(
            pack_kernel,
            rows_of((4 * ny, 4 * nx)) + [(cells, nz)] * 3,
            [pltpu.VMEM((nx * ny, nz), F32)],
            [info, state, ins, zone.reshape(cells, coarse), cat.reshape(cells, coarse),
             warm.reshape(cells, coarse)],
            node,
        )
        sends, (dop, cond, temp) = res[: ux + uy], res[ux + uy :]
        got0, _ = exchange(sends)
        got, diag, tile = got0, [], None
        for k in range(NEWTON):
            last = k == NEWTON - 1
            args = [info, state, ins, ele, dop, cond] + got0
            args += [temp] if k == 0 else got + diag + [tile]
            outs = [(3, nx * ny, nz)]
            if not last:
                outs += rows_of((3 * ny + 3 * cells, 3 * nx + 3 * cells))
            outs += [(3 * cells, nz)]
            scratch = [
                pltpu.VMEM((4, nx, nz), F32),
                pltpu.VMEM((9, nx, nz), F32),
                pltpu.VMEM((cells, nz), F32),
                pltpu.VMEM((cx * ny, nz), F32),
                pltpu.VMEM((3 * ex, ey, nz), F32),
                pltpu.VMEM((cells, nz), F32),
            ]
            res = call(newton_kernel(k), outs, scratch, args, 300 * node)
            state, tile = res[0], res[-1]
            sends = [tile] * (ux + uy) if last else res[1:-1]
            got, diag = exchange(sends, tile)
        (warm,) = call(
            final_kernel,
            [(cells, coarse)],
            [pltpu.VMEM((3 * ex, ey, nz), F32)],
            [info] + got + diag + [tile],
            node,
        )
        return state.reshape(3, nx, ny, nz), warm.reshape(cx, cy, coarse)

    return per_device


def solution(mesh):
    placed = (
        P(None, "gx", "gy", None),
        P("gx", "gy", None),
        P("gx", "gy", None),
        P("gx", "gy", None),
        P("gx", "gy", None),
        P("gx", "gy", None),
    )
    gx, gy = mesh.shape["gx"], mesh.shape["gy"]

    def body(sol, *rest):
        _, nx, ny, nz = sol.shape
        return make(nx, ny, nz, gx, gy)(sol, *rest)

    return jax.shard_map(
        body,
        mesh=mesh,
        in_specs=placed,
        out_specs=(P(None, "gx", "gy", None), P("gx", "gy", None)),
        check_vma=False,
    )
```

time: 166 us -> 56.8 us (0.34)
  the two profiles are of different devices: /device:TPU:9 before, /device:TPU:1 now
where the time goes in v1:
time: 56.8 us; the launch traced here: 56.4 us
  starting transfers between devices  32.3 us (57%)
  Pallas kernels  10.4 us (18%)
  waiting for transfers between devices  10.2 us (18%)
  local copies, waits for them, and re-layouts  2.6 us (5%)
  between operations  0.85 us (1%)
    ppermute x8, starting transfers between devices, exchange(): got.append(lax.ppermute(sends[k], 'gx', pairs))  19.4 us
    pallas_call x5, Pallas kernels, call(): pl.pallas_call(kernel, out_shape=[jax.ShapeDtypeStruct(s, F32) for s in o...  10.4 us
    ppermute x6, starting transfers between devices, exchange(): diag.append(lax.ppermute(tile, ('gx', 'gy'), both(a, b, gy)))  8.74 us
    ppermute x6, waiting for transfers between devices, exchange(): diag.append(lax.ppermute(tile, ('gx', 'gy'), both(a, b, gy)))  7.28 us
    ppermute x4, starting transfers between devices, exchange(): got.append(lax.ppermute(sends[ux + k], 'gy', pairs))  4.25 us
    unnamed x14, local copies, waits for them, and re-layouts  2.5 us
    ppermute x8, waiting for transfers between devices, exchange(): got.append(lax.ppermute(sends[k], 'gx', pairs))  1.7 us
    ppermute x4, waiting for transfers between devices, exchange(): got.append(lax.ppermute(sends[ux + k], 'gy', pairs))  1.25 us
  transfers between devices with their start and end apart: 18, of which 5 were waited for; matrix products, arithmetic and copies ran while one was open for 0% of the time, Pallas kernels for 0%

profile of v1, /device:TPU:1, one launch (start us, length us, event | category | flops | bytes accessed | tf_op | source)
XLA Modules:
  0.0 56.4 jit_solution(9166876685430231808)
XLA Ops:
  0.7 0.1 stack.27
  0.8 0.6 copy-done.6
  1.4 0.9 %copy-done = s32[16,16,128]{2,1,0:T(8,128)S(1)} copy-done((s32[16,16,128]{2,1,0:T(8,128)S(1)}, s32[16,16,128]{2,1,0:T(8,128)}, u32[]{:S(2)}) %copy-start) | copy-done | bytes 131096
  2.3 1.0 %copy-done.2 = f32[3,16,16,128]{3,2,1,0:T(8,128)S(1)} copy-done((f32[3,16,16,128]{3,2,1,0:T(8,128)S(1)}, f32[3,16,16,128]{3,2,1,0:T(8,128)}, u32[]{:S(2)}) %copy-start.2) | copy-done | bytes 393240
  3.3 0.7 %shard_map.77 = (f32[64,128]{1,0:T(8,128)S(1)}, f32[64,128]{1,0:T(8,128)S(1)}, f32[64,128]{1,0:T(8,128)S(1)}, f32[16,128]{1,0:T(8,128)S(1)}, f32[16,128]{1,0:T(8,128)S(1)}, /*index=5*/f32[16,128]{1,0:T(8,128)S(1)}) custom-call(f32[6]{0:T(128)S(1)} %convert_element_type.3.info, f32[3,256,128]{2,1,0:T(8,128)S(1)} %bitcast.18, s32[256,128]{1,0:T(8,128)S(1)} %bitcast.14, ...), custom_call_target="tpu_custom_call" | custom-call | flops 32768 | tf_op jit(solution)/shard_map/pallas_call | solution.py:148
  4.0 0.0 collective-permute-start
  4.1 4.5 %collective-permute-start.1 = (f32[64,128]{1,0:T(8,128)S(1)}, f32[64,128]{1,0:T(8,128)S(1)}, u32[]{:S(2)}, u32[]{:S(2)}) collective-permute-start(f32[64,128]{1,0:T(8,128)S(1)} %get-tuple-element.23), channel_id=1, source_target_pairs={{2,4},{4,2},{6,8},{8,6},{10,12},{12,10},{14,16},{16,14},{18,20},{2... | collective-permute-start | bytes 98312 | tf_op jit(solution)/shard_map/ppermute | solution.py:380
  8.6 1.3 %collective-permute-start.2 = (f32[64,128]{1,0:T(8,128)S(1)}, f32[64,128]{1,0:T(8,128)S(1)}, u32[]{:S(2)}, u32[]{:S(2)}) collective-permute-start(f32[64,128]{1,0:T(8,128)S(1)} %get-tuple-element.24), channel_id=1, source_target_pairs={{0,1},{1,0},{2,3},{3,2},{4,5},{5,4},{6,7},{7,6},{8,9},{9,8},{10,11... | collective-permute-start | bytes 98312 | tf_op jit(solution)/shard_map/ppermute | solution.py:382
  9.8 0.3 collective-permute-done.1.rest_1_
  10.1 1.2 %collective-permute-done.2.rest_2_ = f32[64,128]{1,0:T(8,128)S(1)} collective-permute-done((f32[64,128]{1,0:T(8,128)S(1)}, f32[64,128]{1,0:T(8,128)S(1)}, u32[]{:S(2)}, u32[]{:S(2)}) %collective-permute-start.2) | collective-permute-done | bytes 32800 | tf_op jit(solution)/shard_map/ppermute | solution.py:382
  11.4 2.3 %shard_map.78 = (f32[3,256,128]{2,1,0:T(8,128)S(1)}, f32[96,128]{1,0:T(8,128)S(1)}, f32[96,128]{1,0:T(8,128)S(1)}, f32[96,128]{1,0:T(8,128)S(1)}, f32[48,128]{1,0:T(8,128)S(1)}) custom-call(f32[6]{0:T(128)S(1)} %convert_element_type.3.info, f32[3,256,128]{2,1,0:T(8,128)S(1)} %bitcast.19, s32[256,128]{1,0:T(8,128)S(1)} %bitcast.15, s32[256,128]{1,0:T(8,128)S(1)} %bitcast.20, ...), custom_call_target="tpu_custom_call" | custom-call | flops 9830400 | tf_op jit(solution)/shard_map/pallas_call | solution.py:148
  13.7 0.1 collective-permute-start.3
  13.8 3.8 %collective-permute-start.4 = (f32[96,128]{1,0:T(8,128)S(1)}, f32[96,128]{1,0:T(8,128)S(1)}, u32[]{:S(2)}, u32[]{:S(2)}) collective-permute-start(f32[96,128]{1,0:T(8,128)S(1)} %get-tuple-element.28), channel_id=1, source_target_pairs={{2,4},{4,2},{6,8},{8,6},{10,12},{12,10},{14,16},{16,14},{18,20},{2... | collective-permute-start | bytes 147464 | tf_op jit(solution)/shard_map/ppermute | solution.py:380
  17.6 1.6 %collective-permute-start.5 = (f32[96,128]{1,0:T(8,128)S(1)}, f32[96,128]{1,0:T(8,128)S(1)}, u32[]{:S(2)}, u32[]{:S(2)}) collective-permute-start(f32[96,128]{1,0:T(8,128)S(1)} %get-tuple-element.29), channel_id=1, source_target_pairs={{0,1},{1,0},{2,3},{3,2},{4,5},{5,4},{6,7},{7,6},{8,9},{9,8},{10,11... | collective-permute-start | bytes 147464 | tf_op jit(solution)/shard_map/ppermute | solution.py:382
  19.1 1.9 %collective-permute-start.7 = (f32[48,128]{1,0:T(8,128)S(1)}, f32[48,128]{1,0:T(8,128)S(1)}, u32[]{:S(2)}, u32[]{:S(2)}) collective-permute-start(f32[48,128]{1,0:T(8,128)S(1)} %get-tuple-element.30.rest_8_), channel_id=1, source_target_pairs={{2,5},{3,4},{4,3},{5,2},{6,9},{7,8},{8,7},{9,6},{10,13},{11,12},{1... | collective-permute-start | bytes 73736 | tf_op jit(solution)/shard_map/ppermute | solution.py:387
  21.1 0.1 collective-permute-start.6
  21.1 4.0 %collective-permute-done.7.rest_7_ = f32[48,128]{1,0:T(8,128)S(1)} collective-permute-done((f32[48,128]{1,0:T(8,128)S(1)}, f32[48,128]{1,0:T(8,128)S(1)}, u32[]{:S(2)}, u32[]{:S(2)}) %collective-permute-start.7) | collective-permute-done | bytes 24608 | tf_op jit(solution)/shard_map/ppermute | solution.py:387
  25.2 2.5 %shard_map.79 = (f32[3,256,128]{2,1,0:T(8,128)S(1)}, f32[96,128]{1,0:T(8,128)S(1)}, f32[96,128]{1,0:T(8,128)S(1)}, f32[96,128]{1,0:T(8,128)S(1)}, f32[48,128]{1,0:T(8,128)S(1)}) custom-call(f32[6]{0:T(128)S(1)} %convert_element_type.3.info, f32[3,256,128]{2,1,0:T(8,128)S(1)} %get-tuple-element.26.state, s32[256,128]{1,0:T(8,128)S(1)} %bitcast.16, ...), custom_call_target="tpu_custom_call" | custom-call | flops 9830400 | tf_op jit(solution)/shard_map/pallas_call | solution.py:148
  27.7 0.1 collective-permute-start.8
  27.8 4.9 %collective-permute-start.9 = (f32[96,128]{1,0:T(8,128)S(1)}, f32[96,128]{1,0:T(8,128)S(1)}, u32[]{:S(2)}, u32[]{:S(2)}) collective-permute-start(f32[96,128]{1,0:T(8,128)S(1)} %get-tuple-element.33), channel_id=1, source_target_pairs={{2,4},{4,2},{6,8},{8,6},{10,12},{12,10},{14,16},{16,14},{18,20},{2... | collective-permute-start | bytes 147464 | tf_op jit(solution)/shard_map/ppermute | solution.py:380
  32.7 0.7 %collective-permute-start.10 = (f32[96,128]{1,0:T(8,128)S(1)}, f32[96,128]{1,0:T(8,128)S(1)}, u32[]{:S(2)}, u32[]{:S(2)}) collective-permute-start(f32[96,128]{1,0:T(8,128)S(1)} %get-tuple-element.34), channel_id=1, source_target_pairs={{0,1},{1,0},{2,3},{3,2},{4,5},{5,4},{6,7},{7,6},{8,9},{9,8},{10,11... | collective-permute-start | bytes 147464 | tf_op jit(solution)/shard_map/ppermute | solution.py:382
  33.4 2.7 %collective-permute-start.12 = (f32[48,128]{1,0:T(8,128)S(1)}, f32[48,128]{1,0:T(8,128)S(1)}, u32[]{:S(2)}, u32[]{:S(2)}) collective-permute-start(f32[48,128]{1,0:T(8,128)S(1)} %get-tuple-element.35.rest_8_), channel_id=1, source_target_pairs={{2,5},{3,4},{4,3},{5,2},{6,9},{7,8},{8,7},{9,6},{10,13},{11,12},{1... | collective-permute-start | bytes 73736 | tf_op jit(solution)/shard_map/ppermute | solution.py:387
  36.1 0.1 collective-permute-start.11
  36.2 3.2 %collective-permute-done.12.rest_7_ = f32[48,128]{1,0:T(8,128)S(1)} collective-permute-done((f32[48,128]{1,0:T(8,128)S(1)}, f32[48,128]{1,0:T(8,128)S(1)}, u32[]{:S(2)}, u32[]{:S(2)}) %collective-permute-start.12) | collective-permute-done | bytes 24608 | tf_op jit(solution)/shard_map/ppermute | solution.py:387
  39.5 3.2 %shard_map.80 = (f32[3,256,128]{2,1,0:T(8,128)}, f32[48,128]{1,0:T(8,128)S(1)}) custom-call(f32[6]{0:T(128)S(1)} %convert_element_type.3.info, f32[3,256,128]{2,1,0:T(8,128)S(1)} %get-tuple-element.31.state, s32[256,128]{1,0:T(8,128)S(1)} %bitcast.17, s32[256,128]{1,0:T(8,128)S(1)} %bitcast.22, f32[16,128]{1,0:T(8,128)S(1)} %get-tuple-element.20.dop, ...), custom_call_target="tpu_custom_call" | custom-call | flops 9830400 | tf_op jit(solution)/shard_map/pallas_call | solution.py:148
  42.7 3.9 %collective-permute-start.17 = (f32[48,128]{1,0:T(8,128)S(1)}, f32[48,128]{1,0:T(8,128)S(1)}, u32[]{:S(2)}, u32[]{:S(2)}) collective-permute-start(f32[48,128]{1,0:T(8,128)S(1)} %get-tuple-element.37.rest_5_), channel_id=1, source_target_pairs={{2,5},{3,4},{4,3},{5,2},{6,9},{7,8},{8,7},{9,6},{10,13},{11,12},{1... | collective-permute-start | bytes 73736 | tf_op jit(solution)/shard_map/ppermute | solution.py:387
  46.6 0.1 collective-permute-start.16
  46.6 0.7 %collective-permute-start.15 = (f32[48,128]{1,0:T(8,128)S(1)}, f32[48,128]{1,0:T(8,128)S(1)}, u32[]{:S(2)}, u32[]{:S(2)}) collective-permute-start(f32[48,128]{1,0:T(8,128)S(1)} %get-tuple-element.37.rest_5_), channel_id=1, source_target_pairs={{0,1},{1,0},{2,3},{3,2},{4,5},{5,4},{6,7},{7,6},{8,9},{9,8},{10,11... | collective-permute-start | bytes 73736 | tf_op jit(solution)/shard_map/ppermute | solution.py:382
  47.3 5.9 %collective-permute-start.14 = (f32[48,128]{1,0:T(8,128)S(1)}, f32[48,128]{1,0:T(8,128)S(1)}, u32[]{:S(2)}, u32[]{:S(2)}) collective-permute-start(f32[48,128]{1,0:T(8,128)S(1)} %get-tuple-element.37.rest_5_), channel_id=1, source_target_pairs={{2,4},{4,2},{6,8},{8,6},{10,12},{12,10},{14,16},{16,14},{18,20},{2... | collective-permute-start | bytes 73736 | tf_op jit(solution)/shard_map/ppermute | solution.py:380
  53.3 0.1 collective-permute-start.13
  53.4 1.4 %collective-permute-done.14.rest_1_ = f32[48,128]{1,0:T(8,128)S(1)} collective-permute-done((f32[48,128]{1,0:T(8,128)S(1)}, f32[48,128]{1,0:T(8,128)S(1)}, u32[]{:S(2)}, u32[]{:S(2)}) %collective-permute-start.14) | collective-permute-done | bytes 24608 | tf_op jit(solution)/shard_map/ppermute | solution.py:380
  54.8 1.7 %shard_map.81 = f32[16,32]{1,0:T(8,128)} custom-call(f32[6]{0:T(128)S(1)} %convert_element_type.3.info, f32[48,128]{1,0:T(8,128)S(1)} %collective-permute-done.13.rest_0_, f32[48,128]{1,0:T(8,128)S(1)} %collective-permute-done.14.rest_1_, f32[48,128]{1,0:T(8,128)S(1)} %collective-permute-done.15.rest_2_, f32[48,128]{1,0:T(8,128)S(1)} %collective-permute-done.16.rest_3_, ...), custom_call_target="tpu_custom_call" | custom-call | flops 32768 | tf_op jit(solution)/shard_map/pallas_call | solution.py:148
  (25 shorter events, 0.1 us)
Async XLA Ops:
  0.7 0.7 %copy-start.6 = (f32[4,4,32]{2,1,0:T(4,128)S(1)}, f32[4,4,32]{2,1,0:T(4,128)}, u32[]{:S(2)}) copy-start(f32[4,4,32]{2,1,0:T(4,128)} %param.11) | copy-start | bytes 6148
  0.7 0.7 %copy-start.4 = (s32[4,4,32]{2,1,0:T(4,128)S(1)}, s32[4,4,32]{2,1,0:T(4,128)}, u32[]{:S(2)}) copy-start(s32[4,4,32]{2,1,0:T(4,128)} %param.9) | copy-start | bytes 6148
  0.7 0.7 %copy-start.5 = (s32[4,4,32]{2,1,0:T(4,128)S(1)}, s32[4,4,32]{2,1,0:T(4,128)}, u32[]{:S(2)}) copy-start(s32[4,4,32]{2,1,0:T(4,128)} %param.10) | copy-start | bytes 6148
  1.4 0.9 %copy-start = (s32[16,16,128]{2,1,0:T(8,128)S(1)}, s32[16,16,128]{2,1,0:T(8,128)}, u32[]{:S(2)}) copy-start(s32[16,16,128]{2,1,0:T(8,128)} %param.7) | copy-start | bytes 393220
  2.3 1.0 %copy-start.2 = (f32[3,16,16,128]{3,2,1,0:T(8,128)S(1)}, f32[3,16,16,128]{3,2,1,0:T(8,128)}, u32[]{:S(2)}) copy-start(f32[3,16,16,128]{3,2,1,0:T(8,128)} %param.6) | copy-start | bytes 1179652
  3.3 8.1 %copy-start.3 = (s32[16,16,128]{2,1,0:T(8,128)S(1)}, s32[16,16,128]{2,1,0:T(8,128)}, u32[]{:S(2)}) copy-start(s32[16,16,128]{2,1,0:T(8,128)} %param.8) | copy-start | bytes 393220
  4.0 5.8 %collective-permute-start = (f32[64,128]{1,0:T(8,128)S(1)}, f32[64,128]{1,0:T(8,128)S(1)}, u32[]{:S(2)}, u32[]{:S(2)}) collective-permute-start(f32[64,128]{1,0:T(8,128)S(1)} %get-tuple-element.22), channel_id=1, source_target_pairs={{0,2},{2,0},{4,6},{6,4},{8,10},{10,8},{12,14},{14,12},{16,18},{18,... | collective-permute-start | bytes 98312 | tf_op jit(solution)/shard_map/ppermute | solution.py:380
  4.1 6.1 %collective-permute-start.1 = (f32[64,128]{1,0:T(8,128)S(1)}, f32[64,128]{1,0:T(8,128)S(1)}, u32[]{:S(2)}, u32[]{:S(2)}) collective-permute-start(f32[64,128]{1,0:T(8,128)S(1)} %get-tuple-element.23), channel_id=1, source_target_pairs={{2,4},{4,2},{6,8},{8,6},{10,12},{12,10},{14,16},{16,14},{18,20},{2... | collective-permute-start | bytes 98312 | tf_op jit(solution)/shard_map/ppermute | solution.py:380
  8.6 2.8 %collective-permute-start.2 = (f32[64,128]{1,0:T(8,128)S(1)}, f32[64,128]{1,0:T(8,128)S(1)}, u32[]{:S(2)}, u32[]{:S(2)}) collective-permute-start(f32[64,128]{1,0:T(8,128)S(1)} %get-tuple-element.24), channel_id=1, source_target_pairs={{0,1},{1,0},{2,3},{3,2},{4,5},{5,4},{6,7},{7,6},{8,9},{9,8},{10,11... | collective-permute-start | bytes 98312 | tf_op jit(solution)/shard_map/ppermute | solution.py:382
  11.4 13.8 %copy-start.1 = (s32[16,16,128]{2,1,0:T(8,128)S(1)}, s32[16,16,128]{2,1,0:T(8,128)}, u32[]{:S(2)}) copy-start(s32[16,16,128]{2,1,0:T(8,128)} %param.7) | copy-start | bytes 393220
  13.7 11.5 %collective-permute-start.3 = (f32[96,128]{1,0:T(8,128)S(1)}, f32[96,128]{1,0:T(8,128)S(1)}, u32[]{:S(2)}, u32[]{:S(2)}) collective-permute-start(f32[96,128]{1,0:T(8,128)S(1)} %get-tuple-element.27), channel_id=1, source_target_pairs={{0,2},{2,0},{4,6},{6,4},{8,10},{10,8},{12,14},{14,12},{16,18},{18,... | collective-permute-start | bytes 147464 | tf_op jit(solution)/shard_map/ppermute | solution.py:380
  13.8 11.4 %collective-permute-start.4 = (f32[96,128]{1,0:T(8,128)S(1)}, f32[96,128]{1,0:T(8,128)S(1)}, u32[]{:S(2)}, u32[]{:S(2)}) collective-permute-start(f32[96,128]{1,0:T(8,128)S(1)} %get-tuple-element.28), channel_id=1, source_target_pairs={{2,4},{4,2},{6,8},{8,6},{10,12},{12,10},{14,16},{16,14},{18,20},{2... | collective-permute-start | bytes 147464 | tf_op jit(solution)/shard_map/ppermute | solution.py:380
  17.6 7.6 %collective-permute-start.5 = (f32[96,128]{1,0:T(8,128)S(1)}, f32[96,128]{1,0:T(8,128)S(1)}, u32[]{:S(2)}, u32[]{:S(2)}) collective-permute-start(f32[96,128]{1,0:T(8,128)S(1)} %get-tuple-element.29), channel_id=1, source_target_pairs={{0,1},{1,0},{2,3},{3,2},{4,5},{5,4},{6,7},{7,6},{8,9},{9,8},{10,11... | collective-permute-start | bytes 147464 | tf_op jit(solution)/shard_map/ppermute | solution.py:382
  19.1 6.0 %collective-permute-start.7 = (f32[48,128]{1,0:T(8,128)S(1)}, f32[48,128]{1,0:T(8,128)S(1)}, u32[]{:S(2)}, u32[]{:S(2)}) collective-permute-start(f32[48,128]{1,0:T(8,128)S(1)} %get-tuple-element.30.rest_8_), channel_id=1, source_target_pairs={{2,5},{3,4},{4,3},{5,2},{6,9},{7,8},{8,7},{9,6},{10,13},{11,12},{1... | collective-permute-start | bytes 73736 | tf_op jit(solution)/shard_map/ppermute | solution.py:387
  21.1 4.1 %collective-permute-start.6 = (f32[48,128]{1,0:T(8,128)S(1)}, f32[48,128]{1,0:T(8,128)S(1)}, u32[]{:S(2)}, u32[]{:S(2)}) collective-permute-start(f32[48,128]{1,0:T(8,128)S(1)} %get-tuple-element.30.rest_8_), channel_id=1, source_target_pairs={{0,3},{1,2},{2,1},{3,0},{4,7},{5,6},{6,5},{7,4},{8,11},{9,10},{10,... | collective-permute-start | bytes 73736 | tf_op jit(solution)/shard_map/ppermute | solution.py:387
  27.7 11.8 %collective-permute-start.8 = (f32[96,128]{1,0:T(8,128)S(1)}, f32[96,128]{1,0:T(8,128)S(1)}, u32[]{:S(2)}, u32[]{:S(2)}) collective-permute-start(f32[96,128]{1,0:T(8,128)S(1)} %get-tuple-element.32), channel_id=1, source_target_pairs={{0,2},{2,0},{4,6},{6,4},{8,10},{10,8},{12,14},{14,12},{16,18},{18,... | collective-permute-start | bytes 147464 | tf_op jit(solution)/shard_map/ppermute | solution.py:380
  27.8 11.7 %collective-permute-start.9 = (f32[96,128]{1,0:T(8,128)S(1)}, f32[96,128]{1,0:T(8,128)S(1)}, u32[]{:S(2)}, u32[]{:S(2)}) collective-permute-start(f32[96,128]{1,0:T(8,128)S(1)} %get-tuple-element.33), channel_id=1, source_target_pairs={{2,4},{4,2},{6,8},{8,6},{10,12},{12,10},{14,16},{16,14},{18,20},{2... | collective-permute-start | bytes 147464 | tf_op jit(solution)/shard_map/ppermute | solution.py:380
  32.7 6.8 %collective-permute-start.10 = (f32[96,128]{1,0:T(8,128)S(1)}, f32[96,128]{1,0:T(8,128)S(1)}, u32[]{:S(2)}, u32[]{:S(2)}) collective-permute-start(f32[96,128]{1,0:T(8,128)S(1)} %get-tuple-element.34), channel_id=1, source_target_pairs={{0,1},{1,0},{2,3},{3,2},{4,5},{5,4},{6,7},{7,6},{8,9},{9,8},{10,11... | collective-permute-start | bytes 147464 | tf_op jit(solution)/shard_map/ppermute | solution.py:382
  33.4 6.0 %collective-permute-start.12 = (f32[48,128]{1,0:T(8,128)S(1)}, f32[48,128]{1,0:T(8,128)S(1)}, u32[]{:S(2)}, u32[]{:S(2)}) collective-permute-start(f32[48,128]{1,0:T(8,128)S(1)} %get-tuple-element.35.rest_8_), channel_id=1, source_target_pairs={{2,5},{3,4},{4,3},{5,2},{6,9},{7,8},{8,7},{9,6},{10,13},{11,12},{1... | collective-permute-start | bytes 73736 | tf_op jit(solution)/shard_map/ppermute | solution.py:387
  36.1 3.3 %collective-permute-start.11 = (f32[48,128]{1,0:T(8,128)S(1)}, f32[48,128]{1,0:T(8,128)S(1)}, u32[]{:S(2)}, u32[]{:S(2)}) collective-permute-start(f32[48,128]{1,0:T(8,128)S(1)} %get-tuple-element.35.rest_8_), channel_id=1, source_target_pairs={{0,3},{1,2},{2,1},{3,0},{4,7},{5,6},{6,5},{7,4},{8,11},{9,10},{10,... | collective-permute-start | bytes 73736 | tf_op jit(solution)/shard_map/ppermute | solution.py:387
  42.7 10.7 %collective-permute-start.17 = (f32[48,128]{1,0:T(8,128)S(1)}, f32[48,128]{1,0:T(8,128)S(1)}, u32[]{:S(2)}, u32[]{:S(2)}) collective-permute-start(f32[48,128]{1,0:T(8,128)S(1)} %get-tuple-element.37.rest_5_), channel_id=1, source_target_pairs={{2,5},{3,4},{4,3},{5,2},{6,9},{7,8},{8,7},{9,6},{10,13},{11,12},{1... | collective-permute-start | bytes 73736 | tf_op jit(solution)/shard_map/ppermute | solution.py:387
  46.6 6.8 %collective-permute-start.16 = (f32[48,128]{1,0:T(8,128)S(1)}, f32[48,128]{1,0:T(8,128)S(1)}, u32[]{:S(2)}, u32[]{:S(2)}) collective-permute-start(f32[48,128]{1,0:T(8,128)S(1)} %get-tuple-element.37.rest_5_), channel_id=1, source_target_pairs={{0,3},{1,2},{2,1},{3,0},{4,7},{5,6},{6,5},{7,4},{8,11},{9,10},{10,... | collective-permute-start | bytes 73736 | tf_op jit(solution)/shard_map/ppermute | solution.py:387
  46.6 6.7 %collective-permute-start.15 = (f32[48,128]{1,0:T(8,128)S(1)}, f32[48,128]{1,0:T(8,128)S(1)}, u32[]{:S(2)}, u32[]{:S(2)}) collective-permute-start(f32[48,128]{1,0:T(8,128)S(1)} %get-tuple-element.37.rest_5_), channel_id=1, source_target_pairs={{0,1},{1,0},{2,3},{3,2},{4,5},{5,4},{6,7},{7,6},{8,9},{9,8},{10,11... | collective-permute-start | bytes 73736 | tf_op jit(solution)/shard_map/ppermute | solution.py:382
  47.3 7.4 %collective-permute-start.14 = (f32[48,128]{1,0:T(8,128)S(1)}, f32[48,128]{1,0:T(8,128)S(1)}, u32[]{:S(2)}, u32[]{:S(2)}) collective-permute-start(f32[48,128]{1,0:T(8,128)S(1)} %get-tuple-element.37.rest_5_), channel_id=1, source_target_pairs={{2,4},{4,2},{6,8},{8,6},{10,12},{12,10},{14,16},{16,14},{18,20},{2... | collective-permute-start | bytes 73736 | tf_op jit(solution)/shard_map/ppermute | solution.py:380
  53.3 1.5 %collective-permute-start.13 = (f32[48,128]{1,0:T(8,128)S(1)}, f32[48,128]{1,0:T(8,128)S(1)}, u32[]{:S(2)}, u32[]{:S(2)}) collective-permute-start(f32[48,128]{1,0:T(8,128)S(1)} %get-tuple-element.37.rest_5_), channel_id=1, source_target_pairs={{0,2},{2,0},{4,6},{6,4},{8,10},{10,8},{12,14},{14,12},{16,18},{18,... | collective-permute-start | bytes 73736 | tf_op jit(solution)/shard_map/ppermute | solution.py:380

commit v2 on v1

v2 whole, which is shorter than its diff:
```python
import jax
import jax.numpy as jnp
from jax import lax
from jax.experimental import pallas as pl
from jax.experimental.pallas import tpu as pltpu
from jax.sharding import PartitionSpec as P

R = 4
NEWTON = 3
SWEEPS = 3

POISSON = 2.0
CHARGE = 4.0
SHIFT = 24.0
BIAS = 0.25
GAIN = 1.0
SINK = 0.3
DROP = 0.5
DOPING = (-2.0, -0.5, 0.5, 2.0)
CONDUCT = (0.5, 1.0, 2.0, 4.0)

F32 = jnp.float32


def phases(count):
    out = []
    for start in (0, 1):
        pairs = []
        for i in range(start, count - 1, 2):
            pairs += [(i, i + 1), (i + 1, i)]
        if pairs:
            out.append(pairs)
    return out


def both(pairs_x, pairs_y, count_y):
    return [(i * count_y + j, k * count_y + m) for i, k in pairs_x for j, m in pairs_y]


def lookup(labels, table):
    value = jnp.full(labels.shape, table[0], F32)
    for level in range(1, len(table)):
        value = jnp.where(labels == level, table[level], value)
    return value


def face(here, there, weight=None):
    psi_i, n_i, p_i, e_i = here
    psi_j, n_j, p_j, e_j = there
    d = psi_j - psi_i
    small = jnp.abs(d) < 0.25
    r = 1.0 / jnp.where(small, 1.0, jnp.exp(d) - 1.0)
    q = d * d
    b = jnp.where(
        small, (1.0 - 0.5 * d) + q * (1 / 12 - q * (1 / 720 - q * (1 / 30240))), d * r
    )
    bm = b + d
    s = jnp.where(small, -0.5 + d * (1 / 6 - q * (1 / 180 - q * (1 / 5040))), r * (1.0 - bm))
    e = 0.5 * (e_i + e_j)
    if weight is None:
        gn = n_i + (n_i - n_j) * s
        gp = (p_i - p_j) * s - p_j
    else:
        b = b * weight
        bm = b + d * weight
        s = s * weight
        e = e * weight
        gn = n_i * weight + (n_i - n_j) * s
        gp = (p_i - p_j) * s - p_j * weight
    fe = n_j * b - n_i * bm
    fh = p_j * bm - p_i * b
    j = fe - fh
    return e * d, e, fe, fh, gn, gp, b, bm, j * j


def add_here(acc, f):
    lap, es, fe, fh, gn, gp, b, bm, h = f
    return [x + y for x, y in zip(acc, (lap, es, fe, fh, gn, gp, b, bm, h))]


def add_there(acc, f):
    lap, es, fe, fh, gn, gp, b, bm, h = f
    return [
        acc[0] - lap, acc[1] + es, acc[2] - fe, acc[3] - fh,
        acc[4] + gn, acc[5] + gp, acc[6] + bm, acc[7] + b, acc[8] + h,
    ]


def solve(here, acc, contact, dop, mob):
    psi, n, p, _ = here
    lap, es, fe, fh, gn, gp, fwd, bwd, h = acc
    total = n + p
    rden = 1.0 / (total + 2.0)
    rec = (n * p - 1.0) * rden
    rn = (p + 1.0) * rden
    rn = rn * rn
    rp = (n + 1.0) * rden
    rp = rp * rp
    r0 = POISSON * lap + CHARGE * (p - n + dop)
    r1 = mob * fe - rec
    r2 = mob * fh - rec
    a = -POISSON * es
    b1 = mob * gn
    b2 = -mob * bwd - rn - SHIFT
    g1 = mob * gp
    g3 = -mob * fwd - rp - SHIFT
    caa = b2 * g3 - rp * rn
    cab = -(rp * g1 + b1 * g3)
    cac = -(b1 * rn + b2 * g1)
    rdet = 1.0 / (a * caa + CHARGE * (cac - cab))
    cb1 = CHARGE * b1
    cg1 = CHARGE * g1
    s0 = (caa * r0 + CHARGE * ((g3 - rn) * r1 + (rp - b2) * r2)) * rdet
    s1 = (cab * r0 + (a * g3 - cg1) * r1 + (cb1 + a * rp) * r2) * rdet
    s2 = (cac * r0 + (a * rn - cg1) * r1 + (a * b2 + cb1) * r2) * rdet
    s0 = jnp.where(contact, psi - BIAS * dop, s0)
    s1 = jnp.where(contact, n - 1.0, s1)
    s2 = jnp.where(contact, p - 1.0, s2)
    heat = None if h is None else h / total
    return psi - s0, n * jnp.exp(-s1 / n), p * jnp.exp(-s2 / p), heat


def iota(shape, axis):
    return lax.broadcasted_iota(jnp.int32, shape, axis)


def spread_rows(ref, first, count):
    lanes = ref.shape[-1]
    group = iota((count * R, lanes), 0) // R
    out = jnp.broadcast_to(ref[first : first + 1, :], (count * R, lanes))
    for j in range(1, count):
        out = jnp.where(group == j, ref[first + j : first + j + 1, :], out)
    return out


def make(nx, ny, nz, gx, gy):
    cx, cy = nx // R, ny // R
    cells = cx * cy
    W = SWEEPS
    px, py = phases(gx), phases(gy)
    ux, uy = len(px), len(py)
    ex, ey = cx + 2 * W, -(-(cy + 2 * W) // 8) * 8
    nodes = nx * ny
    params = pltpu.CompilerParams(vmem_limit_bytes=16 * 1024 * 1024)
    smem = pl.BlockSpec(memory_space=pltpu.SMEM)
    vmem = pl.BlockSpec(memory_space=pltpu.VMEM)
    hbm = pl.BlockSpec(memory_space=pl.ANY)

    def call(kernel, outs, scratch, args, cost, specs=None):
        return list(pl.pallas_call(
            kernel,
            out_shape=[jax.ShapeDtypeStruct(s, F32) for s in outs],
            in_specs=specs or [smem] + [vmem] * (len(args) - 1),
            out_specs=[vmem] * len(outs),
            scratch_shapes=scratch,
            compiler_params=params,
            cost_estimate=pl.CostEstimate(flops=cost, bytes_accessed=0, transcendentals=0),
        )(*args))

    def pick(odd, which, values):
        get = lambda k: values[k] if k < len(values) else jnp.zeros_like(values[0])
        return jnp.where(odd, get(which), get(1 - which))

    def put_x(info, fields, sends):
        odd = info[4] > 0.5
        for f, ref in enumerate(fields):
            low, high = ref[0:ny, :], ref[(nx - 1) * ny : nodes, :]
            for k, send in enumerate(sends):
                first, second = (low, high) if k == 0 else (high, low)
                send[f * ny : (f + 1) * ny, :] = jnp.where(odd, first, second)

    def put_y(info, fields, sends):
        odd = info[5] > 0.5
        for f, ref in enumerate(fields):
            low = ref[pl.ds(0, nx, stride=ny), :]
            high = ref[pl.ds(ny - 1, nx, stride=ny), :]
            for k, send in enumerate(sends):
                first, second = (low, high) if k == 0 else (high, low)
                send[f * nx : (f + 1) * nx, :] = jnp.where(odd, first, second)

    def epsof(marks):
        return jnp.where(marks == 1, 0.4, 1.0)

    def turn(f):
        lap, es, fe, fh, gn, gp, b, bm, h = f
        return [-lap, es, -fe, -fh, gn, gp, bm, b, h]

    def whole(accs, rim_x, rim_y, x, qs):
        row = iota((8, nz), 0)
        out = []
        for q in qs:
            a = accs[q][x * ny : (x + 1) * ny, :]
            if x == 0:
                a = a + rim_x[q]
            if x == nx - 1:
                a = a + rim_x[9 + q]
            parts = [a[r : r + 8] for r in range(0, ny, 8)]
            parts[0] = parts[0] + jnp.where(row == 0, rim_y[q, x : x + 1, :], 0.0)
            parts[-1] = parts[-1] + jnp.where(row == 7, rim_y[9 + q, x : x + 1, :], 0.0)
            out.append(jnp.concatenate(parts, 0) if len(parts) > 1 else parts[0])
        return out

    def pack_kernel(info, state_h, ins_h, zone, cat, warm, *rest):
        sends, (dop, cond, temp) = rest[: ux + uy], rest[ux + uy : ux + uy + 3]
        state, eps, marks, sems = rest[ux + uy + 3 :]
        copies = [
            pltpu.make_async_copy(state_h, state, sems.at[0]),
            pltpu.make_async_copy(ins_h, marks, sems.at[1]),
        ]
        for c in copies:
            c.start()
        coarse = nz // R
        pickz = (iota((coarse, nz), 1) // R == iota((coarse, nz), 0)).astype(F32)

        def widen(x):
            return jnp.dot(x, pickz, precision=lax.Precision.HIGHEST, preferred_element_type=F32)

        dop[...] = widen(lookup(zone[...], DOPING))
        cond[...] = widen(lookup(cat[...], CONDUCT))
        temp[...] = widen(warm[...])
        for c in copies:
            c.wait()
        eps[...] = epsof(marks[...])
        fields = [state.at[0], state.at[1], state.at[2], eps]
        put_x(info, fields, sends[:ux])
        put_y(info, fields, sends[ux:])

    def inner_kernel(info, state, ins, *accs):
        zlane = iota((ny, nz), 1)
        wz = jnp.where(zlane < nz - 1, 1.0, 0.0)
        wy = jnp.where(iota((ny, nz), 0) < ny - 1, 1.0, 0.0)

        def plane(x):
            rows = slice(x * ny, (x + 1) * ny)
            return [state[0, rows, :], state[1, rows, :], state[2, rows, :], epsof(ins[rows, :])]

        here = plane(0)
        acc = None
        for x in range(nx):
            f = face(here, [pltpu.roll(v, nz - 1, 1) for v in here], wz)
            acc = list(f) if acc is None else add_here(acc, f)
            acc = add_there(acc, [pltpu.roll(v, 1, 1) for v in f])
            f = face(here, [pltpu.roll(v, ny - 1, 0) for v in here], wy)
            acc = add_here(acc, f)
            acc = add_there(acc, [pltpu.roll(v, 1, 0) for v in f])
            later = None
            if x + 1 < nx:
                here, old = plane(x + 1), here
                f = face(old, here)
                acc = add_here(acc, f)
                later = turn(f)
            for q in range(9):
                accs[q][x * ny : (x + 1) * ny, :] = acc[q]
            acc = later

    def sweeps(info, own, tiles_x, tiles_y, base, ext):
        odd_x, odd_y = info[4] > 0.5, info[5] > 0.5
        ext[...] = jnp.zeros_like(ext)

        def grab(ref, f, at):
            return ref[at + f * cells : at + (f + 1) * cells, :]

        def place(f, sx, sy, tile):
            xs = {-1: range(cx - W, cx), 0: range(cx), 1: range(W)}[sx]
            lo, hi, to = {-1: (cy - W, cy, 0), 0: (0, cy, W), 1: (0, W, W + cy)}[sy]
            at = {-1: 0, 0: W, 1: W + cx}[sx]
            for k, x in enumerate(xs):
                ext[f * ex + at + k, to : to + hi - lo, :] = tile[x * cy + lo : x * cy + hi, :]

        for f in range(3):
            place(f, 0, 0, own[f])
            for sy in (-1, 1):
                tile = pick(odd_y, (sy + 1) // 2, [grab(r, f, base[1]) for r in tiles_y])
                place(f, 0, sy, tile)
            for sx in (-1, 1):
                tile = pick(odd_x, (sx + 1) // 2, [grab(r, f, base[0]) for r in tiles_x])
                place(f, sx, 0, tile)
                for sy in (-1, 1):
                    along = [
                        pick(
                            odd_y,
                            (sy + 1) // 2,
                            [grab(r, f, base[0] + 3 * cells * (1 + b)) for b in range(uy)],
                        )
                        for r in tiles_x
                    ]
                    place(f, sx, sy, pick(odd_x, (sx + 1) // 2, along))
        lane = iota((ey, nz), 1)
        has_low, has_high = lane >= R, lane < nz - R
        src = [ext[x] for x in range(ex)]
        tem = [ext[ex + x] for x in range(ex)]
        con = [ext[2 * ex + x] for x in range(ex)]
        inv = [1.0 / (SINK + 6.0 * c) for c in con]
        for s in range(1, W + 1):
            new = list(tem)
            for x in range(s, ex - s):
                t = tem[x]
                total = tem[x - 1] + tem[x + 1]
                total = total + (pltpu.roll(t, 1, 0) + pltpu.roll(t, ey - 1, 0))
                total = total + jnp.where(has_low, pltpu.roll(t, R, 1), 0.0)
                total = total + jnp.where(has_high, pltpu.roll(t, nz - R, 1), 0.0)
                new[x] = (src[x] + con[x] * total) * inv[x]
            tem = new
        return [tem[W + x][W : W + cy, :] for x in range(cx)]

    def outer_kernel(k, split):
        first = k == 0

        def kernel(info, state, ins, ele, dop, cond, *rest):
            rest = list(rest)
            take = lambda c: [rest.pop(0) for _ in range(c)]
            accs = take(9)
            got0 = take(ux + uy)
            got = got0 if first else take(ux + uy)
            (tile,) = take(1)
            if not split:
                out, *faces = take(1 + ux)
                sends = take(uy)
            tile_out, rim_x, rim_y, temp, heat, ext, mobs = take(7)
            odd_x, odd_y = info[4] > 0.5, info[5] > 0.5

            if first:
                temp[...] = tile[...]
            else:
                own = [tile[f * cells : (f + 1) * cells, :] for f in range(3)]
                rows = sweeps(info, own, got[:ux], got[ux:], (3 * ny, 3 * nx), ext)
                for x in range(cx):
                    temp[x * cy : (x + 1) * cy, :] = rows[x]
            mobs[...] = 1.0 / (1.0 + DROP * temp[...])

            def side(axis, which, f):
                src = got0 if f == 3 else got
                if axis == 0:
                    return pick(odd_x, which, [r[f * ny : (f + 1) * ny, :] for r in src[:ux]])
                return pick(odd_y, which, [r[f * nx : (f + 1) * nx, :] for r in src[ux:]])

            def edge(rows):
                return [state[f, rows, :] for f in range(3)] + [epsof(ins[rows, :])]

            at = [
                (0, 0, slice(0, ny)), (0, 1, slice(nodes - ny, nodes)),
                (1, 0, pl.ds(0, nx, stride=ny)), (1, 1, pl.ds(ny - 1, nx, stride=ny)),
            ]
            for axis, which, rows in at:
                there = [side(axis, which, f) for f in range(4)]
                here = edge(rows)
                weight = info[2 * axis + which]
                f = face(here, there, weight) if which else turn(face(there, here, weight))
                for q, v in enumerate(f):
                    (rim_y if axis else rim_x)[9 * which + q] = v

            hsum = None
            for x in range(nx):
                rows = slice(x * ny, (x + 1) * ny)
                if split:
                    (h,) = whole(accs, rim_x, rim_y, x, [8])
                    h = h / (state[1, rows, :] + state[2, rows, :])
                else:
                    if x % R == 0:
                        mob = spread_rows(mobs, (x // R) * cy, cy)
                        dopx = spread_rows(dop, (x // R) * cy, cy)
                    here = [state[0, rows, :], state[1, rows, :], state[2, rows, :], None]
                    acc = whole(accs, rim_x, rim_y, x, range(9))
                    psi, n, p, h = solve(here, acc, ele[rows, :] == 1, dopx, mob)
                    out[0, rows, :] = psi
                    out[1, rows, :] = n
                    out[2, rows, :] = p
                hsum = h if x % R == 0 else hsum + h
                if x % R == R - 1:
                    xc = x // R
                    heat[xc * ny : (xc + 1) * ny, :] = hsum

            v = heat[pl.ds(0, cells, stride=R), :]
            for j in range(1, R):
                v = v + heat[pl.ds(j, cells, stride=R), :]
            lane = iota((cells, nz), 1)
            step = 1
            while step < R:
                v = v + jnp.where(
                    lane % (2 * step) < step, pltpu.roll(v, nz - step, 1), pltpu.roll(v, step, 1)
                )
                step *= 2
            tile_out[0:cells, :] = (GAIN * 0.5 / R**3) * mobs[...] * v
            tile_out[cells : 2 * cells, :] = temp[...]
            tile_out[2 * cells : 3 * cells, :] = cond[...]
            if not split:
                fields = [out.at[f] for f in range(3)]
                put_x(info, fields, faces)
                put_y(info, fields, sends)
                for s in sends:
                    s[3 * nx : 3 * nx + 3 * cells, :] = tile_out[...]

        return kernel

    def solve_kernel(info, state, ele, dop, tile, *rest):
        accs, (rim_x, rim_y, out, mobs) = rest[:9], rest[9:]
        mobs[...] = 1.0 / (1.0 + DROP * tile[cells : 2 * cells, :])
        for x in range(nx):
            rows = slice(x * ny, (x + 1) * ny)
            if x % R == 0:
                mob = spread_rows(mobs, (x // R) * cy, cy)
                dopx = spread_rows(dop, (x // R) * cy, cy)
            here = [state[0, rows, :], state[1, rows, :], state[2, rows, :], None]
            acc = whole(accs, rim_x, rim_y, x, range(8)) + [None]
            psi, n, p, _ = solve(here, acc, ele[rows, :] == 1, dopx, mob)
            out[0, rows, :] = psi
            out[1, rows, :] = n
            out[2, rows, :] = p

    def join_kernel(has_faces, base_y):
        def kernel(info, *rest):
            rest = list(rest)
            take = lambda c: [rest.pop(0) for _ in range(c)]
            faces = take(ux if has_faces else 0)
            (tile,) = take(1)
            got_y, sends = take(uy), take(ux)
            for k, s in enumerate(sends):
                at = 0
                if has_faces:
                    s[0 : 3 * ny, :] = faces[k][...]
                    at = 3 * ny
                s[at : at + 3 * cells, :] = tile[...]
                for b in range(uy):
                    at += 3 * cells
                    s[at : at + 3 * cells, :] = got_y[b][base_y : base_y + 3 * cells, :]

        return kernel

    def final_kernel(info, *rest):
        got, (tile, out, ext, flat) = rest[: ux + uy], rest[ux + uy :]
        own = [tile[f * cells : (f + 1) * cells, :] for f in range(3)]
        rows = sweeps(info, own, got[:ux], got[ux:], (0, 0), ext)
        for x in range(cx):
            flat[x * cy : (x + 1) * cy, :] = rows[x]
        coarse = nz // R
        sel = (iota((nz, coarse), 0) == R * iota((nz, coarse), 1)).astype(F32)
        out[...] = jnp.dot(
            flat[...], sel, precision=lax.Precision.HIGHEST, preferred_element_type=F32
        )

    def along(axis, pairings, sends):
        return [lax.ppermute(s, axis, pairs) for s, pairs in zip(sends, pairings)]

    def per_device(sol, ins, ele, zone, cat, warm):
        state = sol.reshape(3, nodes, nz)
        ins = ins.reshape(nodes, nz)
        ele = ele.reshape(nodes, nz)
        coarse = nz // R
        ix, iy = lax.axis_index("gx"), lax.axis_index("gy")
        info = jnp.stack(
            [ix > 0, ix < gx - 1, iy > 0, iy < gy - 1, ix % 2 == 1, iy % 2 == 1]
        ).astype(F32)
        work = nodes * nz
        V = pltpu.VMEM
        res = call(
            pack_kernel,
            [(4 * ny, nz)] * ux + [(4 * nx, nz)] * uy + [(cells, nz)] * 3,
            [V((3, nodes, nz), F32), V((nodes, nz), F32), V((nodes, nz), jnp.int32),
             pltpu.SemaphoreType.DMA((2,))],
            [info, state, ins, zone.reshape(cells, coarse), cat.reshape(cells, coarse),
             warm.reshape(cells, coarse)],
            work,
            specs=[smem, hbm, hbm, vmem, vmem, vmem],
        )
        sends, (dop, cond, tile) = res[: ux + uy], res[ux + uy :]
        got0 = along("gx", px, sends[:ux]) + along("gy", py, sends[ux:])
        got_y, faces = [], []
        for k in range(NEWTON):
            last = k == NEWTON - 1
            accs = call(inner_kernel, [(nodes, nz)] * 9, [], [info, state, ins], 200 * work)
            got = []
            if k:
                joined = call(
                    join_kernel(True, 3 * nx),
                    [(3 * ny + 3 * cells * (1 + uy), nz)] * ux,
                    [],
                    [info] + faces + [tile] + got_y,
                    work,
                )
                got = along("gx", px, joined) + got_y
            args = [info, state, ins, ele, dop, cond] + accs + got0 + got + [tile]
            outs = []
            if not last:
                outs += [(3, nodes, nz)] + [(3 * ny, nz)] * ux + [(3 * nx + 3 * cells, nz)] * uy
            outs += [(3 * cells, nz)]
            rims = [(18, ny, nz), (18, nx, nz)]
            scratch = [
                V((cells, nz), F32), V((cx * ny, nz), F32), V((3 * ex, ey, nz), F32),
                V((cells, nz), F32),
            ]
            if last:
                outs += rims
            else:
                scratch = [V(r, F32) for r in rims] + scratch
            res = call(outer_kernel(k, last), outs, scratch, args, 100 * work)
            if last:
                tile = res[0]
                got_y = along("gy", py, [tile] * uy)
                (state,) = call(
                    solve_kernel, [(3, nodes, nz)], [V((cells, nz), F32)],
                    [info, state, ele, dop, tile] + accs + res[1:], 100 * work,
                )
            else:
                state, faces, sends, tile = res[0], res[1 : 1 + ux], res[1 + ux : -1], res[-1]
                got_y = along("gy", py, sends)
        joined = call(
            join_kernel(False, 0), [(3 * cells * (1 + uy), nz)] * ux, [],
            [info, tile] + got_y, work,
        )
        got = along("gx", px, joined) + got_y
        (warm,) = call(
            final_kernel,
            [(cells, coarse)],
            [V((3 * ex, ey, nz), F32), V((cells, nz), F32)],
            [info] + got + [tile],
            work,
        )
        return state.reshape(3, nx, ny, nz), warm.reshape(cx, cy, coarse)

    return per_device


def solution(mesh):
    placed = (
        P(None, "gx", "gy", None),
        P("gx", "gy", None),
        P("gx", "gy", None),
        P("gx", "gy", None),
        P("gx", "gy", None),
        P("gx", "gy", None),
    )
    gx, gy = mesh.shape["gx"], mesh.shape["gy"]

    def body(sol, *rest):
        _, nx, ny, nz = sol.shape
        return make(nx, ny, nz, gx, gy)(sol, *rest)

    return jax.shard_map(
        body,
        mesh=mesh,
        in_specs=placed,
        out_specs=(P(None, "gx", "gy", None), P("gx", "gy", None)),
        check_vma=False,
    )
```

time: 56.8 us -> 51.4 us (0.905)
  the two profiles are of different devices: /device:TPU:1 before, /device:TPU:9 now
where the time goes in v2:
time: 51.4 us; the launch traced here: 51.1 us
  starting transfers between devices  19.9 us (39%)
  Pallas kernels  15.5 us (30%)
  waiting for transfers between devices  12.2 us (24%)
  local copies, waits for them, and re-layouts  2.61 us (5%)
  between operations  0.86 us (2%)
    ppermute x12, starting transfers between devices, along(): return [lax.ppermute(s, axis, pairs) for s, pairs in zip(sends, pairings)]  19.9 us
    pallas_call x12, Pallas kernels, call(): pl.pallas_call(kernel, out_shape=[jax.ShapeDtypeStruct(s, F32) for s in o...  15.5 us
    ppermute x12, waiting for transfers between devices, along(): return [lax.ppermute(s, axis, pairs) for s, pairs in zip(sends, pairings)]  12.2 us
    unnamed x14, local copies, waits for them, and re-layouts  2.5 us
  transfers between devices with their start and end apart: 12, of which 6 were waited for; matrix products, arithmetic and copies ran while one was open for 0% of the time, Pallas kernels for 15%

profile of v2, /device:TPU:9, one launch (start us, length us, event | category | flops | bytes accessed | tf_op | source)
XLA Modules:
  0.0 51.1 jit_solution(5438789482372430705)
XLA Ops:
  0.8 0.6 %copy-done.6 = f32[4,4,32]{2,1,0:T(4,128)S(1)} copy-done((f32[4,4,32]{2,1,0:T(4,128)S(1)}, f32[4,4,32]{2,1,0:T(4,128)}, u32[]{:S(2)}) %copy-start.6) | copy-done | bytes 2072
  1.4 0.9 %copy-done = s32[16,16,128]{2,1,0:T(8,128)S(1)} copy-done((s32[16,16,128]{2,1,0:T(8,128)S(1)}, s32[16,16,128]{2,1,0:T(8,128)}, u32[]{:S(2)}) %copy-start) | copy-done | bytes 131096
  2.3 1.0 %copy-done.2 = f32[3,16,16,128]{3,2,1,0:T(8,128)S(1)} copy-done((f32[3,16,16,128]{3,2,1,0:T(8,128)S(1)}, f32[3,16,16,128]{3,2,1,0:T(8,128)}, u32[]{:S(2)}) %copy-start.2) | copy-done | bytes 393240
  3.3 1.1 %shard_map.77 = (f32[64,128]{1,0:T(8,128)S(1)}, f32[64,128]{1,0:T(8,128)S(1)}, f32[64,128]{1,0:T(8,128)S(1)}, f32[16,128]{1,0:T(8,128)S(1)}, f32[16,128]{1,0:T(8,128)S(1)}, /*index=5*/f32[16,128]{1,0:T(8,128)S(1)}) custom-call(f32[6]{0:T(128)S(1)} %convert_element_type.3.info, f32[3,256,128]{2,1,0:T(8,128)S(1)} %bitcast.21, s32[256,128]{1,0:T(8,128)S(1)} %bitcast.14, ...), custom_call_target="tpu_custom_call" | custom-call | flops 32768 | tf_op jit(solution)/shard_map/pallas_call | solution.py:150
  4.4 0.7 %collective-permute-start = (f32[64,128]{1,0:T(8,128)S(1)}, f32[64,128]{1,0:T(8,128)S(1)}, u32[]{:S(2)}, u32[]{:S(2)}) collective-permute-start(f32[64,128]{1,0:T(8,128)S(1)} %get-tuple-element.65), channel_id=1, source_target_pairs={{0,2},{2,0},{4,6},{6,4},{8,10},{10,8},{12,14},{14,12},{16,18},{18,... | collective-permute-start | bytes 98312 | tf_op jit(solution)/shard_map/ppermute | solution.py:442
  5.2 3.0 %collective-permute-start.1 = (f32[64,128]{1,0:T(8,128)S(1)}, f32[64,128]{1,0:T(8,128)S(1)}, u32[]{:S(2)}, u32[]{:S(2)}) collective-permute-start(f32[64,128]{1,0:T(8,128)S(1)} %get-tuple-element.66), channel_id=1, source_target_pairs={{2,4},{4,2},{6,8},{8,6},{10,12},{12,10},{14,16},{16,14},{18,20},{2... | collective-permute-start | bytes 98312 | tf_op jit(solution)/shard_map/ppermute | solution.py:442
  8.2 1.3 %collective-permute-start.2 = (f32[64,128]{1,0:T(8,128)S(1)}, f32[64,128]{1,0:T(8,128)S(1)}, u32[]{:S(2)}, u32[]{:S(2)}) collective-permute-start(f32[64,128]{1,0:T(8,128)S(1)} %get-tuple-element.67), channel_id=1, source_target_pairs={{0,1},{1,0},{2,3},{3,2},{4,5},{5,4},{6,7},{7,6},{8,9},{9,8},{10,11... | collective-permute-start | bytes 98312 | tf_op jit(solution)/shard_map/ppermute | solution.py:442
  9.5 1.9 %shard_map.78 = (f32[256,128]{1,0:T(8,128)S(1)}, f32[256,128]{1,0:T(8,128)S(1)}, f32[256,128]{1,0:T(8,128)S(1)}, f32[256,128]{1,0:T(8,128)S(1)}, f32[256,128]{1,...) custom-call(f32[6]{0:T(128)S(1)} %convert_element_type.3.info, ...), custom_call_target="tpu_custom_call" | custom-call | flops 6553600 | tf_op jit(solution)/shard_map/pallas_call | solution.py:150
  11.5 1.3 %shard_map.79 = (f32[3,256,128]{2,1,0:T(8,128)S(1)}, f32[48,128]{1,0:T(8,128)S(1)}, f32[48,128]{1,0:T(8,128)S(1)}, f32[96,128]{1,0:T(8,128)S(1)}, f32[48,128]{1,0:T(8,128)S(1)}) custom-call(f32[6]{0:T(128)S(1)} %convert_element_type.3.info, f32[3,256,128]{2,1,0:T(8,128)S(1)} %bitcast.23, s32[256,128]{1,0:T(8,128)S(1)} %bitcast.16, s32[256,128]{1,0:T(8,128)S(1)} %bitcast.24, ...), custom_call_target="tpu_custom_call" | custom-call | flops 3276800 | tf_op jit(solution)/shard_map/pallas_call | solution.py:150
  12.8 0.8 %collective-permute-start.3 = (f32[96,128]{1,0:T(8,128)S(1)}, f32[96,128]{1,0:T(8,128)S(1)}, u32[]{:S(2)}, u32[]{:S(2)}) collective-permute-start(f32[96,128]{1,0:T(8,128)S(1)} %get-tuple-element.82), channel_id=1, source_target_pairs={{0,1},{1,0},{2,3},{3,2},{4,5},{5,4},{6,7},{7,6},{8,9},{9,8},{10,11... | collective-permute-start | bytes 147464 | tf_op jit(solution)/shard_map/ppermute | solution.py:442
  13.6 2.2 %collective-permute-done.3.rest_3_.rest_14_ = f32[96,128]{1,0:T(8,128)S(1)} collective-permute-done((f32[96,128]{1,0:T(8,128)S(1)}, f32[96,128]{1,0:T(8,128)S(1)}, u32[]{:S(2)}, u32[]{:S(2)}) %collective-permute-start.3) | collective-permute-done | bytes 49184 | tf_op jit(solution)/shard_map/ppermute | solution.py:442
  15.8 0.6 %shard_map.81 = (f32[144,128]{1,0:T(8,128)S(1)}, f32[144,128]{1,0:T(8,128)S(1)}) custom-call(f32[6]{0:T(128)S(1)} %convert_element_type.3.info, f32[48,128]{1,0:T(8,128)S(1)} %get-tuple-element.79.rest_0_, f32[48,128]{1,0:T(8,128)S(1)} %get-tuple-element.80.rest_1_, f32[48,128]{1,0:T(8,128)S(1)} %get-tuple-element.81.rest_2_.rest_15_, ...), custom_call_target="tpu_custom_call" | custom-call | flops 32768 | tf_op jit(solution)/shard_map/pallas_call | solution.py:150
  16.3 2.3 %collective-permute-start.4 = (f32[144,128]{1,0:T(8,128)S(1)}, f32[144,128]{1,0:T(8,128)S(1)}, u32[]{:S(2)}, u32[]{:S(2)}) collective-permute-start(f32[144,128]{1,0:T(8,128)S(1)} %get-tuple-element.83), channel_id=1, source_target_pairs={{0,2},{2,0},{4,6},{6,4},{8,10},{10,8},{12,14},{14,12},{16,18},{18,... | collective-permute-start | bytes 221192 | tf_op jit(solution)/shard_map/ppermute | solution.py:442
  18.6 2.4 %collective-permute-start.5 = (f32[144,128]{1,0:T(8,128)S(1)}, f32[144,128]{1,0:T(8,128)S(1)}, u32[]{:S(2)}, u32[]{:S(2)}) collective-permute-start(f32[144,128]{1,0:T(8,128)S(1)} %get-tuple-element.84), channel_id=1, source_target_pairs={{2,4},{4,2},{6,8},{8,6},{10,12},{12,10},{14,16},{16,14},{18,20},{2... | collective-permute-start | bytes 221192 | tf_op jit(solution)/shard_map/ppermute | solution.py:442
  21.1 1.9 %shard_map.80 = (f32[256,128]{1,0:T(8,128)S(1)}, f32[256,128]{1,0:T(8,128)S(1)}, f32[256,128]{1,0:T(8,128)S(1)}, f32[256,128]{1,0:T(8,128)S(1)}, f32[256,128]{1,...) custom-call(f32[6]{0:T(128)S(1)} %convert_element_type.3.info, ...), custom_call_target="tpu_custom_call" | custom-call | flops 6553600 | tf_op jit(solution)/shard_map/pallas_call | solution.py:150
  23.0 2.0 %collective-permute-done.5.rest_13_ = f32[144,128]{1,0:T(8,128)S(1)} collective-permute-done((f32[144,128]{1,0:T(8,128)S(1)}, f32[144,128]{1,0:T(8,128)S(1)}, u32[]{:S(2)}, u32[]{:S(2)}) %collective-permute-start.5) | collective-permute-done | bytes 73760 | tf_op jit(solution)/shard_map/ppermute | solution.py:442
  25.1 1.4 %shard_map.82 = (f32[3,256,128]{2,1,0:T(8,128)S(1)}, f32[48,128]{1,0:T(8,128)S(1)}, f32[48,128]{1,0:T(8,128)S(1)}, f32[96,128]{1,0:T(8,128)S(1)}, f32[48,128]{1,0:T(8,128)S(1)}) custom-call(f32[6]{0:T(128)S(1)} %convert_element_type.3.info, f32[3,256,128]{2,1,0:T(8,128)S(1)} %get-tuple-element.69.state, s32[256,128]{1,0:T(8,128)S(1)} %bitcast.18, ...), custom_call_target="tpu_custom_call" | custom-call | flops 3276800 | tf_op jit(solution)/shard_map/pallas_call | solution.py:150
  26.5 1.3 %collective-permute-start.6 = (f32[96,128]{1,0:T(8,128)S(1)}, f32[96,128]{1,0:T(8,128)S(1)}, u32[]{:S(2)}, u32[]{:S(2)}) collective-permute-start(f32[96,128]{1,0:T(8,128)S(1)} %get-tuple-element.98), channel_id=1, source_target_pairs={{0,1},{1,0},{2,3},{3,2},{4,5},{5,4},{6,7},{7,6},{8,9},{9,8},{10,11... | collective-permute-start | bytes 147464 | tf_op jit(solution)/shard_map/ppermute | solution.py:442
  27.8 1.7 %collective-permute-done.6.rest_3_.rest_14_ = f32[96,128]{1,0:T(8,128)S(1)} collective-permute-done((f32[96,128]{1,0:T(8,128)S(1)}, f32[96,128]{1,0:T(8,128)S(1)}, u32[]{:S(2)}, u32[]{:S(2)}) %collective-permute-start.6) | collective-permute-done | bytes 49184 | tf_op jit(solution)/shard_map/ppermute | solution.py:442
  29.5 0.6 %shard_map.84 = (f32[144,128]{1,0:T(8,128)S(1)}, f32[144,128]{1,0:T(8,128)S(1)}) custom-call(f32[6]{0:T(128)S(1)} %convert_element_type.3.info, f32[48,128]{1,0:T(8,128)S(1)} %get-tuple-element.95.rest_0_, f32[48,128]{1,0:T(8,128)S(1)} %get-tuple-element.96.rest_1_, f32[48,128]{1,0:T(8,128)S(1)} %get-tuple-element.97.rest_2_.rest_15_, ...), custom_call_target="tpu_custom_call" | custom-call | flops 32768 | tf_op jit(solution)/shard_map/pallas_call | solution.py:150
  30.1 1.4 %collective-permute-start.7 = (f32[144,128]{1,0:T(8,128)S(1)}, f32[144,128]{1,0:T(8,128)S(1)}, u32[]{:S(2)}, u32[]{:S(2)}) collective-permute-start(f32[144,128]{1,0:T(8,128)S(1)} %get-tuple-element.99), channel_id=1, source_target_pairs={{0,2},{2,0},{4,6},{6,4},{8,10},{10,8},{12,14},{14,12},{16,18},{18,... | collective-permute-start | bytes 221192 | tf_op jit(solution)/shard_map/ppermute | solution.py:442
  31.5 1.9 %collective-permute-start.8 = (f32[144,128]{1,0:T(8,128)S(1)}, f32[144,128]{1,0:T(8,128)S(1)}, u32[]{:S(2)}, u32[]{:S(2)}) collective-permute-start(f32[144,128]{1,0:T(8,128)S(1)} %get-tuple-element.100), channel_id=1, source_target_pairs={{2,4},{4,2},{6,8},{8,6},{10,12},{12,10},{14,16},{16,14},{18,20},{2... | collective-permute-start | bytes 221192 | tf_op jit(solution)/shard_map/ppermute | solution.py:442
  33.5 1.9 %shard_map.83 = (f32[256,128]{1,0:T(8,128)S(1)}, f32[256,128]{1,0:T(8,128)S(1)}, f32[256,128]{1,0:T(8,128)S(1)}, f32[256,128]{1,0:T(8,128)S(1)}, f32[256,128]{1,...) custom-call(f32[6]{0:T(128)S(1)} %convert_element_type.3.info, ...), custom_call_target="tpu_custom_call" | custom-call | flops 6553600 | tf_op jit(solution)/shard_map/pallas_call | solution.py:150
  35.4 2.6 %collective-permute-done.8.rest_13_ = f32[144,128]{1,0:T(8,128)S(1)} collective-permute-done((f32[144,128]{1,0:T(8,128)S(1)}, f32[144,128]{1,0:T(8,128)S(1)}, u32[]{:S(2)}, u32[]{:S(2)}) %collective-permute-start.8) | collective-permute-done | bytes 73760 | tf_op jit(solution)/shard_map/ppermute | solution.py:442
  38.0 0.9 %shard_map.85 = (f32[48,128]{1,0:T(8,128)S(1)}, f32[18,16,128]{2,1,0:T(8,128)S(1)}, f32[18,16,128]{2,1,0:T(8,128)S(1)}) custom-call(f32[6]{0:T(128)S(1)} %convert_element_type.3.info, f32[3,256,128]{2,1,0:T(8,128)S(1)} %get-tuple-element.85.state, s32[256,128]{1,0:T(8,128)S(1)} %bitcast.20, s32[256,128]{1,0:T(8,128)S(1)} %bitcast.26, ...), custom_call_target="tpu_custom_call" | custom-call | flops 3276800 | tf_op jit(solution)/shard_map/pallas_call | solution.py:150
  38.8 1.3 %collective-permute-start.9 = (f32[48,128]{1,0:T(8,128)S(1)}, f32[48,128]{1,0:T(8,128)S(1)}, u32[]{:S(2)}, u32[]{:S(2)}) collective-permute-start(f32[48,128]{1,0:T(8,128)S(1)} %get-tuple-element.101.tile.rest_0_.rest_3_), channel_id=1, source_target_pairs={{0,1},{1,0},{2,3},{3,2},{4,5},{5,4},{6,7},{7,6},{8,9},{9,8},{10,11... | collective-permute-start | bytes 73736 | tf_op jit(solution)/shard_map/ppermute | solution.py:442
  40.1 1.5 %collective-permute-done.9.rest_1_.rest_2_ = f32[48,128]{1,0:T(8,128)S(1)} collective-permute-done((f32[48,128]{1,0:T(8,128)S(1)}, f32[48,128]{1,0:T(8,128)S(1)}, u32[]{:S(2)}, u32[]{:S(2)}) %collective-permute-start.9) | collective-permute-done | bytes 24608 | tf_op jit(solution)/shard_map/ppermute | solution.py:442
  42.1 1.4 %collective-permute-start.10 = (f32[96,128]{1,0:T(8,128)S(1)}, f32[96,128]{1,0:T(8,128)S(1)}, u32[]{:S(2)}, u32[]{:S(2)}) collective-permute-start(f32[96,128]{1,0:T(8,128)S(1)} %get-tuple-element.104), channel_id=1, source_target_pairs={{0,2},{2,0},{4,6},{6,4},{8,10},{10,8},{12,14},{14,12},{16,18},{18,... | collective-permute-start | bytes 147464 | tf_op jit(solution)/shard_map/ppermute | solution.py:442
  43.6 1.9 %collective-permute-start.11 = (f32[96,128]{1,0:T(8,128)S(1)}, f32[96,128]{1,0:T(8,128)S(1)}, u32[]{:S(2)}, u32[]{:S(2)}) collective-permute-start(f32[96,128]{1,0:T(8,128)S(1)} %get-tuple-element.105), channel_id=1, source_target_pairs={{2,4},{4,2},{6,8},{8,6},{10,12},{12,10},{14,16},{16,14},{18,20},{2... | collective-permute-start | bytes 147464 | tf_op jit(solution)/shard_map/ppermute | solution.py:442
  45.5 1.8 %shard_map.86 = f32[3,256,128]{2,1,0:T(8,128)} custom-call(f32[6]{0:T(128)S(1)} %convert_element_type.3.info, f32[3,256,128]{2,1,0:T(8,128)S(1)} %get-tuple-element.85.state, s32[256,128]{1,0:T(8,128)S(1)} %bitcast.27, f32[16,128]{1,0:T(8,128)S(1)} %get-tuple-element.54.dop, f32[48,128]{1,0:T(8,128)S(1)} %get-tuple-element.101.tile.rest_0_.rest_3_, ...), custom_call_target="tpu_custom_call" | custom-call | flops 3276800 | tf_op jit(solution)/shard_map/pallas_call | solution.py:150
  47.3 2.2 %collective-permute-done.11.rest_1_ = f32[96,128]{1,0:T(8,128)S(1)} collective-permute-done((f32[96,128]{1,0:T(8,128)S(1)}, f32[96,128]{1,0:T(8,128)S(1)}, u32[]{:S(2)}, u32[]{:S(2)}) %collective-permute-start.11) | collective-permute-done | bytes 49184 | tf_op jit(solution)/shard_map/ppermute | solution.py:442
  49.5 1.6 %shard_map.88 = f32[16,32]{1,0:T(8,128)} custom-call(f32[6]{0:T(128)S(1)} %convert_element_type.3.info, f32[96,128]{1,0:T(8,128)S(1)} %collective-permute-done.10.rest_0_, f32[96,128]{1,0:T(8,128)S(1)} %collective-permute-done.11.rest_1_, f32[48,128]{1,0:T(8,128)S(1)} %collective-permute-done.9.rest_1_.rest_2_, ...), custom_call_target="tpu_custom_call" | custom-call | flops 32768 | tf_op jit(solution)/shard_map/pallas_call | solution.py:150
  (20 shorter events, 0.7 us)
Async XLA Ops:
  0.7 0.7 %copy-start.6 = (f32[4,4,32]{2,1,0:T(4,128)S(1)}, f32[4,4,32]{2,1,0:T(4,128)}, u32[]{:S(2)}) copy-start(f32[4,4,32]{2,1,0:T(4,128)} %param.11) | copy-start | bytes 6148
  0.7 0.7 %copy-start.4 = (s32[4,4,32]{2,1,0:T(4,128)S(1)}, s32[4,4,32]{2,1,0:T(4,128)}, u32[]{:S(2)}) copy-start(s32[4,4,32]{2,1,0:T(4,128)} %param.9) | copy-start | bytes 6148
  0.7 0.7 %copy-start.5 = (s32[4,4,32]{2,1,0:T(4,128)S(1)}, s32[4,4,32]{2,1,0:T(4,128)}, u32[]{:S(2)}) copy-start(s32[4,4,32]{2,1,0:T(4,128)} %param.10) | copy-start | bytes 6148
  1.4 0.9 %copy-start = (s32[16,16,128]{2,1,0:T(8,128)S(1)}, s32[16,16,128]{2,1,0:T(8,128)}, u32[]{:S(2)}) copy-start(s32[16,16,128]{2,1,0:T(8,128)} %param.7) | copy-start | bytes 393220
  2.3 1.0 %copy-start.2 = (f32[3,16,16,128]{3,2,1,0:T(8,128)S(1)}, f32[3,16,16,128]{3,2,1,0:T(8,128)}, u32[]{:S(2)}) copy-start(f32[3,16,16,128]{3,2,1,0:T(8,128)} %param.6) | copy-start | bytes 1179652
  4.4 7.0 %collective-permute-start = (f32[64,128]{1,0:T(8,128)S(1)}, f32[64,128]{1,0:T(8,128)S(1)}, u32[]{:S(2)}, u32[]{:S(2)}) collective-permute-start(f32[64,128]{1,0:T(8,128)S(1)} %get-tuple-element.65), channel_id=1, source_target_pairs={{0,2},{2,0},{4,6},{6,4},{8,10},{10,8},{12,14},{14,12},{16,18},{18,... | collective-permute-start | bytes 98312 | tf_op jit(solution)/shard_map/ppermute | solution.py:442
  5.2 6.3 %collective-permute-start.1 = (f32[64,128]{1,0:T(8,128)S(1)}, f32[64,128]{1,0:T(8,128)S(1)}, u32[]{:S(2)}, u32[]{:S(2)}) collective-permute-start(f32[64,128]{1,0:T(8,128)S(1)} %get-tuple-element.66), channel_id=1, source_target_pairs={{2,4},{4,2},{6,8},{8,6},{10,12},{12,10},{14,16},{16,14},{18,20},{2... | collective-permute-start | bytes 98312 | tf_op jit(solution)/shard_map/ppermute | solution.py:442
  8.2 3.3 %copy-start.3 = (s32[16,16,128]{2,1,0:T(8,128)S(1)}, s32[16,16,128]{2,1,0:T(8,128)}, u32[]{:S(2)}) copy-start(s32[16,16,128]{2,1,0:T(8,128)} %param.8) | copy-start | bytes 393220
  8.2 3.2 %collective-permute-start.2 = (f32[64,128]{1,0:T(8,128)S(1)}, f32[64,128]{1,0:T(8,128)S(1)}, u32[]{:S(2)}, u32[]{:S(2)}) collective-permute-start(f32[64,128]{1,0:T(8,128)S(1)} %get-tuple-element.67), channel_id=1, source_target_pairs={{0,1},{1,0},{2,3},{3,2},{4,5},{5,4},{6,7},{7,6},{8,9},{9,8},{10,11... | collective-permute-start | bytes 98312 | tf_op jit(solution)/shard_map/ppermute | solution.py:442
  12.8 8.3 %copy-start.1 = (s32[16,16,128]{2,1,0:T(8,128)S(1)}, s32[16,16,128]{2,1,0:T(8,128)}, u32[]{:S(2)}) copy-start(s32[16,16,128]{2,1,0:T(8,128)} %param.7) | copy-start | bytes 393220
  12.8 3.0 %collective-permute-start.3 = (f32[96,128]{1,0:T(8,128)S(1)}, f32[96,128]{1,0:T(8,128)S(1)}, u32[]{:S(2)}, u32[]{:S(2)}) collective-permute-start(f32[96,128]{1,0:T(8,128)S(1)} %get-tuple-element.82), channel_id=1, source_target_pairs={{0,1},{1,0},{2,3},{3,2},{4,5},{5,4},{6,7},{7,6},{8,9},{9,8},{10,11... | collective-permute-start | bytes 147464 | tf_op jit(solution)/shard_map/ppermute | solution.py:442
  16.3 6.7 %collective-permute-start.4 = (f32[144,128]{1,0:T(8,128)S(1)}, f32[144,128]{1,0:T(8,128)S(1)}, u32[]{:S(2)}, u32[]{:S(2)}) collective-permute-start(f32[144,128]{1,0:T(8,128)S(1)} %get-tuple-element.83), channel_id=1, source_target_pairs={{0,2},{2,0},{4,6},{6,4},{8,10},{10,8},{12,14},{14,12},{16,18},{18,... | collective-permute-start | bytes 221192 | tf_op jit(solution)/shard_map/ppermute | solution.py:442
  18.6 6.5 %collective-permute-start.5 = (f32[144,128]{1,0:T(8,128)S(1)}, f32[144,128]{1,0:T(8,128)S(1)}, u32[]{:S(2)}, u32[]{:S(2)}) collective-permute-start(f32[144,128]{1,0:T(8,128)S(1)} %get-tuple-element.84), channel_id=1, source_target_pairs={{2,4},{4,2},{6,8},{8,6},{10,12},{12,10},{14,16},{16,14},{18,20},{2... | collective-permute-start | bytes 221192 | tf_op jit(solution)/shard_map/ppermute | solution.py:442
  26.5 3.0 %collective-permute-start.6 = (f32[96,128]{1,0:T(8,128)S(1)}, f32[96,128]{1,0:T(8,128)S(1)}, u32[]{:S(2)}, u32[]{:S(2)}) collective-permute-start(f32[96,128]{1,0:T(8,128)S(1)} %get-tuple-element.98), channel_id=1, source_target_pairs={{0,1},{1,0},{2,3},{3,2},{4,5},{5,4},{6,7},{7,6},{8,9},{9,8},{10,11... | collective-permute-start | bytes 147464 | tf_op jit(solution)/shard_map/ppermute | solution.py:442
  30.1 5.3 %collective-permute-start.7 = (f32[144,128]{1,0:T(8,128)S(1)}, f32[144,128]{1,0:T(8,128)S(1)}, u32[]{:S(2)}, u32[]{:S(2)}) collective-permute-start(f32[144,128]{1,0:T(8,128)S(1)} %get-tuple-element.99), channel_id=1, source_target_pairs={{0,2},{2,0},{4,6},{6,4},{8,10},{10,8},{12,14},{14,12},{16,18},{18,... | collective-permute-start | bytes 221192 | tf_op jit(solution)/shard_map/ppermute | solution.py:442
  31.5 6.5 %collective-permute-start.8 = (f32[144,128]{1,0:T(8,128)S(1)}, f32[144,128]{1,0:T(8,128)S(1)}, u32[]{:S(2)}, u32[]{:S(2)}) collective-permute-start(f32[144,128]{1,0:T(8,128)S(1)} %get-tuple-element.100), channel_id=1, source_target_pairs={{2,4},{4,2},{6,8},{8,6},{10,12},{12,10},{14,16},{16,14},{18,20},{2... | collective-permute-start | bytes 221192 | tf_op jit(solution)/shard_map/ppermute | solution.py:442
  38.8 2.7 %collective-permute-start.9 = (f32[48,128]{1,0:T(8,128)S(1)}, f32[48,128]{1,0:T(8,128)S(1)}, u32[]{:S(2)}, u32[]{:S(2)}) collective-permute-start(f32[48,128]{1,0:T(8,128)S(1)} %get-tuple-element.101.tile.rest_0_.rest_3_), channel_id=1, source_target_pairs={{0,1},{1,0},{2,3},{3,2},{4,5},{5,4},{6,7},{7,6},{8,9},{9,8},{10,11... | collective-permute-start | bytes 73736 | tf_op jit(solution)/shard_map/ppermute | solution.py:442
  42.1 5.2 %collective-permute-start.10 = (f32[96,128]{1,0:T(8,128)S(1)}, f32[96,128]{1,0:T(8,128)S(1)}, u32[]{:S(2)}, u32[]{:S(2)}) collective-permute-start(f32[96,128]{1,0:T(8,128)S(1)} %get-tuple-element.104), channel_id=1, source_target_pairs={{0,2},{2,0},{4,6},{6,4},{8,10},{10,8},{12,14},{14,12},{16,18},{18,... | collective-permute-start | bytes 147464 | tf_op jit(solution)/shard_map/ppermute | solution.py:442
  43.6 5.9 %collective-permute-start.11 = (f32[96,128]{1,0:T(8,128)S(1)}, f32[96,128]{1,0:T(8,128)S(1)}, u32[]{:S(2)}, u32[]{:S(2)}) collective-permute-start(f32[96,128]{1,0:T(8,128)S(1)} %get-tuple-element.105), channel_id=1, source_target_pairs={{2,4},{4,2},{6,8},{8,6},{10,12},{12,10},{14,16},{16,14},{18,20},{2... | collective-permute-start | bytes 147464 | tf_op jit(solution)/shard_map/ppermute | solution.py:442

commit v3 on v2

--- a/solution.py
+++ b/solution.py
@@ -142,35 +142,41 @@
     ex, ey = cx + 2 * W, -(-(cy + 2 * W) // 8) * 8
     nodes = nx * ny
     params = pltpu.CompilerParams(vmem_limit_bytes=16 * 1024 * 1024)
-    smem = pl.BlockSpec(memory_space=pltpu.SMEM)
     vmem = pl.BlockSpec(memory_space=pltpu.VMEM)
-    hbm = pl.BlockSpec(memory_space=pl.ANY)
-
-    def call(kernel, outs, scratch, args, cost, specs=None):
-        return list(pl.pallas_call(
-            kernel,
-            out_shape=[jax.ShapeDtypeStruct(s, F32) for s in outs],
-            in_specs=specs or [smem] + [vmem] * (len(args) - 1),
-            out_specs=[vmem] * len(outs),
-            scratch_shapes=scratch,
-            compiler_params=params,
-            cost_estimate=pl.CostEstimate(flops=cost, bytes_accessed=0, transcendentals=0),
-        )(*args))
+    deep = {True: (W - 1, W, W - 1), False: (W - 1, W)}
+    wide = {f: sum(deep[f]) for f in deep}
+
+    def call(kernel, outs, scratch, args, cost):
+        return list(
+            pl.pallas_call(
+                kernel,
+                out_shape=[jax.ShapeDtypeStruct(s, F32) for s in outs],
+                in_specs=[vmem] * len(args),
+                out_specs=[vmem] * len(outs),
+                scratch_shapes=scratch,
+                compiler_params=params,
+                cost_estimate=pl.CostEstimate(flops=cost, bytes_accessed=0, transcendentals=0),
+            )(*args)
+        )
+
+    def place_of():
+        ix, iy = lax.axis_index("gx"), lax.axis_index("gy")
+        some = lambda test: jnp.where(test, 1.0, 0.0)
+        weights = [some(ix > 0), some(ix < gx - 1), some(iy > 0), some(iy < gy - 1)]
+        return ix % 2 == 1, iy % 2 == 1, weights
 
     def pick(odd, which, values):
         get = lambda k: values[k] if k < len(values) else jnp.zeros_like(values[0])
         return jnp.where(odd, get(which), get(1 - which))
 
-    def put_x(info, fields, sends):
-        odd = info[4] > 0.5
+    def put_x(odd, fields, sends):
         for f, ref in enumerate(fields):
             low, high = ref[0:ny, :], ref[(nx - 1) * ny : nodes, :]
             for k, send in enumerate(sends):
                 first, second = (low, high) if k == 0 else (high, low)
                 send[f * ny : (f + 1) * ny, :] = jnp.where(odd, first, second)
 
-    def put_y(info, fields, sends):
-        odd = info[5] > 0.5
+    def put_y(odd, fields, sends):
         for f, ref in enumerate(fields):
             low = ref[pl.ds(0, nx, stride=ny), :]
             high = ref[pl.ds(ny - 1, nx, stride=ny), :]
@@ -178,8 +184,25 @@
                 first, second = (low, high) if k == 0 else (high, low)
                 send[f * nx : (f + 1) * nx, :] = jnp.where(odd, first, second)
 
-    def epsof(marks):
-        return jnp.where(marks == 1, 0.4, 1.0)
+    def put_cells_y(odd, fresh, fields, sends, at):
+        for (ref, base), depth in zip(fields, deep[fresh]):
+            for i in range(depth):
+                low = ref[pl.ds(base + i, cx, stride=cy), :]
+                high = ref[pl.ds(base + cy - depth + i, cx, stride=cy), :]
+                for k, send in enumerate(sends):
+                    first, second = (low, high) if k == 0 else (high, low)
+                    send[at : at + cx, :] = jnp.where(odd, first, second)
+                at += cx
+
+    def put_cells_x(odd, fresh, fields, sends, at):
+        for (ref, base), depth in zip(fields, deep[fresh]):
+            low = ref[base : base + depth * cy, :]
+            high = ref[base + cells - depth * cy : base + cells, :]
+            for k, send in enumerate(sends):
+                first, second = (low, high) if k == 0 else (high, low)
+                send[at : at + depth * cy, :] = jnp.where(odd, first, second)
+            at += depth * cy
+        return at
 
     def turn(f):
         lap, es, fe, fh, gn, gp, b, bm, h = f
@@ -200,15 +223,13 @@
             out.append(jnp.concatenate(parts, 0) if len(parts) > 1 else parts[0])
         return out
 
-    def pack_kernel(info, state_h, ins_h, zone, cat, warm, *rest):
-        sends, (dop, cond, temp) = rest[: ux + uy], rest[ux + uy : ux + uy + 3]
-        state, eps, marks, sems = rest[ux + uy + 3 :]
-        copies = [
-            pltpu.make_async_copy(state_h, state, sems.at[0]),
-            pltpu.make_async_copy(ins_h, marks, sems.at[1]),
-        ]
-        for c in copies:
-            c.start()
+    def pack_kernel(start, *sends):
+        odd_x, odd_y, _ = place_of()
+        fields = [start.at[f] for f in range(4)]
+        put_x(odd_x, fields, sends[:ux])
+        put_y(odd_y, fields, sends[ux:])
+
+    def table_kernel(after, zone, cat, warm, dop, cond, temp):
         coarse = nz // R
         pickz = (iota((coarse, nz), 1) // R == iota((coarse, nz), 0)).astype(F32)
 
@@ -218,21 +239,15 @@
         dop[...] = widen(lookup(zone[...], DOPING))
         cond[...] = widen(lookup(cat[...], CONDUCT))
         temp[...] = widen(warm[...])
-        for c in copies:
-            c.wait()
-        eps[...] = epsof(marks[...])
-        fields = [state.at[0], state.at[1], state.at[2], eps]
-        put_x(info, fields, sends[:ux])
-        put_y(info, fields, sends[ux:])
-
-    def inner_kernel(info, state, ins, *accs):
+
+    def inner_kernel(state, eps, *accs):
         zlane = iota((ny, nz), 1)
         wz = jnp.where(zlane < nz - 1, 1.0, 0.0)
         wy = jnp.where(iota((ny, nz), 0) < ny - 1, 1.0, 0.0)
 
         def plane(x):
             rows = slice(x * ny, (x + 1) * ny)
-            return [state[0, rows, :], state[1, rows, :], state[2, rows, :], epsof(ins[rows, :])]
+            return [state[0, rows, :], state[1, rows, :], state[2, rows, :], eps[3, rows, :]]
 
         here = plane(0)
         acc = None
@@ -253,43 +268,65 @@
                 accs[q][x * ny : (x + 1) * ny, :] = acc[q]
             acc = later
 
-    def sweeps(info, own, tiles_x, tiles_y, base, ext):
-        odd_x, odd_y = info[4] > 0.5, info[5] > 0.5
+    def sweeps(fresh, own, tiles_x, tiles_y, base, ext, cext):
+        odd_x, odd_y, _ = place_of()
+        grids = [(ext, 0), (ext, ex), (cext, 0)]
         ext[...] = jnp.zeros_like(ext)
-
-        def grab(ref, f, at):
-            return ref[at + f * cells : at + (f + 1) * cells, :]
-
-        def place(f, sx, sy, tile):
-            xs = {-1: range(cx - W, cx), 0: range(cx), 1: range(W)}[sx]
-            lo, hi, to = {-1: (cy - W, cy, 0), 0: (0, cy, W), 1: (0, W, W + cy)}[sy]
-            at = {-1: 0, 0: W, 1: W + cx}[sx]
-            for k, x in enumerate(xs):
-                ext[f * ex + at + k, to : to + hi - lo, :] = tile[x * cy + lo : x * cy + hi, :]
-
-        for f in range(3):
-            place(f, 0, 0, own[f])
-            for sy in (-1, 1):
-                tile = pick(odd_y, (sy + 1) // 2, [grab(r, f, base[1]) for r in tiles_y])
-                place(f, 0, sy, tile)
-            for sx in (-1, 1):
-                tile = pick(odd_x, (sx + 1) // 2, [grab(r, f, base[0]) for r in tiles_x])
-                place(f, sx, 0, tile)
-                for sy in (-1, 1):
-                    along = [
-                        pick(
-                            odd_y,
-                            (sy + 1) // 2,
-                            [grab(r, f, base[0] + 3 * cells * (1 + b)) for b in range(uy)],
-                        )
-                        for r in tiles_x
-                    ]
-                    place(f, sx, sy, pick(odd_x, (sx + 1) // 2, along))
+        if fresh:
+            cext[...] = jnp.zeros_like(cext)
+        past = base[0] + wide[fresh] * cy
+        off_x, off_y = base[0], base[1]
+        gone = 0
+        for f, depth in enumerate(deep[fresh]):
+            (ref, row), (grid, g) = own[f], grids[f]
+            for x in range(cx):
+                grid[g + W + x, W : W + cy, :] = ref[row + x * cy : row + (x + 1) * cy, :]
+            for sy in (0, 1):
+                to = W + cy if sy else W - depth
+                for x in range(cx):
+                    tile = pick(
+                        odd_y, sy, [r[pl.ds(off_y + x, depth, stride=cx), :] for r in tiles_y]
+                    )
+                    grid[g + W + x, to : to + depth, :] = tile
+            for sx in (0, 1):
+                to = W + cx if sx else W - depth
+                tile = pick(odd_x, sx, [r[off_x : off_x + depth * cy, :] for r in tiles_x])
+                for i in range(depth):
+                    grid[g + to + i, W : W + cy, :] = tile[i * cy : (i + 1) * cy]
+                near = depth - 1
+                for i in range(near):
+                    x = i if sx else cx - near + i
+                    at = W + cx + i if sx else W - near + i
+                    for sy in (0, 1):
+                        skip = 0 if sy else depth - near
+                        along = [
+                            pick(
+                                odd_y,
+                                sy,
+                                [
+                                    r[
+                                        pl.ds(
+                                            past + b * wide[fresh] * cx + gone + skip * cx + x,
+                                            near,
+                                            stride=cx,
+                                        ),
+                                        :,
+                                    ]
+                                    for b in range(uy)
+                                ],
+                            )
+                            for r in tiles_x
+                        ]
+                        to_y = W + cy if sy else W - near
+                        grid[g + at, to_y : to_y + near, :] = pick(odd_x, sx, along)
+            off_x += depth * cy
+            off_y += depth * cx
+            gone += depth * cx
         lane = iota((ey, nz), 1)
         has_low, has_high = lane >= R, lane < nz - R
         src = [ext[x] for x in range(ex)]
         tem = [ext[ex + x] for x in range(ex)]
-        con = [ext[2 * ex + x] for x in range(ex)]
+        con = [cext[x] for x in range(ex)]
         inv = [1.0 / (SINK + 6.0 * c) for c in con]
         for s in range(1, W + 1):
             new = list(tem)
@@ -304,26 +341,30 @@
         return [tem[W + x][W : W + cy, :] for x in range(cx)]
 
     def outer_kernel(k, split):
-        first = k == 0
-
-        def kernel(info, state, ins, ele, dop, cond, *rest):
+        first, fresh = k == 0, k == 1
+
+        def kernel(state, eps, ele, dop, cond, *rest):
             rest = list(rest)
             take = lambda c: [rest.pop(0) for _ in range(c)]
             accs = take(9)
             got0 = take(ux + uy)
             got = got0 if first else take(ux + uy)
             (tile,) = take(1)
+            cext = None if first or fresh else take(1)[0]
             if not split:
                 out, *faces = take(1 + ux)
-                sends = take(uy)
-            tile_out, rim_x, rim_y, temp, heat, ext, mobs = take(7)
-            odd_x, odd_y = info[4] > 0.5, info[5] > 0.5
+            sends = take(uy)
+            (tile_out,) = take(1)
+            if fresh:
+                (cext,) = take(1)
+            rim_x, rim_y, temp, heat, ext, mobs = take(6)
+            odd_x, odd_y, weights = place_of()
 
             if first:
                 temp[...] = tile[...]
             else:
-                own = [tile[f * cells : (f + 1) * cells, :] for f in range(3)]
-                rows = sweeps(info, own, got[:ux], got[ux:], (3 * ny, 3 * nx), ext)
+                own = [(tile, 0), (tile, cells), (cond, 0)]
+                rows = sweeps(fresh, own, got[:ux], got[ux:], (3 * ny, 3 * nx), ext, cext)
                 for x in range(cx):
                     temp[x * cy : (x + 1) * cy, :] = rows[x]
             mobs[...] = 1.0 / (1.0 + DROP * temp[...])
@@ -335,7 +376,7 @@
                 return pick(odd_y, which, [r[f * nx : (f + 1) * nx, :] for r in src[ux:]])
 
             def edge(rows):
-                return [state[f, rows, :] for f in range(3)] + [epsof(ins[rows, :])]
+                return [state[f, rows, :] for f in range(3)] + [eps[3, rows, :]]
 
             at = [
                 (0, 0, slice(0, ny)), (0, 1, slice(nodes - ny, nodes)),
@@ -344,7 +385,7 @@
             for axis, which, rows in at:
                 there = [side(axis, which, f) for f in range(4)]
                 here = edge(rows)
-                weight = info[2 * axis + which]
+                weight = weights[2 * axis + which]
                 f = face(here, there, weight) if which else turn(face(there, here, weight))
                 for q, v in enumerate(f):
                     (rim_y if axis else rim_x)[9 * which + q] = v
@@ -382,18 +423,20 @@
                 step *= 2
             tile_out[0:cells, :] = (GAIN * 0.5 / R**3) * mobs[...] * v
             tile_out[cells : 2 * cells, :] = temp[...]
-            tile_out[2 * cells : 3 * cells, :] = cond[...]
+            at = 0
             if not split:
                 fields = [out.at[f] for f in range(3)]
-                put_x(info, fields, faces)
-                put_y(info, fields, sends)
-                for s in sends:
-                    s[3 * nx : 3 * nx + 3 * cells, :] = tile_out[...]
+                put_x(odd_x, fields, faces)
+                put_y(odd_y, fields, sends)
+                at = 3 * nx
+            parts = [(tile_out, 0), (tile_out, cells), (cond, 0)]
+            put_cells_y(odd_y, first, parts, sends, at)
 
         return kernel
 
-    def solve_kernel(info, state, ele, dop, tile, *rest):
-        accs, (rim_x, rim_y, out, mobs) = rest[:9], rest[9:]
+    def solve_kernel(state, ele, dop, tile, *rest):
+        accs, (rim_x, rim_y, out, token, mobs) = rest[:9], rest[9:]
+        token[...] = jnp.zeros_like(token)
         mobs[...] = 1.0 / (1.0 + DROP * tile[cells : 2 * cells, :])
         for x in range(nx):
             rows = slice(x * ny, (x + 1) * ny)
@@ -407,29 +450,31 @@
             out[1, rows, :] = n
             out[2, rows, :] = p
 
-    def join_kernel(has_faces, base_y):
-        def kernel(info, *rest):
+    def join_kernel(fresh, has_faces):
+        def kernel(after, cond, tile, *rest):
             rest = list(rest)
             take = lambda c: [rest.pop(0) for _ in range(c)]
             faces = take(ux if has_faces else 0)
-            (tile,) = take(1)
             got_y, sends = take(uy), take(ux)
+            odd_x, _, _ = place_of()
+            at = base = 0
+            if has_faces:
+                at, base = 3 * ny, 3 * nx
+                for k, s in enumerate(sends):
+                    s[0:at, :] = faces[k][...]
+            parts = [(tile, 0), (tile, cells), (cond, 0)]
+            at = put_cells_x(odd_x, fresh, parts, sends, at)
+            more = wide[fresh] * cx
             for k, s in enumerate(sends):
-                at = 0
-                if has_faces:
-                    s[0 : 3 * ny, :] = faces[k][...]
-                    at = 3 * ny
-                s[at : at + 3 * cells, :] = tile[...]
                 for b in range(uy):
-                    at += 3 * cells
-                    s[at : at + 3 * cells, :] = got_y[b][base_y : base_y + 3 * cells, :]
+                    s[at + b * more : at + (b + 1) * more, :] = got_y[b][base : base + more, :]
 
         return kernel
 
-    def final_kernel(info, *rest):
+    def final_kernel(cext, *rest):
         got, (tile, out, ext, flat) = rest[: ux + uy], rest[ux + uy :]
-        own = [tile[f * cells : (f + 1) * cells, :] for f in range(3)]
-        rows = sweeps(info, own, got[:ux], got[ux:], (0, 0), ext)
+        own = [(tile, 0), (tile, cells)]
+        rows = sweeps(False, own, got[:ux], got[ux:], (0, 0), ext, cext)
         for x in range(cx):
             flat[x * cy : (x + 1) * cy, :] = rows[x]
         coarse = nz // R
@@ -442,50 +487,49 @@
         return [lax.ppermute(s, axis, pairs) for s, pairs in zip(sends, pairings)]
 
     def per_device(sol, ins, ele, zone, cat, warm):
-        state = sol.reshape(3, nodes, nz)
-        ins = ins.reshape(nodes, nz)
         ele = ele.reshape(nodes, nz)
         coarse = nz // R
-        ix, iy = lax.axis_index("gx"), lax.axis_index("gy")
-        info = jnp.stack(
-            [ix > 0, ix < gx - 1, iy > 0, iy < gy - 1, ix % 2 == 1, iy % 2 == 1]
-        ).astype(F32)
         work = nodes * nz
         V = pltpu.VMEM
-        res = call(
-            pack_kernel,
-            [(4 * ny, nz)] * ux + [(4 * nx, nz)] * uy + [(cells, nz)] * 3,
-            [V((3, nodes, nz), F32), V((nodes, nz), F32), V((nodes, nz), jnp.int32),
-             pltpu.SemaphoreType.DMA((2,))],
-            [info, state, ins, zone.reshape(cells, coarse), cat.reshape(cells, coarse),
+        eps = jnp.where(ins.reshape(1, nodes, nz) == 1, 0.4, 1.0).astype(F32)
+        state = eps = jnp.concatenate([sol.reshape(3, nodes, nz), eps], 0)
+        sends = call(
+            pack_kernel, [(4 * ny, nz)] * ux + [(4 * nx, nz)] * uy, [], [state], work
+        )
+        dop, cond, tile = call(
+            table_kernel, [(cells, nz)] * 3, [],
+            [sends[0], zone.reshape(cells, coarse), cat.reshape(cells, coarse),
              warm.reshape(cells, coarse)],
             work,
-            specs=[smem, hbm, hbm, vmem, vmem, vmem],
         )
-        sends, (dop, cond, tile) = res[: ux + uy], res[ux + uy :]
         got0 = along("gx", px, sends[:ux]) + along("gy", py, sends[ux:])
-        got_y, faces = [], []
+        got_y, faces, cext = [], [], []
         for k in range(NEWTON):
-            last = k == NEWTON - 1
-            accs = call(inner_kernel, [(nodes, nz)] * 9, [], [info, state, ins], 200 * work)
+            first, fresh, last = k == 0, k == 1, k == NEWTON - 1
+            accs = call(inner_kernel, [(nodes, nz)] * 9, [], [state, eps], 200 * work)
             got = []
-            if k:
+            if not first:
                 joined = call(
-                    join_kernel(True, 3 * nx),
-                    [(3 * ny + 3 * cells * (1 + uy), nz)] * ux,
+                    join_kernel(fresh, True),
+                    [(3 * ny + wide[fresh] * (cy + cx * uy), nz)] * ux,
                     [],
-                    [info] + faces + [tile] + got_y,
+                    [accs[0], cond, tile] + faces + got_y,
                     work,
                 )
                 got = along("gx", px, joined) + got_y
-            args = [info, state, ins, ele, dop, cond] + accs + got0 + got + [tile]
+            args = [state, eps, ele, dop, cond] + accs + got0 + got + [tile]
             outs = []
+            if not (first or fresh):
+                args += cext
             if not last:
-                outs += [(3, nodes, nz)] + [(3 * ny, nz)] * ux + [(3 * nx + 3 * cells, nz)] * uy
-            outs += [(3 * cells, nz)]
+                outs += [(3, nodes, nz)] + [(3 * ny, nz)] * ux
+            outs += [((0 if last else 3 * nx) + wide[first] * cx, nz)] * uy
+            outs += [(2 * cells, nz)]
+            if fresh:
+                outs += [(ex, ey, nz)]
             rims = [(18, ny, nz), (18, nx, nz)]
             scratch = [
-                V((cells, nz), F32), V((cx * ny, nz), F32), V((3 * ex, ey, nz), F32),
+                V((cells, nz), F32), V((cx * ny, nz), F32), V((2 * ex, ey, nz), F32),
                 V((cells, nz), F32),
             ]
             if last:
@@ -493,26 +537,28 @@
             else:
                 scratch = [V(r, F32) for r in rims] + scratch
             res = call(outer_kernel(k, last), outs, scratch, args, 100 * work)
+            take = lambda c: [res.pop(0) for _ in range(c)]
+            if not last:
+                state, *faces = take(1 + ux)
+            got_y = along("gy", py, take(uy))
+            (tile,) = take(1)
+            if fresh:
+                cext = take(1)
             if last:
-                tile = res[0]
-                got_y = along("gy", py, [tile] * uy)
-                (state,) = call(
-                    solve_kernel, [(3, nodes, nz)], [V((cells, nz), F32)],
-                    [info, state, ele, dop, tile] + accs + res[1:], 100 * work,
+                state, token = call(
+                    solve_kernel, [(3, nodes, nz), (8, nz)], [V((cells, nz), F32)],
+                    [state, ele, dop, tile] + accs + res, 100 * work,
                 )
-            else:
-                state, faces, sends, tile = res[0], res[1 : 1 + ux], res[1 + ux : -1], res[-1]
-                got_y = along("gy", py, sends)
         joined = call(
-            join_kernel(False, 0), [(3 * cells * (1 + uy), nz)] * ux, [],
-            [info, tile] + got_y, work,
+            join_kernel(False, False), [(wide[False] * (cy + cx * uy), nz)] * ux, [],
+            [token, cond, tile] + got_y, work,
         )
         got = along("gx", px, joined) + got_y
         (warm,) = call(
             final_kernel,
             [(cells, coarse)],
-            [V((3 * ex, ey, nz), F32), V((cells, nz), F32)],
-            [info] + got + [tile],
+            [V((2 * ex, ey, nz), F32), V((cells, nz), F32)],
+            cext + got + [tile],
             work,
         )
         return state.reshape(3, nx, ny, nz), warm.reshape(cx, cy, coarse)

time: 51.4 us -> 43.7 us (0.85)
  Pallas kernels: 15.5 us -> 8.63 us
  local copies, waits for them, and re-layouts: 2.61 us -> 0.02 us
  other arithmetic: 0.01 us -> 1.96 us
    pallas_call x12 -> x13, Pallas kernels: 15.5 us -> 8.63 us  [call(): pl.pallas_call(kernel, out_shape=[jax.ShapeDtypeStruct(s, F32) for s in o...]
    unnamed x14 -> x8, local copies, waits for them, and re-layouts: 2.5 us -> 0.02 us
    concatenate x0 -> x1, other arithmetic: none -> 1.04 us  [per_device(): state = eps = jnp.concatenate([sol.reshape(3, nodes, nz), eps], 0)]
    select_n x0 -> x1, other arithmetic: none -> 0.92 us  [per_device(): eps = jnp.where(ins.reshape(1, nodes, nz) == 1, 0.4, 1.0).astype(F32)]
  transfers between devices with their start and end apart: 12 -> 12, of which waited for: 6 -> 6; matrix products, arithmetic and copies ran while one was open for 0% -> 0% of each run, Pallas kernels for 15% -> 13%
where the time goes in v3:
time: 43.7 us; the launch traced here: 43.4 us
  starting transfers between devices  20.3 us (46%)
  waiting for transfers between devices  11.7 us (27%)
  Pallas kernels  8.63 us (20%)
  other arithmetic  1.96 us (4%)
  between operations  0.78 us (2%)
    ppermute x12, starting transfers between devices, along(): return [lax.ppermute(s, axis, pairs) for s, pairs in zip(sends, pairings)]  20.3 us
    ppermute x12, waiting for transfers between devices, along(): return [lax.ppermute(s, axis, pairs) for s, pairs in zip(sends, pairings)]  11.7 us
    pallas_call x13, Pallas kernels, call(): pl.pallas_call(kernel, out_shape=[jax.ShapeDtypeStruct(s, F32) for s in o...  8.63 us
    concatenate x1, other arithmetic, per_device(): state = eps = jnp.concatenate([sol.reshape(3, nodes, nz), eps], 0)  1.04 us
    select_n x1, other arithmetic, per_device(): eps = jnp.where(ins.reshape(1, nodes, nz) == 1, 0.4, 1.0).astype(F32)  0.92 us
  transfers between devices with their start and end apart: 12, of which 6 were waited for; matrix products, arithmetic and copies ran while one was open for 0% of the time, Pallas kernels for 13%

profile of v3, /device:TPU:9, one launch (start us, length us, event | category | flops | bytes accessed | tf_op | source)
XLA Modules:
  0.0 43.4 jit_solution(6000674743143461925)
XLA Ops:
  0.6 0.9 %compare_select_fusion = f32[16,16,128]{2,1,0:T(8,128)S(1)} fusion(s32[16,16,128]{2,1,0:T(8,128)} %param.7), kind=kLoop, calls=%fused_computation.1 | loop fusion | flops 65536 | bytes 262144 | tf_op jit(solution)/shard_map/jit(_where)/select_n | solution.py:494
  1.6 1.0 %pad_maximum_fusion.start.state.eps = f32[4,256,128]{2,1,0:T(8,128)S(1)} fusion(f32[1,256,128]{2,1,0:T(8,128)S(1)} %bitcast.15, f32[3,256,128]{2,1,0:T(8,128)} %bitcast.16), kind=kLoop, calls=%fused_computation | loop fusion | flops 131072 | bytes 1048576 | tf_op jit(solution)/shard_map/concatenate | solution.py:495
  2.6 0.0 copy-start.2
  2.6 0.0 copy-start.3
  2.7 0.0 copy-start.1
  2.7 3.7 %collective-permute-start.1 = (f32[64,128]{1,0:T(8,128)S(1)}, f32[64,128]{1,0:T(8,128)S(1)}, u32[]{:S(2)}, u32[]{:S(2)}) collective-permute-start(f32[64,128]{1,0:T(8,128)S(1)} %get-tuple-element.70), channel_id=1, source_target_pairs={{2,4},{4,2},{6,8},{8,6},{10,12},{12,10},{14,16},{16,14},{18,20},{2... | collective-permute-start | bytes 98312 | tf_op jit(solution)/shard_map/ppermute | solution.py:487
  6.4 1.3 %collective-permute-start.2 = (f32[64,128]{1,0:T(8,128)S(1)}, f32[64,128]{1,0:T(8,128)S(1)}, u32[]{:S(2)}, u32[]{:S(2)}) collective-permute-start(f32[64,128]{1,0:T(8,128)S(1)} %get-tuple-element.71), channel_id=1, source_target_pairs={{0,1},{1,0},{2,3},{3,2},{4,5},{5,4},{6,7},{7,6},{8,9},{9,8},{10,11... | collective-permute-start | bytes 98312 | tf_op jit(solution)/shard_map/ppermute | solution.py:487
  7.7 0.2 shard_map.78
  7.8 1.4 %shard_map.79 = (f32[256,128]{1,0:T(8,128)S(1)}, f32[256,128]{1,0:T(8,128)S(1)}, f32[256,128]{1,0:T(8,128)S(1)}, f32[256,128]{1,0:T(8,128)S(1)}, f32[256,128]{1,...) custom-call(f32[4,256,128]{2,1,0:T(8,128)S(1)} %pad_maximum_fusion.s, ...), custom_call_target="tpu_custom_call" | custom-call | flops 6553600 | tf_op jit(solution)/shard_map/pallas_call | solution.py:151
  9.3 0.4 collective-permute-done.2.rest_11_
  9.7 0.7 %shard_map.80 = (f32[3,256,128]{2,1,0:T(8,128)S(1)}, f32[48,128]{1,0:T(8,128)S(1)}, f32[48,128]{1,0:T(8,128)S(1)}, f32[76,128]{1,0:T(8,128)S(1)}, f32[32,128]{1,0:T(8,128)S(1)}) custom-call(f32[4,256,128]{2,1,0:T(8,128)S(1)} %pad_maximum_fusion.start.state.eps, f32[4,256,128]{2,1,0:T(8,128)S(1)} %pad_maximum_fusion.start.state.eps, s32[256,128]{1,0:T(8,128)S(1)} %bitcast.8, ...), custom_call_target="tpu_custom_call" | custom-call | flops 3276800 | tf_op jit(solution)/shard_map/pallas_call | solution.py:151
  10.4 1.3 %collective-permute-start.3 = (f32[76,128]{1,0:T(8,128)S(1)}, f32[76,128]{1,0:T(8,128)S(1)}, u32[]{:S(2)}, u32[]{:S(2)}) collective-permute-start(f32[76,128]{1,0:T(8,128)S(1)} %get-tuple-element.86), channel_id=1, source_target_pairs={{0,1},{1,0},{2,3},{3,2},{4,5},{5,4},{6,7},{7,6},{8,9},{9,8},{10,11... | collective-permute-start | bytes 116744 | tf_op jit(solution)/shard_map/ppermute | solution.py:487
  11.7 1.4 %shard_map.81 = (f32[256,128]{1,0:T(8,128)S(1)}, f32[256,128]{1,0:T(8,128)S(1)}, f32[256,128]{1,0:T(8,128)S(1)}, f32[256,128]{1,0:T(8,128)S(1)}, f32[256,128]{1,...) custom-call(f32[3,256,128]{2,1,0:T(8,128)S(1)} %get-tuple-element.73, ...), custom_call_target="tpu_custom_call" | custom-call | flops 6553600 | tf_op jit(solution)/shard_map/pallas_call | solution.py:151
  13.1 0.2 collective-permute-done.3.rest_2_.rest_14_
  13.3 1.8 %collective-permute-start.4 = (f32[104,128]{1,0:T(8,128)S(1)}, f32[104,128]{1,0:T(8,128)S(1)}, u32[]{:S(2)}, u32[]{:S(2)}) collective-permute-start(f32[104,128]{1,0:T(8,128)S(1)} %get-tuple-element.87), channel_id=1, source_target_pairs={{0,2},{2,0},{4,6},{6,4},{8,10},{10,8},{12,14},{14,12},{16,18},{18,... | collective-permute-start | bytes 159752 | tf_op jit(solution)/shard_map/ppermute | solution.py:487
  15.1 2.6 %collective-permute-start.5 = (f32[104,128]{1,0:T(8,128)S(1)}, f32[104,128]{1,0:T(8,128)S(1)}, u32[]{:S(2)}, u32[]{:S(2)}) collective-permute-start(f32[104,128]{1,0:T(8,128)S(1)} %get-tuple-element.88), channel_id=1, source_target_pairs={{2,4},{4,2},{6,8},{8,6},{10,12},{12,10},{14,16},{16,14},{18,20},{2... | collective-permute-start | bytes 159752 | tf_op jit(solution)/shard_map/ppermute | solution.py:487
  17.8 3.4 %collective-permute-done.5.rest_13_ = f32[104,128]{1,0:T(8,128)S(1)} collective-permute-done((f32[104,128]{1,0:T(8,128)S(1)}, f32[104,128]{1,0:T(8,128)S(1)}, u32[]{:S(2)}, u32[]{:S(2)}) %collective-permute-start.5) | collective-permute-done | bytes 53280 | tf_op jit(solution)/shard_map/ppermute | solution.py:487
  21.2 0.9 %shard_map.83 = (f32[3,256,128]{2,1,0:T(8,128)S(1)}, f32[48,128]{1,0:T(8,128)S(1)}, f32[48,128]{1,0:T(8,128)S(1)}, f32[68,128]{1,0:T(8,128)S(1)}, f32[32,128]{1,0:T(8,128)S(1)}, /*index=5*/f32[10,16,128]{2,1,0:T(8,128)S(1)}) custom-call(f32[3,256,128]{2,1,0:T(8,128)S(1)} %get-tuple-element.73.state, f32[4,256,128]{2,1,0:T(8,128)S(1)} %pad_maximum_fusion.start.state.eps, ...), custom_call_target="tpu_custom_call" | custom-call | flops 3276800 | tf_op jit(solution)/shard_map/pallas_call | solution.py:151
  22.0 1.3 %collective-permute-start.6 = (f32[68,128]{1,0:T(8,128)S(1)}, f32[68,128]{1,0:T(8,128)S(1)}, u32[]{:S(2)}, u32[]{:S(2)}) collective-permute-start(f32[68,128]{1,0:T(8,128)S(1)} %get-tuple-element.102), channel_id=1, source_target_pairs={{0,1},{1,0},{2,3},{3,2},{4,5},{5,4},{6,7},{7,6},{8,9},{9,8},{10,11... | collective-permute-start | bytes 104456 | tf_op jit(solution)/shard_map/ppermute | solution.py:487
  23.3 1.4 %shard_map.84 = (f32[256,128]{1,0:T(8,128)S(1)}, f32[256,128]{1,0:T(8,128)S(1)}, f32[256,128]{1,0:T(8,128)S(1)}, f32[256,128]{1,0:T(8,128)S(1)}, f32[256,128]{1,...) custom-call(f32[3,256,128]{2,1,0:T(8,128)S(1)} %get-tuple-element.89, ...), custom_call_target="tpu_custom_call" | custom-call | flops 6553600 | tf_op jit(solution)/shard_map/pallas_call | solution.py:151
  24.7 0.2 collective-permute-done.6.rest_2_.rest_14_
  24.9 1.7 %collective-permute-start.7 = (f32[88,128]{1,0:T(8,128)S(1)}, f32[88,128]{1,0:T(8,128)S(1)}, u32[]{:S(2)}, u32[]{:S(2)}) collective-permute-start(f32[88,128]{1,0:T(8,128)S(1)} %get-tuple-element.103), channel_id=1, source_target_pairs={{0,2},{2,0},{4,6},{6,4},{8,10},{10,8},{12,14},{14,12},{16,18},{18,... | collective-permute-start | bytes 135176 | tf_op jit(solution)/shard_map/ppermute | solution.py:487
  26.6 1.9 %collective-permute-start.8 = (f32[88,128]{1,0:T(8,128)S(1)}, f32[88,128]{1,0:T(8,128)S(1)}, u32[]{:S(2)}, u32[]{:S(2)}) collective-permute-start(f32[88,128]{1,0:T(8,128)S(1)} %get-tuple-element.104), channel_id=1, source_target_pairs={{2,4},{4,2},{6,8},{8,6},{10,12},{12,10},{14,16},{16,14},{18,20},{2... | collective-permute-start | bytes 135176 | tf_op jit(solution)/shard_map/ppermute | solution.py:487
  28.5 4.0 %collective-permute-done.8.rest_13_ = f32[88,128]{1,0:T(8,128)S(1)} collective-permute-done((f32[88,128]{1,0:T(8,128)S(1)}, f32[88,128]{1,0:T(8,128)S(1)}, u32[]{:S(2)}, u32[]{:S(2)}) %collective-permute-start.8) | collective-permute-done | bytes 45088 | tf_op jit(solution)/shard_map/ppermute | solution.py:487
  32.5 0.3 shard_map.86
  32.8 1.3 %collective-permute-start.9 = (f32[20,128]{1,0:T(8,128)S(1)}, f32[20,128]{1,0:T(8,128)S(1)}, u32[]{:S(2)}, u32[]{:S(2)}) collective-permute-start(f32[20,128]{1,0:T(8,128)S(1)} %get-tuple-element.111), channel_id=1, source_target_pairs={{0,1},{1,0},{2,3},{3,2},{4,5},{5,4},{6,7},{7,6},{8,9},{9,8},{10,11... | collective-permute-start | bytes 30728 | tf_op jit(solution)/shard_map/ppermute | solution.py:487
  34.0 1.3 %shard_map.87 = (f32[3,256,128]{2,1,0:T(8,128)}, f32[8,128]{1,0:T(8,128)S(1)}) custom-call(f32[3,256,128]{2,1,0:T(8,128)S(1)} %get-tuple-element.89.state, s32[256,128]{1,0:T(8,128)S(1)} %bitcast.11, f32[16,128]{1,0:T(8,128)S(1)} %get-tuple-element.59.dop, f32[32,128]{1,0:T(8,128)S(1)} %get-tuple-element.106.tile.rest_3_, ...), custom_call_target="tpu_custom_call" | custom-call | flops 3276800 | tf_op jit(solution)/shard_map/pallas_call | solution.py:151
  35.3 0.0 collective-permute-done.9.rest_0_.rest_2_
  35.4 1.6 %collective-permute-start.10 = (f32[40,128]{1,0:T(8,128)S(1)}, f32[40,128]{1,0:T(8,128)S(1)}, u32[]{:S(2)}, u32[]{:S(2)}) collective-permute-start(f32[40,128]{1,0:T(8,128)S(1)} %get-tuple-element.112), channel_id=1, source_target_pairs={{0,2},{2,0},{4,6},{6,4},{8,10},{10,8},{12,14},{14,12},{16,18},{18,... | collective-permute-start | bytes 61448 | tf_op jit(solution)/shard_map/ppermute | solution.py:487
  37.0 1.9 %collective-permute-start.11 = (f32[40,128]{1,0:T(8,128)S(1)}, f32[40,128]{1,0:T(8,128)S(1)}, u32[]{:S(2)}, u32[]{:S(2)}) collective-permute-start(f32[40,128]{1,0:T(8,128)S(1)} %get-tuple-element.113), channel_id=1, source_target_pairs={{2,4},{4,2},{6,8},{8,6},{10,12},{12,10},{14,16},{16,14},{18,20},{2... | collective-permute-start | bytes 61448 | tf_op jit(solution)/shard_map/ppermute | solution.py:487
  39.0 3.5 %collective-permute-done.11.rest_1_ = f32[40,128]{1,0:T(8,128)S(1)} collective-permute-done((f32[40,128]{1,0:T(8,128)S(1)}, f32[40,128]{1,0:T(8,128)S(1)}, u32[]{:S(2)}, u32[]{:S(2)}) %collective-permute-start.11) | collective-permute-done | bytes 20512 | tf_op jit(solution)/shard_map/ppermute | solution.py:487
  42.4 1.0 %shard_map.89 = f32[16,32]{1,0:T(8,128)} custom-call(f32[10,16,128]{2,1,0:T(8,128)S(1)} %get-tuple-element.105.rest_16_.cext, f32[40,128]{1,0:T(8,128)S(1)} %collective-permute-done.10.rest_0_, f32[40,128]{1,0:T(8,128)S(1)} %collective-permute-done.11.rest_1_, f32[20,128]{1,0:T(8,128)S(1)} %collective-permute-done.9.rest_0_.rest_2_, ...), custom_call_target="tpu_custom_call" | custom-call | flops 32768 | tf_op jit(solution)/shard_map/pallas_call | solution.py:151
  (15 shorter events, 0.1 us)
Async XLA Ops:
  2.6 5.1 %copy-start.2 = (s32[4,4,32]{2,1,0:T(4,128)S(1)}, s32[4,4,32]{2,1,0:T(4,128)}, u32[]{:S(2)}) copy-start(s32[4,4,32]{2,1,0:T(4,128)} %param.10) | copy-start | bytes 6148
  2.6 5.1 %copy-start.3 = (f32[4,4,32]{2,1,0:T(4,128)S(1)}, f32[4,4,32]{2,1,0:T(4,128)}, u32[]{:S(2)}) copy-start(f32[4,4,32]{2,1,0:T(4,128)} %param.11) | copy-start | bytes 6148
  2.7 5.0 %copy-start.1 = (s32[4,4,32]{2,1,0:T(4,128)S(1)}, s32[4,4,32]{2,1,0:T(4,128)}, u32[]{:S(2)}) copy-start(s32[4,4,32]{2,1,0:T(4,128)} %param.9) | copy-start | bytes 6148
  2.7 6.6 %collective-permute-start.1 = (f32[64,128]{1,0:T(8,128)S(1)}, f32[64,128]{1,0:T(8,128)S(1)}, u32[]{:S(2)}, u32[]{:S(2)}) collective-permute-start(f32[64,128]{1,0:T(8,128)S(1)} %get-tuple-element.70), channel_id=1, source_target_pairs={{2,4},{4,2},{6,8},{8,6},{10,12},{12,10},{14,16},{16,14},{18,20},{2... | collective-permute-start | bytes 98312 | tf_op jit(solution)/shard_map/ppermute | solution.py:487
  6.4 3.3 %collective-permute-start.2 = (f32[64,128]{1,0:T(8,128)S(1)}, f32[64,128]{1,0:T(8,128)S(1)}, u32[]{:S(2)}, u32[]{:S(2)}) collective-permute-start(f32[64,128]{1,0:T(8,128)S(1)} %get-tuple-element.71), channel_id=1, source_target_pairs={{0,1},{1,0},{2,3},{3,2},{4,5},{5,4},{6,7},{7,6},{8,9},{9,8},{10,11... | collective-permute-start | bytes 98312 | tf_op jit(solution)/shard_map/ppermute | solution.py:487
  7.7 2.0 %collective-permute-start = (f32[64,128]{1,0:T(8,128)S(1)}, f32[64,128]{1,0:T(8,128)S(1)}, u32[]{:S(2)}, u32[]{:S(2)}) collective-permute-start(f32[64,128]{1,0:T(8,128)S(1)} %get-tuple-element.58.after), channel_id=1, source_target_pairs={{0,2},{2,0},{4,6},{6,4},{8,10},{10,8},{12,14},{14,12},{16,18},{18,... | collective-permute-start | bytes 98312 | tf_op jit(solution)/shard_map/ppermute | solution.py:487
  7.8 1.8 %copy-start = (s32[16,16,128]{2,1,0:T(8,128)S(1)}, s32[16,16,128]{2,1,0:T(8,128)}, u32[]{:S(2)}) copy-start(s32[16,16,128]{2,1,0:T(8,128)} %param.8) | copy-start | bytes 393220
  10.4 2.9 %collective-permute-start.3 = (f32[76,128]{1,0:T(8,128)S(1)}, f32[76,128]{1,0:T(8,128)S(1)}, u32[]{:S(2)}, u32[]{:S(2)}) collective-permute-start(f32[76,128]{1,0:T(8,128)S(1)} %get-tuple-element.86), channel_id=1, source_target_pairs={{0,1},{1,0},{2,3},{3,2},{4,5},{5,4},{6,7},{7,6},{8,9},{9,8},{10,11... | collective-permute-start | bytes 116744 | tf_op jit(solution)/shard_map/ppermute | solution.py:487
  13.3 4.4 %collective-permute-start.4 = (f32[104,128]{1,0:T(8,128)S(1)}, f32[104,128]{1,0:T(8,128)S(1)}, u32[]{:S(2)}, u32[]{:S(2)}) collective-permute-start(f32[104,128]{1,0:T(8,128)S(1)} %get-tuple-element.87), channel_id=1, source_target_pairs={{0,2},{2,0},{4,6},{6,4},{8,10},{10,8},{12,14},{14,12},{16,18},{18,... | collective-permute-start | bytes 159752 | tf_op jit(solution)/shard_map/ppermute | solution.py:487
  15.1 6.0 %collective-permute-start.5 = (f32[104,128]{1,0:T(8,128)S(1)}, f32[104,128]{1,0:T(8,128)S(1)}, u32[]{:S(2)}, u32[]{:S(2)}) collective-permute-start(f32[104,128]{1,0:T(8,128)S(1)} %get-tuple-element.88), channel_id=1, source_target_pairs={{2,4},{4,2},{6,8},{8,6},{10,12},{12,10},{14,16},{16,14},{18,20},{2... | collective-permute-start | bytes 159752 | tf_op jit(solution)/shard_map/ppermute | solution.py:487
  22.0 2.9 %collective-permute-start.6 = (f32[68,128]{1,0:T(8,128)S(1)}, f32[68,128]{1,0:T(8,128)S(1)}, u32[]{:S(2)}, u32[]{:S(2)}) collective-permute-start(f32[68,128]{1,0:T(8,128)S(1)} %get-tuple-element.102), channel_id=1, source_target_pairs={{0,1},{1,0},{2,3},{3,2},{4,5},{5,4},{6,7},{7,6},{8,9},{9,8},{10,11... | collective-permute-start | bytes 104456 | tf_op jit(solution)/shard_map/ppermute | solution.py:487
  24.9 3.6 %collective-permute-start.7 = (f32[88,128]{1,0:T(8,128)S(1)}, f32[88,128]{1,0:T(8,128)S(1)}, u32[]{:S(2)}, u32[]{:S(2)}) collective-permute-start(f32[88,128]{1,0:T(8,128)S(1)} %get-tuple-element.103), channel_id=1, source_target_pairs={{0,2},{2,0},{4,6},{6,4},{8,10},{10,8},{12,14},{14,12},{16,18},{18,... | collective-permute-start | bytes 135176 | tf_op jit(solution)/shard_map/ppermute | solution.py:487
  26.6 5.9 %collective-permute-start.8 = (f32[88,128]{1,0:T(8,128)S(1)}, f32[88,128]{1,0:T(8,128)S(1)}, u32[]{:S(2)}, u32[]{:S(2)}) collective-permute-start(f32[88,128]{1,0:T(8,128)S(1)} %get-tuple-element.104), channel_id=1, source_target_pairs={{2,4},{4,2},{6,8},{8,6},{10,12},{12,10},{14,16},{16,14},{18,20},{2... | collective-permute-start | bytes 135176 | tf_op jit(solution)/shard_map/ppermute | solution.py:487
  32.8 2.6 %collective-permute-start.9 = (f32[20,128]{1,0:T(8,128)S(1)}, f32[20,128]{1,0:T(8,128)S(1)}, u32[]{:S(2)}, u32[]{:S(2)}) collective-permute-start(f32[20,128]{1,0:T(8,128)S(1)} %get-tuple-element.111), channel_id=1, source_target_pairs={{0,1},{1,0},{2,3},{3,2},{4,5},{5,4},{6,7},{7,6},{8,9},{9,8},{10,11... | collective-permute-start | bytes 30728 | tf_op jit(solution)/shard_map/ppermute | solution.py:487
  35.4 3.6 %collective-permute-start.10 = (f32[40,128]{1,0:T(8,128)S(1)}, f32[40,128]{1,0:T(8,128)S(1)}, u32[]{:S(2)}, u32[]{:S(2)}) collective-permute-start(f32[40,128]{1,0:T(8,128)S(1)} %get-tuple-element.112), channel_id=1, source_target_pairs={{0,2},{2,0},{4,6},{6,4},{8,10},{10,8},{12,14},{14,12},{16,18},{18,... | collective-permute-start | bytes 61448 | tf_op jit(solution)/shard_map/ppermute | solution.py:487
  37.0 5.4 %collective-permute-start.11 = (f32[40,128]{1,0:T(8,128)S(1)}, f32[40,128]{1,0:T(8,128)S(1)}, u32[]{:S(2)}, u32[]{:S(2)}) collective-permute-start(f32[40,128]{1,0:T(8,128)S(1)} %get-tuple-element.113), channel_id=1, source_target_pairs={{2,4},{4,2},{6,8},{8,6},{10,12},{12,10},{14,16},{16,14},{18,20},{2... | collective-permute-start | bytes 61448 | tf_op jit(solution)/shard_map/ppermute | solution.py:487

commit v4 on v3

--- a/solution.py
+++ b/solution.py
@@ -4,6 +4,7 @@
 from jax.experimental import pallas as pl
 from jax.experimental.pallas import tpu as pltpu
 from jax.sharding import PartitionSpec as P
+
 
 R = 4
 NEWTON = 3
@@ -31,10 +32,6 @@
         if pairs:
             out.append(pairs)
     return out
-
-
-def both(pairs_x, pairs_y, count_y):
-    return [(i * count_y + j, k * count_y + m) for i, k in pairs_x for j, m in pairs_y]
 
 
 def lookup(labels, table):
@@ -450,26 +447,32 @@
             out[1, rows, :] = n
             out[2, rows, :] = p
 
-    def join_kernel(fresh, has_faces):
+    def join_kernel(k, fresh, has_faces):
         def kernel(after, cond, tile, *rest):
-            rest = list(rest)
-            take = lambda c: [rest.pop(0) for _ in range(c)]
-            faces = take(ux if has_faces else 0)
-            got_y, sends = take(uy), take(ux)
+            faces, got_y, s = rest[:-1][: -uy or None], rest[-1 - uy : -1], rest[-1]
             odd_x, _, _ = place_of()
             at = base = 0
             if has_faces:
                 at, base = 3 * ny, 3 * nx
-                for k, s in enumerate(sends):
-                    s[0:at, :] = faces[k][...]
+                s[0:at, :] = faces[0][...]
             parts = [(tile, 0), (tile, cells), (cond, 0)]
-            at = put_cells_x(odd_x, fresh, parts, sends, at)
+            at = put_cells_x(odd_x == (k == 0), fresh, parts, [s], at)
             more = wide[fresh] * cx
-            for k, s in enumerate(sends):
-                for b in range(uy):
-                    s[at + b * more : at + (b + 1) * more, :] = got_y[b][base : base + more, :]
+            for b in range(uy):
+                s[at + b * more : at + (b + 1) * more, :] = got_y[b][base : base + more, :]
 
         return kernel
+
+    def join(after, cond, tile, faces, got_y, fresh):
+        sends = []
+        rows = (3 * ny if faces else 0) + wide[fresh] * (cy + cx * uy)
+        for k in range(ux)[::-1]:
+            (after,) = call(
+                join_kernel(k, fresh, bool(faces)), [(rows, nz)], [],
+                [after, cond, tile] + faces[k : k + 1] + got_y, nodes,
+            )
+            sends.insert(0, after)
+        return sends
 
     def final_kernel(cext, *rest):
         got, (tile, out, ext, flat) = rest[: ux + uy], rest[ux + uy :]
@@ -486,13 +489,22 @@
     def along(axis, pairings, sends):
         return [lax.ppermute(s, axis, pairs) for s, pairs in zip(sends, pairings)]
 
+    def across(sends):
+        got = []
+        for k, pairs in enumerate(px):
+            got.append(lax.ppermute(sends[k], "gx", pairs))
+        return got
+
     def per_device(sol, ins, ele, zone, cat, warm):
         ele = ele.reshape(nodes, nz)
         coarse = nz // R
         work = nodes * nz
         V = pltpu.VMEM
-        eps = jnp.where(ins.reshape(1, nodes, nz) == 1, 0.4, 1.0).astype(F32)
-        state = eps = jnp.concatenate([sol.reshape(3, nodes, nz), eps], 0)
+        marks = lax.broadcast_in_dim(ins, (1, nx, ny, nz), (1, 2, 3))
+        marks = lax.pad(marks, jnp.int32(-1), [(3, 0, 0)] + [(0, 0, 0)] * 3)
+        sol = lax.pad(sol, F32(0), [(0, 1, 0)] + [(0, 0, 0)] * 3)
+        start = jnp.where(marks < 0, sol, jnp.where(marks == 1, 0.4, 1.0).astype(F32))
+        state = eps = start.reshape(4, nodes, nz)
         sends = call(
             pack_kernel, [(4 * ny, nz)] * ux + [(4 * nx, nz)] * uy, [], [state], work
         )
@@ -509,14 +521,8 @@
             accs = call(inner_kernel, [(nodes, nz)] * 9, [], [state, eps], 200 * work)
             got = []
             if not first:
-                joined = call(
-                    join_kernel(fresh, True),
-                    [(3 * ny + wide[fresh] * (cy + cx * uy), nz)] * ux,
-                    [],
-                    [accs[0], cond, tile] + faces + got_y,
-                    work,
-                )
-                got = along("gx", px, joined) + got_y
+                joined = join(accs[0], cond, tile, faces, got_y, fresh)
+                got = across(joined) + got_y
             args = [state, eps, ele, dop, cond] + accs + got0 + got + [tile]
             outs = []
             if not (first or fresh):
@@ -549,11 +555,8 @@
                     solve_kernel, [(3, nodes, nz), (8, nz)], [V((cells, nz), F32)],
                     [state, ele, dop, tile] + accs + res, 100 * work,
                 )
-        joined = call(
-            join_kernel(False, False), [(wide[False] * (cy + cx * uy), nz)] * ux, [],
-            [token, cond, tile] + got_y, work,
-        )
-        got = along("gx", px, joined) + got_y
+        joined = join(token, cond, tile, [], got_y, False)
+        got = across(joined) + got_y
         (warm,) = call(
             final_kernel,
             [(cells, coarse)],

time: 43.7 us -> 42.9 us (0.982)
  other arithmetic: 1.96 us -> 1.06 us
    ppermute x0 -> x6, starting transfers between devices: none -> 11.6 us  [across(): got.append(lax.ppermute(sends[k], 'gx', pairs))]
    ppermute x12 -> x6, starting transfers between devices: 20.3 us -> 8.8 us  [along(): return [lax.ppermute(s, axis, pairs) for s, pairs in zip(sends, pairings)]]
    ppermute x12 -> x6, waiting for transfers between devices: 11.7 us -> 0.9 us  [along(): return [lax.ppermute(s, axis, pairs) for s, pairs in zip(sends, pairings)]]
    ppermute x0 -> x6, waiting for transfers between devices: none -> 10.8 us  [across(): got.append(lax.ppermute(sends[k], 'gx', pairs))]
    concatenate x1 -> x0, other arithmetic: 1.04 us -> none  [per_device(): state = eps = jnp.concatenate([sol.reshape(3, nodes, nz), eps], 0)]
    pallas_call x13 -> x16, Pallas kernels: 8.63 us -> 8.68 us  [call(): pl.pallas_call(kernel, out_shape=[jax.ShapeDtypeStruct(s, F32) for s in o...]
where the time goes in v4:
time: 42.9 us; the launch traced here: 42.7 us
  starting transfers between devices  20.4 us (48%)
  waiting for transfers between devices  11.7 us (27%)
  Pallas kernels  8.68 us (20%)
  other arithmetic  1.06 us (2%)
  between operations  0.8 us (2%)
    ppermute x6, starting transfers between devices, across(): got.append(lax.ppermute(sends[k], 'gx', pairs))  11.6 us
    ppermute x6, waiting for transfers between devices, across(): got.append(lax.ppermute(sends[k], 'gx', pairs))  10.8 us
    ppermute x6, starting transfers between devices, along(): return [lax.ppermute(s, axis, pairs) for s, pairs in zip(sends, pairings)]  8.8 us
    pallas_call x16, Pallas kernels, call(): pl.pallas_call(kernel, out_shape=[jax.ShapeDtypeStruct(s, F32) for s in o...  8.68 us
    select_n x1, other arithmetic, per_device(): jnp.where(marks < 0, sol, jnp.where(marks == 1, 0.4, 1.0).astype(F32))  1.06 us
    ppermute x6, waiting for transfers between devices, along(): return [lax.ppermute(s, axis, pairs) for s, pairs in zip(sends, pairings)]  0.9 us
  transfers between devices with their start and end apart: 12, of which 6 were waited for; matrix products, arithmetic and copies ran while one was open for 0% of the time, Pallas kernels for 13%

profile of v4, /device:TPU:9, one launch (start us, length us, event | category | flops | bytes accessed | tf_op | source)
XLA Modules:
  0.0 42.7 jit_solution(13160291956022285051)
XLA Ops:
  0.6 1.1 %select_select_fusion = f32[4,16,16,128]{3,2,1,0:T(8,128)S(1)} fusion(f32[3,16,16,128]{3,2,1,0:T(8,128)} %param.6, s32[1,16,16,128]{3,2,1,0:T(8,128)} %bitcast.24), kind=kLoop, calls=%fused_computation.2 | loop fusion | flops 524288 | bytes 1048576 | tf_op jit(solution)/shard_map/jit(_where)/select_n | solution.py:506
  1.7 0.0 copy-start.2
  1.7 0.0 copy-start.3
  1.8 0.0 copy-start.1
  1.8 3.7 %collective-permute-start.1 = (f32[64,128]{1,0:T(8,128)S(1)}, f32[64,128]{1,0:T(8,128)S(1)}, u32[]{:S(2)}, u32[]{:S(2)}) collective-permute-start(f32[64,128]{1,0:T(8,128)S(1)} %get-tuple-element.64), channel_id=1, source_target_pairs={{2,4},{4,2},{6,8},{8,6},{10,12},{12,10},{14,16},{16,14},{18,20},{2... | collective-permute-start | bytes 98312 | tf_op jit(solution)/shard_map/ppermute | solution.py:490
  5.5 1.3 %collective-permute-start.2 = (f32[64,128]{1,0:T(8,128)S(1)}, f32[64,128]{1,0:T(8,128)S(1)}, u32[]{:S(2)}, u32[]{:S(2)}) collective-permute-start(f32[64,128]{1,0:T(8,128)S(1)} %get-tuple-element.65), channel_id=1, source_target_pairs={{0,1},{1,0},{2,3},{3,2},{4,5},{5,4},{6,7},{7,6},{8,9},{9,8},{10,11... | collective-permute-start | bytes 98312 | tf_op jit(solution)/shard_map/ppermute | solution.py:490
  6.8 0.0 collective-permute-start
  6.8 0.2 shard_map.78
  6.9 1.4 %shard_map.79 = (f32[256,128]{1,0:T(8,128)S(1)}, f32[256,128]{1,0:T(8,128)S(1)}, f32[256,128]{1,0:T(8,128)S(1)}, f32[256,128]{1,0:T(8,128)S(1)}, f32[256,128]{1,...) custom-call(f32[4,256,128]{2,1,0:T(8,128)S(1)} %bitcast.9, ...), custom_call_target="tpu_custom_call" | custom-call | flops 6553600 | tf_op jit(solution)/shard_map/pallas_call | solution.py:148
  8.4 0.4 collective-permute-done.2.rest_11_
  8.8 0.7 %shard_map.80 = (f32[3,256,128]{2,1,0:T(8,128)S(1)}, f32[48,128]{1,0:T(8,128)S(1)}, f32[48,128]{1,0:T(8,128)S(1)}, f32[76,128]{1,0:T(8,128)S(1)}, f32[32,128]{1,0:T(8,128)S(1)}) custom-call(f32[4,256,128]{2,1,0:T(8,128)S(1)} %bitcast.11, f32[4,256,128]{2,1,0:T(8,128)S(1)} %bitcast.12, s32[256,128]{1,0:T(8,128)S(1)} %bitcast.17, ...), custom_call_target="tpu_custom_call" | custom-call | flops 3276800 | tf_op jit(solution)/shard_map/pallas_call | solution.py:148
  9.5 1.3 %collective-permute-start.3 = (f32[76,128]{1,0:T(8,128)S(1)}, f32[76,128]{1,0:T(8,128)S(1)}, u32[]{:S(2)}, u32[]{:S(2)}) collective-permute-start(f32[76,128]{1,0:T(8,128)S(1)} %get-tuple-element.79), channel_id=1, source_target_pairs={{0,1},{1,0},{2,3},{3,2},{4,5},{5,4},{6,7},{7,6},{8,9},{9,8},{10,11... | collective-permute-start | bytes 116744 | tf_op jit(solution)/shard_map/ppermute | solution.py:490
  10.8 1.4 %shard_map.81 = (f32[256,128]{1,0:T(8,128)S(1)}, f32[256,128]{1,0:T(8,128)S(1)}, f32[256,128]{1,0:T(8,128)S(1)}, f32[256,128]{1,0:T(8,128)S(1)}, f32[256,128]{1,...) custom-call(f32[3,256,128]{2,1,0:T(8,128)S(1)} %get-tuple-element.67, ...), custom_call_target="tpu_custom_call" | custom-call | flops 6553600 | tf_op jit(solution)/shard_map/pallas_call | solution.py:148
  12.2 0.2 collective-permute-done.3.rest_1_.rest_14_
  12.5 1.8 %collective-permute-start.4 = (f32[104,128]{1,0:T(8,128)S(1)}, f32[104,128]{1,0:T(8,128)S(1)}, u32[]{:S(2)}, u32[]{:S(2)}) collective-permute-start(f32[104,128]{1,0:T(8,128)S(1)} %shard_map.83), channel_id=1, source_target_pairs={{0,2},{2,0},{4,6},{6,4},{8,10},{10,8},{12,14},{14,12},{16,18},{18,... | collective-permute-start | bytes 159752 | tf_op jit(solution)/shard_map/ppermute | solution.py:495
  14.3 2.6 %collective-permute-start.5 = (f32[104,128]{1,0:T(8,128)S(1)}, f32[104,128]{1,0:T(8,128)S(1)}, u32[]{:S(2)}, u32[]{:S(2)}) collective-permute-start(f32[104,128]{1,0:T(8,128)S(1)} %shard_map.82.after), channel_id=1, source_target_pairs={{2,4},{4,2},{6,8},{8,6},{10,12},{12,10},{14,16},{16,14},{18,20},{2... | collective-permute-start | bytes 159752 | tf_op jit(solution)/shard_map/ppermute | solution.py:495
  16.9 3.4 %collective-permute-done.5.rest_13_ = f32[104,128]{1,0:T(8,128)S(1)} collective-permute-done((f32[104,128]{1,0:T(8,128)S(1)}, f32[104,128]{1,0:T(8,128)S(1)}, u32[]{:S(2)}, u32[]{:S(2)}) %collective-permute-start.5) | collective-permute-done | bytes 53280 | tf_op jit(solution)/shard_map/ppermute | solution.py:495
  20.3 0.9 %shard_map.84 = (f32[3,256,128]{2,1,0:T(8,128)S(1)}, f32[48,128]{1,0:T(8,128)S(1)}, f32[48,128]{1,0:T(8,128)S(1)}, f32[68,128]{1,0:T(8,128)S(1)}, f32[32,128]{1,0:T(8,128)S(1)}, /*index=5*/f32[10,16,128]{2,1,0:T(8,128)S(1)}) custom-call(f32[3,256,128]{2,1,0:T(8,128)S(1)} %get-tuple-element.67.state, f32[4,256,128]{2,1,0:T(8,128)S(1)} %bitcast.14, ...), custom_call_target="tpu_custom_call" | custom-call | flops 3276800 | tf_op jit(solution)/shard_map/pallas_call | solution.py:148
  21.1 1.3 %collective-permute-start.6 = (f32[68,128]{1,0:T(8,128)S(1)}, f32[68,128]{1,0:T(8,128)S(1)}, u32[]{:S(2)}, u32[]{:S(2)}) collective-permute-start(f32[68,128]{1,0:T(8,128)S(1)} %get-tuple-element.93), channel_id=1, source_target_pairs={{0,1},{1,0},{2,3},{3,2},{4,5},{5,4},{6,7},{7,6},{8,9},{9,8},{10,11... | collective-permute-start | bytes 104456 | tf_op jit(solution)/shard_map/ppermute | solution.py:490
  22.4 1.4 %shard_map.85 = (f32[256,128]{1,0:T(8,128)S(1)}, f32[256,128]{1,0:T(8,128)S(1)}, f32[256,128]{1,0:T(8,128)S(1)}, f32[256,128]{1,0:T(8,128)S(1)}, f32[256,128]{1,...) custom-call(f32[3,256,128]{2,1,0:T(8,128)S(1)} %get-tuple-element.81, ...), custom_call_target="tpu_custom_call" | custom-call | flops 6553600 | tf_op jit(solution)/shard_map/pallas_call | solution.py:148
  23.8 0.2 collective-permute-done.6.rest_1_.rest_14_
  24.1 1.7 %collective-permute-start.7 = (f32[88,128]{1,0:T(8,128)S(1)}, f32[88,128]{1,0:T(8,128)S(1)}, u32[]{:S(2)}, u32[]{:S(2)}) collective-permute-start(f32[88,128]{1,0:T(8,128)S(1)} %shard_map.87), channel_id=1, source_target_pairs={{0,2},{2,0},{4,6},{6,4},{8,10},{10,8},{12,14},{14,12},{16,18},{18,... | collective-permute-start | bytes 135176 | tf_op jit(solution)/shard_map/ppermute | solution.py:495
  25.7 1.9 %collective-permute-start.8 = (f32[88,128]{1,0:T(8,128)S(1)}, f32[88,128]{1,0:T(8,128)S(1)}, u32[]{:S(2)}, u32[]{:S(2)}) collective-permute-start(f32[88,128]{1,0:T(8,128)S(1)} %shard_map.86.after), channel_id=1, source_target_pairs={{2,4},{4,2},{6,8},{8,6},{10,12},{12,10},{14,16},{16,14},{18,20},{2... | collective-permute-start | bytes 135176 | tf_op jit(solution)/shard_map/ppermute | solution.py:495
  27.6 4.0 %collective-permute-done.8.rest_13_ = f32[88,128]{1,0:T(8,128)S(1)} collective-permute-done((f32[88,128]{1,0:T(8,128)S(1)}, f32[88,128]{1,0:T(8,128)S(1)}, u32[]{:S(2)}, u32[]{:S(2)}) %collective-permute-start.8) | collective-permute-done | bytes 45088 | tf_op jit(solution)/shard_map/ppermute | solution.py:495
  31.6 0.3 shard_map.88
  31.9 1.3 %collective-permute-start.9 = (f32[20,128]{1,0:T(8,128)S(1)}, f32[20,128]{1,0:T(8,128)S(1)}, u32[]{:S(2)}, u32[]{:S(2)}) collective-permute-start(f32[20,128]{1,0:T(8,128)S(1)} %get-tuple-element.101), channel_id=1, source_target_pairs={{0,1},{1,0},{2,3},{3,2},{4,5},{5,4},{6,7},{7,6},{8,9},{9,8},{10,11... | collective-permute-start | bytes 30728 | tf_op jit(solution)/shard_map/ppermute | solution.py:490
  33.2 1.3 %shard_map.89 = (f32[3,256,128]{2,1,0:T(8,128)}, f32[8,128]{1,0:T(8,128)S(1)}) custom-call(f32[3,256,128]{2,1,0:T(8,128)S(1)} %get-tuple-element.81.state, s32[256,128]{1,0:T(8,128)S(1)} %bitcast.20, f32[16,128]{1,0:T(8,128)S(1)} %get-tuple-element.53.dop, f32[32,128]{1,0:T(8,128)S(1)} %get-tuple-element.96.tile.rest_3_, ...), custom_call_target="tpu_custom_call" | custom-call | flops 3276800 | tf_op jit(solution)/shard_map/pallas_call | solution.py:148
  34.5 0.0 collective-permute-done.9.rest_0_.rest_2_
  34.6 1.7 %collective-permute-start.10 = (f32[40,128]{1,0:T(8,128)S(1)}, f32[40,128]{1,0:T(8,128)S(1)}, u32[]{:S(2)}, u32[]{:S(2)}) collective-permute-start(f32[40,128]{1,0:T(8,128)S(1)} %shard_map.91), channel_id=1, source_target_pairs={{0,2},{2,0},{4,6},{6,4},{8,10},{10,8},{12,14},{14,12},{16,18},{18,... | collective-permute-start | bytes 61448 | tf_op jit(solution)/shard_map/ppermute | solution.py:495
  36.3 1.9 %collective-permute-start.11 = (f32[40,128]{1,0:T(8,128)S(1)}, f32[40,128]{1,0:T(8,128)S(1)}, u32[]{:S(2)}, u32[]{:S(2)}) collective-permute-start(f32[40,128]{1,0:T(8,128)S(1)} %shard_map.90.after), channel_id=1, source_target_pairs={{2,4},{4,2},{6,8},{8,6},{10,12},{12,10},{14,16},{16,14},{18,20},{2... | collective-permute-start | bytes 61448 | tf_op jit(solution)/shard_map/ppermute | solution.py:495
  38.2 3.5 %collective-permute-done.11.rest_1_ = f32[40,128]{1,0:T(8,128)S(1)} collective-permute-done((f32[40,128]{1,0:T(8,128)S(1)}, f32[40,128]{1,0:T(8,128)S(1)}, u32[]{:S(2)}, u32[]{:S(2)}) %collective-permute-start.11) | collective-permute-done | bytes 20512 | tf_op jit(solution)/shard_map/ppermute | solution.py:495
  41.6 1.0 %shard_map.92 = f32[16,32]{1,0:T(8,128)} custom-call(f32[10,16,128]{2,1,0:T(8,128)S(1)} %get-tuple-element.95.rest_16_.cext, f32[40,128]{1,0:T(8,128)S(1)} %collective-permute-done.10.rest_0_, f32[40,128]{1,0:T(8,128)S(1)} %collective-permute-done.11.rest_1_, f32[20,128]{1,0:T(8,128)S(1)} %collective-permute-done.9.rest_0_.rest_2_, ...), custom_call_target="tpu_custom_call" | custom-call | flops 32768 | tf_op jit(solution)/shard_map/pallas_call | solution.py:148
  (17 shorter events, 0.1 us)
Async XLA Ops:
  1.7 5.1 %copy-start.2 = (s32[4,4,32]{2,1,0:T(4,128)S(1)}, s32[4,4,32]{2,1,0:T(4,128)}, u32[]{:S(2)}) copy-start(s32[4,4,32]{2,1,0:T(4,128)} %param.10) | copy-start | bytes 6148
  1.7 5.1 %copy-start.3 = (f32[4,4,32]{2,1,0:T(4,128)S(1)}, f32[4,4,32]{2,1,0:T(4,128)}, u32[]{:S(2)}) copy-start(f32[4,4,32]{2,1,0:T(4,128)} %param.11) | copy-start | bytes 6148
  1.8 5.0 %copy-start.1 = (s32[4,4,32]{2,1,0:T(4,128)S(1)}, s32[4,4,32]{2,1,0:T(4,128)}, u32[]{:S(2)}) copy-start(s32[4,4,32]{2,1,0:T(4,128)} %param.9) | copy-start | bytes 6148
  1.8 6.6 %collective-permute-start.1 = (f32[64,128]{1,0:T(8,128)S(1)}, f32[64,128]{1,0:T(8,128)S(1)}, u32[]{:S(2)}, u32[]{:S(2)}) collective-permute-start(f32[64,128]{1,0:T(8,128)S(1)} %get-tuple-element.64), channel_id=1, source_target_pairs={{2,4},{4,2},{6,8},{8,6},{10,12},{12,10},{14,16},{16,14},{18,20},{2... | collective-permute-start | bytes 98312 | tf_op jit(solution)/shard_map/ppermute | solution.py:490
  5.5 3.3 %collective-permute-start.2 = (f32[64,128]{1,0:T(8,128)S(1)}, f32[64,128]{1,0:T(8,128)S(1)}, u32[]{:S(2)}, u32[]{:S(2)}) collective-permute-start(f32[64,128]{1,0:T(8,128)S(1)} %get-tuple-element.65), channel_id=1, source_target_pairs={{0,1},{1,0},{2,3},{3,2},{4,5},{5,4},{6,7},{7,6},{8,9},{9,8},{10,11... | collective-permute-start | bytes 98312 | tf_op jit(solution)/shard_map/ppermute | solution.py:490
  6.8 2.0 %collective-permute-start = (f32[64,128]{1,0:T(8,128)S(1)}, f32[64,128]{1,0:T(8,128)S(1)}, u32[]{:S(2)}, u32[]{:S(2)}) collective-permute-start(f32[64,128]{1,0:T(8,128)S(1)} %get-tuple-element.52.after), channel_id=1, source_target_pairs={{0,2},{2,0},{4,6},{6,4},{8,10},{10,8},{12,14},{14,12},{16,18},{18,... | collective-permute-start | bytes 98312 | tf_op jit(solution)/shard_map/ppermute | solution.py:490
  6.9 1.8 %copy-start = (s32[16,16,128]{2,1,0:T(8,128)S(1)}, s32[16,16,128]{2,1,0:T(8,128)}, u32[]{:S(2)}) copy-start(s32[16,16,128]{2,1,0:T(8,128)} %param.8) | copy-start | bytes 393220
  9.5 2.9 %collective-permute-start.3 = (f32[76,128]{1,0:T(8,128)S(1)}, f32[76,128]{1,0:T(8,128)S(1)}, u32[]{:S(2)}, u32[]{:S(2)}) collective-permute-start(f32[76,128]{1,0:T(8,128)S(1)} %get-tuple-element.79), channel_id=1, source_target_pairs={{0,1},{1,0},{2,3},{3,2},{4,5},{5,4},{6,7},{7,6},{8,9},{9,8},{10,11... | collective-permute-start | bytes 116744 | tf_op jit(solution)/shard_map/ppermute | solution.py:490
  12.5 4.4 %collective-permute-start.4 = (f32[104,128]{1,0:T(8,128)S(1)}, f32[104,128]{1,0:T(8,128)S(1)}, u32[]{:S(2)}, u32[]{:S(2)}) collective-permute-start(f32[104,128]{1,0:T(8,128)S(1)} %shard_map.83), channel_id=1, source_target_pairs={{0,2},{2,0},{4,6},{6,4},{8,10},{10,8},{12,14},{14,12},{16,18},{18,... | collective-permute-start | bytes 159752 | tf_op jit(solution)/shard_map/ppermute | solution.py:495
  14.3 6.0 %collective-permute-start.5 = (f32[104,128]{1,0:T(8,128)S(1)}, f32[104,128]{1,0:T(8,128)S(1)}, u32[]{:S(2)}, u32[]{:S(2)}) collective-permute-start(f32[104,128]{1,0:T(8,128)S(1)} %shard_map.82.after), channel_id=1, source_target_pairs={{2,4},{4,2},{6,8},{8,6},{10,12},{12,10},{14,16},{16,14},{18,20},{2... | collective-permute-start | bytes 159752 | tf_op jit(solution)/shard_map/ppermute | solution.py:495
  21.1 2.9 %collective-permute-start.6 = (f32[68,128]{1,0:T(8,128)S(1)}, f32[68,128]{1,0:T(8,128)S(1)}, u32[]{:S(2)}, u32[]{:S(2)}) collective-permute-start(f32[68,128]{1,0:T(8,128)S(1)} %get-tuple-element.93), channel_id=1, source_target_pairs={{0,1},{1,0},{2,3},{3,2},{4,5},{5,4},{6,7},{7,6},{8,9},{9,8},{10,11... | collective-permute-start | bytes 104456 | tf_op jit(solution)/shard_map/ppermute | solution.py:490
  24.1 3.6 %collective-permute-start.7 = (f32[88,128]{1,0:T(8,128)S(1)}, f32[88,128]{1,0:T(8,128)S(1)}, u32[]{:S(2)}, u32[]{:S(2)}) collective-permute-start(f32[88,128]{1,0:T(8,128)S(1)} %shard_map.87), channel_id=1, source_target_pairs={{0,2},{2,0},{4,6},{6,4},{8,10},{10,8},{12,14},{14,12},{16,18},{18,... | collective-permute-start | bytes 135176 | tf_op jit(solution)/shard_map/ppermute | solution.py:495
  25.7 5.9 %collective-permute-start.8 = (f32[88,128]{1,0:T(8,128)S(1)}, f32[88,128]{1,0:T(8,128)S(1)}, u32[]{:S(2)}, u32[]{:S(2)}) collective-permute-start(f32[88,128]{1,0:T(8,128)S(1)} %shard_map.86.after), channel_id=1, source_target_pairs={{2,4},{4,2},{6,8},{8,6},{10,12},{12,10},{14,16},{16,14},{18,20},{2... | collective-permute-start | bytes 135176 | tf_op jit(solution)/shard_map/ppermute | solution.py:495
  31.9 2.6 %collective-permute-start.9 = (f32[20,128]{1,0:T(8,128)S(1)}, f32[20,128]{1,0:T(8,128)S(1)}, u32[]{:S(2)}, u32[]{:S(2)}) collective-permute-start(f32[20,128]{1,0:T(8,128)S(1)} %get-tuple-element.101), channel_id=1, source_target_pairs={{0,1},{1,0},{2,3},{3,2},{4,5},{5,4},{6,7},{7,6},{8,9},{9,8},{10,11... | collective-permute-start | bytes 30728 | tf_op jit(solution)/shard_map/ppermute | solution.py:490
  34.6 3.6 %collective-permute-start.10 = (f32[40,128]{1,0:T(8,128)S(1)}, f32[40,128]{1,0:T(8,128)S(1)}, u32[]{:S(2)}, u32[]{:S(2)}) collective-permute-start(f32[40,128]{1,0:T(8,128)S(1)} %shard_map.91), channel_id=1, source_target_pairs={{0,2},{2,0},{4,6},{6,4},{8,10},{10,8},{12,14},{14,12},{16,18},{18,... | collective-permute-start | bytes 61448 | tf_op jit(solution)/shard_map/ppermute | solution.py:495
  36.3 5.4 %collective-permute-start.11 = (f32[40,128]{1,0:T(8,128)S(1)}, f32[40,128]{1,0:T(8,128)S(1)}, u32[]{:S(2)}, u32[]{:S(2)}) collective-permute-start(f32[40,128]{1,0:T(8,128)S(1)} %shard_map.90.after), channel_id=1, source_target_pairs={{2,4},{4,2},{6,8},{8,6},{10,12},{12,10},{14,16},{16,14},{18,20},{2... | collective-permute-start | bytes 61448 | tf_op jit(solution)/shard_map/ppermute | solution.py:495

commit v5 on v4

--- a/solution.py
+++ b/solution.py
@@ -83,16 +83,18 @@
     ]
 
 
-def solve(here, acc, contact, dop, mob):
-    psi, n, p, _ = here
-    lap, es, fe, fh, gn, gp, fwd, bwd, h = acc
+def ahead(psi, n, p):
     total = n + p
     rden = 1.0 / (total + 2.0)
-    rec = (n * p - 1.0) * rden
     rn = (p + 1.0) * rden
-    rn = rn * rn
     rp = (n + 1.0) * rden
-    rp = rp * rp
+    return (n * p - 1.0) * rden, rn * rn, rp * rp, 1.0 / total, 1.0 / n, 1.0 / p
+
+
+def solve(here, acc, pre, contact, dop, mob):
+    psi, n, p = here
+    lap, es, fe, fh, gn, gp, fwd, bwd, h = acc
+    rec, rn, rp, over_total, over_n, over_p = pre
     r0 = POISSON * lap + CHARGE * (p - n + dop)
     r1 = mob * fe - rec
     r2 = mob * fh - rec
@@ -113,8 +115,8 @@
     s0 = jnp.where(contact, psi - BIAS * dop, s0)
     s1 = jnp.where(contact, n - 1.0, s1)
     s2 = jnp.where(contact, p - 1.0, s2)
-    heat = None if h is None else h / total
-    return psi - s0, n * jnp.exp(-s1 / n), p * jnp.exp(-s2 / p), heat
+    heat = None if h is None else h * over_total
+    return psi - s0, n * jnp.exp(-s1 * over_n), p * jnp.exp(-s2 * over_p), heat
 
 
 def iota(shape, axis):
@@ -142,6 +144,7 @@
     vmem = pl.BlockSpec(memory_space=pltpu.VMEM)
     deep = {True: (W - 1, W, W - 1), False: (W - 1, W)}
     wide = {f: sum(deep[f]) for f in deep}
+    corner = {f: sum((d - 1) ** 2 for d in deep[f]) for f in deep}
 
     def call(kernel, outs, scratch, args, cost):
         return list(
@@ -249,6 +252,8 @@
         here = plane(0)
         acc = None
         for x in range(nx):
+            for q, v in enumerate(ahead(*here[:3])):
+                accs[9 + q][x * ny : (x + 1) * ny, :] = v
             f = face(here, [pltpu.roll(v, nz - 1, 1) for v in here], wz)
             acc = list(f) if acc is None else add_here(acc, f)
             acc = add_there(acc, [pltpu.roll(v, 1, 1) for v in f])
@@ -292,23 +297,14 @@
                     grid[g + to + i, W : W + cy, :] = tile[i * cy : (i + 1) * cy]
                 near = depth - 1
                 for i in range(near):
-                    x = i if sx else cx - near + i
                     at = W + cx + i if sx else W - near + i
                     for sy in (0, 1):
-                        skip = 0 if sy else depth - near
                         along = [
                             pick(
                                 odd_y,
                                 sy,
                                 [
-                                    r[
-                                        pl.ds(
-                                            past + b * wide[fresh] * cx + gone + skip * cx + x,
-                                            near,
-                                            stride=cx,
-                                        ),
-                                        :,
-                                    ]
+                                    r[pl.ds(past + b * corner[fresh] + gone + i, near, stride=near), :]
                                     for b in range(uy)
                                 ],
                             )
@@ -318,7 +314,7 @@
                         grid[g + at, to_y : to_y + near, :] = pick(odd_x, sx, along)
             off_x += depth * cy
             off_y += depth * cx
-            gone += depth * cx
+            gone += near * near
         lane = iota((ey, nz), 1)
         has_low, has_high = lane >= R, lane < nz - R
         src = [ext[x] for x in range(ex)]
@@ -344,6 +340,7 @@
             rest = list(rest)
             take = lambda c: [rest.pop(0) for _ in range(c)]
             accs = take(9)
+            pre = take(6)
             got0 = take(ux + uy)
             got = got0 if first else take(ux + uy)
             (tile,) = take(1)
@@ -392,14 +389,14 @@
                 rows = slice(x * ny, (x + 1) * ny)
                 if split:
                     (h,) = whole(accs, rim_x, rim_y, x, [8])
-                    h = h / (state[1, rows, :] + state[2, rows, :])
+                    h = h * pre[3][rows, :]
                 else:
                     if x % R == 0:
                         mob = spread_rows(mobs, (x // R) * cy, cy)
                         dopx = spread_rows(dop, (x // R) * cy, cy)
-                    here = [state[0, rows, :], state[1, rows, :], state[2, rows, :], None]
+                    here = [state[f, rows, :] for f in range(3)]
                     acc = whole(accs, rim_x, rim_y, x, range(9))
-                    psi, n, p, h = solve(here, acc, ele[rows, :] == 1, dopx, mob)
+                    psi, n, p, h = solve(here, acc, [v[rows, :] for v in pre], ele[rows, :] == 1, dopx, mob)
                     out[0, rows, :] = psi
                     out[1, rows, :] = n
                     out[2, rows, :] = p
@@ -432,7 +429,7 @@
         return kernel
 
     def solve_kernel(state, ele, dop, tile, *rest):
-        accs, (rim_x, rim_y, out, token, mobs) = rest[:9], rest[9:]
+        accs, pre, (rim_x, rim_y, out, token, mobs) = rest[:9], rest[9:15], rest[15:]
         token[...] = jnp.zeros_like(token)
         mobs[...] = 1.0 / (1.0 + DROP * tile[cells : 2 * cells, :])
         for x in range(nx):
@@ -440,9 +437,9 @@
             if x % R == 0:
                 mob = spread_rows(mobs, (x // R) * cy, cy)
                 dopx = spread_rows(dop, (x // R) * cy, cy)
-            here = [state[0, rows, :], state[1, rows, :], state[2, rows, :], None]
+            here = [state[f, rows, :] for f in range(3)]
             acc = whole(accs, rim_x, rim_y, x, range(8)) + [None]
-            psi, n, p, _ = solve(here, acc, ele[rows, :] == 1, dopx, mob)
+            psi, n, p, _ = solve(here, acc, [v[rows, :] for v in pre], ele[rows, :] == 1, dopx, mob)
             out[0, rows, :] = psi
             out[1, rows, :] = n
             out[2, rows, :] = p
@@ -450,22 +447,34 @@
     def join_kernel(k, fresh, has_faces):
         def kernel(after, cond, tile, *rest):
             faces, got_y, s = rest[:-1][: -uy or None], rest[-1 - uy : -1], rest[-1]
-            odd_x, _, _ = place_of()
+            odd_x, odd_y, _ = place_of()
+            to_low = odd_x == (k == 0)
             at = base = 0
             if has_faces:
                 at, base = 3 * ny, 3 * nx
                 s[0:at, :] = faces[0][...]
             parts = [(tile, 0), (tile, cells), (cond, 0)]
-            at = put_cells_x(odd_x == (k == 0), fresh, parts, [s], at)
-            more = wide[fresh] * cx
-            for b in range(uy):
-                s[at + b * more : at + (b + 1) * more, :] = got_y[b][base : base + more, :]
+            at = put_cells_x(to_low, fresh, parts, [s], at)
+            for b, g in enumerate(got_y):
+                from_high = odd_y == (b == 1)
+                off = base
+                for depth in deep[fresh]:
+                    near = depth - 1
+                    for i in range(near):
+                        ends = []
+                        for layer in (i, depth - near + i):
+                            row = off + layer * cx
+                            low, high = g[row : row + near, :], g[row + cx - near : row + cx, :]
+                            ends.append(jnp.where(to_low, low, high))
+                        s[at : at + near, :] = jnp.where(from_high, *ends)
+                        at += near
+                    off += depth * cx
 
         return kernel
 
     def join(after, cond, tile, faces, got_y, fresh):
         sends = []
-        rows = (3 * ny if faces else 0) + wide[fresh] * (cy + cx * uy)
+        rows = (3 * ny if faces else 0) + wide[fresh] * cy + corner[fresh] * uy
         for k in range(ux)[::-1]:
             (after,) = call(
                 join_kernel(k, fresh, bool(faces)), [(rows, nz)], [],
@@ -480,11 +489,8 @@
         rows = sweeps(False, own, got[:ux], got[ux:], (0, 0), ext, cext)
         for x in range(cx):
             flat[x * cy : (x + 1) * cy, :] = rows[x]
-        coarse = nz // R
-        sel = (iota((nz, coarse), 0) == R * iota((nz, coarse), 1)).astype(F32)
-        out[...] = jnp.dot(
-            flat[...], sel, precision=lax.Precision.HIGHEST, preferred_element_type=F32
-        )
+        first = jnp.minimum(R * iota((cells, nz), 1), nz - 1)
+        out[...] = jnp.take_along_axis(flat[...], first, axis=1)[:, : nz // R]
 
     def along(axis, pairings, sends):
         return [lax.ppermute(s, axis, pairs) for s, pairs in zip(sends, pairings)]
@@ -518,7 +524,7 @@
         got_y, faces, cext = [], [], []
         for k in range(NEWTON):
             first, fresh, last = k == 0, k == 1, k == NEWTON - 1
-            accs = call(inner_kernel, [(nodes, nz)] * 9, [], [state, eps], 200 * work)
+            accs = call(inner_kernel, [(nodes, nz)] * 15, [], [state, eps], 200 * work)
             got = []
             if not first:
                 joined = join(accs[0], cond, tile, faces, got_y, fresh)

time: 42.9 us -> 42.6 us (level)
  transfers between devices with their start and end apart: 12 -> 12, of which waited for: 6 -> 7; matrix products, arithmetic and copies ran while one was open for 0% -> 0% of each run, Pallas kernels for 13% -> 13%
where the time goes in v5:
time: 42.6 us; the launch traced here: 42.3 us
  starting transfers between devices  20.4 us (48%)
  waiting for transfers between devices  11.6 us (27%)
  Pallas kernels  8.45 us (20%)
  other arithmetic  1.06 us (2%)
  between operations  0.81 us (2%)
    ppermute x6, starting transfers between devices, across(): got.append(lax.ppermute(sends[k], 'gx', pairs))  11.6 us
    ppermute x6, waiting for transfers between devices, across(): got.append(lax.ppermute(sends[k], 'gx', pairs))  10.6 us
    ppermute x6, starting transfers between devices, along(): return [lax.ppermute(s, axis, pairs) for s, pairs in zip(sends, pairings)]  8.81 us
    pallas_call x16, Pallas kernels, call(): pl.pallas_call(kernel, out_shape=[jax.ShapeDtypeStruct(s, F32) for s in o...  8.45 us
    select_n x1, other arithmetic, per_device(): jnp.where(marks < 0, sol, jnp.where(marks == 1, 0.4, 1.0).astype(F32))  1.06 us
    ppermute x6, waiting for transfers between devices, along(): return [lax.ppermute(s, axis, pairs) for s, pairs in zip(sends, pairings)]  0.96 us
  transfers between devices with their start and end apart: 12, of which 7 were waited for; matrix products, arithmetic and copies ran while one was open for 0% of the time, Pallas kernels for 13%

profile of v5, /device:TPU:9, one launch (start us, length us, event | category | flops | bytes accessed | tf_op | source)
XLA Modules:
  0.0 42.3 jit_solution(2217472478697529727)
XLA Ops:
  0.6 1.1 %select_select_fusion = f32[4,16,16,128]{3,2,1,0:T(8,128)S(1)} fusion(f32[3,16,16,128]{3,2,1,0:T(8,128)} %param.6, s32[1,16,16,128]{3,2,1,0:T(8,128)} %bitcast.24), kind=kLoop, calls=%fused_computation.2 | loop fusion | flops 524288 | bytes 1048576 | tf_op jit(solution)/shard_map/jit(_where)/select_n | solution.py:512
  1.7 0.0 copy-start.2
  1.7 0.0 copy-start.3
  1.8 0.0 copy-start.1
  1.8 3.7 %collective-permute-start.1 = (f32[64,128]{1,0:T(8,128)S(1)}, f32[64,128]{1,0:T(8,128)S(1)}, u32[]{:S(2)}, u32[]{:S(2)}) collective-permute-start(f32[64,128]{1,0:T(8,128)S(1)} %get-tuple-element.88), channel_id=1, source_target_pairs={{2,4},{4,2},{6,8},{8,6},{10,12},{12,10},{14,16},{16,14},{18,20},{2... | collective-permute-start | bytes 98312 | tf_op jit(solution)/shard_map/ppermute | solution.py:496
  5.5 1.3 %collective-permute-start.2 = (f32[64,128]{1,0:T(8,128)S(1)}, f32[64,128]{1,0:T(8,128)S(1)}, u32[]{:S(2)}, u32[]{:S(2)}) collective-permute-start(f32[64,128]{1,0:T(8,128)S(1)} %get-tuple-element.89), channel_id=1, source_target_pairs={{0,1},{1,0},{2,3},{3,2},{4,5},{5,4},{6,7},{7,6},{8,9},{9,8},{10,11... | collective-permute-start | bytes 98312 | tf_op jit(solution)/shard_map/ppermute | solution.py:496
  6.8 0.2 shard_map.78
  6.9 1.4 %shard_map.79 = (f32[256,128]{1,0:T(8,128)S(1)}, f32[256,128]{1,0:T(8,128)S(1)}, f32[256,128]{1,0:T(8,128)S(1)}, f32[256,128]{1,0:T(8,128)S(1)}, f32[256,128]{1,...) custom-call(f32[4,256,128]{2,1,0:T(8,128)S(1)} %bitcast.9, ...), custom_call_target="tpu_custom_call" | custom-call | flops 6553600 | tf_op jit(solution)/shard_map/pallas_call | solution.py:151
  8.4 0.0 collective-permute-done.1.rest_16_
  8.4 0.4 collective-permute-done.2.rest_17_
  8.8 0.7 %shard_map.80 = (f32[3,256,128]{2,1,0:T(8,128)S(1)}, f32[48,128]{1,0:T(8,128)S(1)}, f32[48,128]{1,0:T(8,128)S(1)}, f32[76,128]{1,0:T(8,128)S(1)}, f32[32,128]{1,0:T(8,128)S(1)}) custom-call(f32[4,256,128]{2,1,0:T(8,128)S(1)} %bitcast.11, f32[4,256,128]{2,1,0:T(8,128)S(1)} %bitcast.12, s32[256,128]{1,0:T(8,128)S(1)} %bitcast.17, ...), custom_call_target="tpu_custom_call" | custom-call | flops 3276800 | tf_op jit(solution)/shard_map/pallas_call | solution.py:151
  9.5 1.3 %collective-permute-start.3 = (f32[76,128]{1,0:T(8,128)S(1)}, f32[76,128]{1,0:T(8,128)S(1)}, u32[]{:S(2)}, u32[]{:S(2)}) collective-permute-start(f32[76,128]{1,0:T(8,128)S(1)} %get-tuple-element.109), channel_id=1, source_target_pairs={{0,1},{1,0},{2,3},{3,2},{4,5},{5,4},{6,7},{7,6},{8,9},{9,8},{10,11... | collective-permute-start | bytes 116744 | tf_op jit(solution)/shard_map/ppermute | solution.py:496
  10.7 1.4 %shard_map.81 = (f32[256,128]{1,0:T(8,128)S(1)}, f32[256,128]{1,0:T(8,128)S(1)}, f32[256,128]{1,0:T(8,128)S(1)}, f32[256,128]{1,0:T(8,128)S(1)}, f32[256,128]{1,...) custom-call(f32[3,256,128]{2,1,0:T(8,128)S(1)} %get-tuple-element.91, ...), custom_call_target="tpu_custom_call" | custom-call | flops 6553600 | tf_op jit(solution)/shard_map/pallas_call | solution.py:151
  12.1 0.2 collective-permute-done.3.rest_1_.rest_20_
  12.4 1.8 %collective-permute-start.4 = (f32[82,128]{1,0:T(8,128)S(1)}, f32[82,128]{1,0:T(8,128)S(1)}, u32[]{:S(2)}, u32[]{:S(2)}) collective-permute-start(f32[82,128]{1,0:T(8,128)S(1)} %shard_map.83), channel_id=1, source_target_pairs={{0,2},{2,0},{4,6},{6,4},{8,10},{10,8},{12,14},{14,12},{16,18},{18,... | collective-permute-start | bytes 125960 | tf_op jit(solution)/shard_map/ppermute | solution.py:501
  14.2 2.6 %collective-permute-start.5 = (f32[82,128]{1,0:T(8,128)S(1)}, f32[82,128]{1,0:T(8,128)S(1)}, u32[]{:S(2)}, u32[]{:S(2)}) collective-permute-start(f32[82,128]{1,0:T(8,128)S(1)} %shard_map.82.after), channel_id=1, source_target_pairs={{2,4},{4,2},{6,8},{8,6},{10,12},{12,10},{14,16},{16,14},{18,20},{2... | collective-permute-start | bytes 125960 | tf_op jit(solution)/shard_map/ppermute | solution.py:501
  16.8 3.3 %collective-permute-done.5.rest_19_ = f32[82,128]{1,0:T(8,128)S(1)} collective-permute-done((f32[82,128]{1,0:T(8,128)S(1)}, f32[82,128]{1,0:T(8,128)S(1)}, u32[]{:S(2)}, u32[]{:S(2)}) %collective-permute-start.5) | collective-permute-done | bytes 42016 | tf_op jit(solution)/shard_map/ppermute | solution.py:501
  20.1 0.8 %shard_map.84 = (f32[3,256,128]{2,1,0:T(8,128)S(1)}, f32[48,128]{1,0:T(8,128)S(1)}, f32[48,128]{1,0:T(8,128)S(1)}, f32[68,128]{1,0:T(8,128)S(1)}, f32[32,128]{1,0:T(8,128)S(1)}, /*index=5*/f32[10,16,128]{2,1,0:T(8,128)S(1)}) custom-call(f32[3,256,128]{2,1,0:T(8,128)S(1)} %get-tuple-element.91.state, f32[4,256,128]{2,1,0:T(8,128)S(1)} %bitcast.14, ...), custom_call_target="tpu_custom_call" | custom-call | flops 3276800 | tf_op jit(solution)/shard_map/pallas_call | solution.py:151
  20.9 1.3 %collective-permute-start.6 = (f32[68,128]{1,0:T(8,128)S(1)}, f32[68,128]{1,0:T(8,128)S(1)}, u32[]{:S(2)}, u32[]{:S(2)}) collective-permute-start(f32[68,128]{1,0:T(8,128)S(1)} %get-tuple-element.129), channel_id=1, source_target_pairs={{0,1},{1,0},{2,3},{3,2},{4,5},{5,4},{6,7},{7,6},{8,9},{9,8},{10,11... | collective-permute-start | bytes 104456 | tf_op jit(solution)/shard_map/ppermute | solution.py:496
  22.2 1.4 %shard_map.85 = (f32[256,128]{1,0:T(8,128)S(1)}, f32[256,128]{1,0:T(8,128)S(1)}, f32[256,128]{1,0:T(8,128)S(1)}, f32[256,128]{1,0:T(8,128)S(1)}, f32[256,128]{1,...) custom-call(f32[3,256,128]{2,1,0:T(8,128)S(1)} %get-tuple-element.11, ...), custom_call_target="tpu_custom_call" | custom-call | flops 6553600 | tf_op jit(solution)/shard_map/pallas_call | solution.py:151
  23.6 0.2 collective-permute-done.6.rest_1_.rest_20_
  23.8 1.7 %collective-permute-start.7 = (f32[73,128]{1,0:T(8,128)S(1)}, f32[73,128]{1,0:T(8,128)S(1)}, u32[]{:S(2)}, u32[]{:S(2)}) collective-permute-start(f32[73,128]{1,0:T(8,128)S(1)} %shard_map.87), channel_id=1, source_target_pairs={{0,2},{2,0},{4,6},{6,4},{8,10},{10,8},{12,14},{14,12},{16,18},{18,... | collective-permute-start | bytes 112136 | tf_op jit(solution)/shard_map/ppermute | solution.py:501
  25.6 1.9 %collective-permute-start.8 = (f32[73,128]{1,0:T(8,128)S(1)}, f32[73,128]{1,0:T(8,128)S(1)}, u32[]{:S(2)}, u32[]{:S(2)}) collective-permute-start(f32[73,128]{1,0:T(8,128)S(1)} %shard_map.86.after), channel_id=1, source_target_pairs={{2,4},{4,2},{6,8},{8,6},{10,12},{12,10},{14,16},{16,14},{18,20},{2... | collective-permute-start | bytes 112136 | tf_op jit(solution)/shard_map/ppermute | solution.py:501
  27.5 3.9 %collective-permute-done.8.rest_19_ = f32[73,128]{1,0:T(8,128)S(1)} collective-permute-done((f32[73,128]{1,0:T(8,128)S(1)}, f32[73,128]{1,0:T(8,128)S(1)}, u32[]{:S(2)}, u32[]{:S(2)}) %collective-permute-start.8) | collective-permute-done | bytes 37408 | tf_op jit(solution)/shard_map/ppermute | solution.py:501
  31.4 0.3 shard_map.88
  31.7 1.3 %collective-permute-start.9 = (f32[20,128]{1,0:T(8,128)S(1)}, f32[20,128]{1,0:T(8,128)S(1)}, u32[]{:S(2)}, u32[]{:S(2)}) collective-permute-start(f32[20,128]{1,0:T(8,128)S(1)} %get-tuple-element.137), channel_id=1, source_target_pairs={{0,1},{1,0},{2,3},{3,2},{4,5},{5,4},{6,7},{7,6},{8,9},{9,8},{10,11... | collective-permute-start | bytes 30728 | tf_op jit(solution)/shard_map/ppermute | solution.py:496
  33.0 1.2 %shard_map.89 = (f32[3,256,128]{2,1,0:T(8,128)}, f32[8,128]{1,0:T(8,128)S(1)}) custom-call(f32[3,256,128]{2,1,0:T(8,128)S(1)} %get-tuple-element.111.state, s32[256,128]{1,0:T(8,128)S(1)} %bitcast.20, f32[16,128]{1,0:T(8,128)S(1)} %get-tuple-element.71.dop, f32[32,128]{1,0:T(8,128)S(1)} %get-tuple-element.132.tile.rest_3_, ...), custom_call_target="tpu_custom_call" | custom-call | flops 3276800 | tf_op jit(solution)/shard_map/pallas_call | solution.py:151
  34.2 0.1 collective-permute-done.9.rest_0_.rest_2_
  34.4 1.7 %collective-permute-start.10 = (f32[25,128]{1,0:T(8,128)S(1)}, f32[25,128]{1,0:T(8,128)S(1)}, u32[]{:S(2)}, u32[]{:S(2)}) collective-permute-start(f32[25,128]{1,0:T(8,128)S(1)} %shard_map.91), channel_id=1, source_target_pairs={{0,2},{2,0},{4,6},{6,4},{8,10},{10,8},{12,14},{14,12},{16,18},{18,... | collective-permute-start | bytes 38408 | tf_op jit(solution)/shard_map/ppermute | solution.py:501
  36.1 1.9 %collective-permute-start.11 = (f32[25,128]{1,0:T(8,128)S(1)}, f32[25,128]{1,0:T(8,128)S(1)}, u32[]{:S(2)}, u32[]{:S(2)}) collective-permute-start(f32[25,128]{1,0:T(8,128)S(1)} %shard_map.90.after), channel_id=1, source_target_pairs={{2,4},{4,2},{6,8},{8,6},{10,12},{12,10},{14,16},{16,14},{18,20},{2... | collective-permute-start | bytes 38408 | tf_op jit(solution)/shard_map/ppermute | solution.py:501
  38.0 3.4 %collective-permute-done.11.rest_1_ = f32[25,128]{1,0:T(8,128)S(1)} collective-permute-done((f32[25,128]{1,0:T(8,128)S(1)}, f32[25,128]{1,0:T(8,128)S(1)}, u32[]{:S(2)}, u32[]{:S(2)}) %collective-permute-start.11) | collective-permute-done | bytes 12832 | tf_op jit(solution)/shard_map/ppermute | solution.py:501
  41.4 0.9 %shard_map.92 = f32[16,32]{1,0:T(8,128)} custom-call(f32[10,16,128]{2,1,0:T(8,128)S(1)} %get-tuple-element.131.rest_22_.cext, f32[25,128]{1,0:T(8,128)S(1)} %collective-permute-done.10.rest_0_, f32[25,128]{1,0:T(8,128)S(1)} %collective-permute-done.11.rest_1_, f32[20,128]{1,0:T(8,128)S(1)} %collective-permute-done.9.rest_0_.rest_2_, ...), custom_call_target="tpu_custom_call" | custom-call | flops 32768 | tf_op jit(solution)/shard_map/pallas_call | solution.py:151
  (17 shorter events, 0.1 us)
Async XLA Ops:
  1.7 5.1 %copy-start.2 = (s32[4,4,32]{2,1,0:T(4,128)S(1)}, s32[4,4,32]{2,1,0:T(4,128)}, u32[]{:S(2)}) copy-start(s32[4,4,32]{2,1,0:T(4,128)} %param.10) | copy-start | bytes 6148
  1.7 5.1 %copy-start.3 = (f32[4,4,32]{2,1,0:T(4,128)S(1)}, f32[4,4,32]{2,1,0:T(4,128)}, u32[]{:S(2)}) copy-start(f32[4,4,32]{2,1,0:T(4,128)} %param.11) | copy-start | bytes 6148
  1.8 5.0 %copy-start.1 = (s32[4,4,32]{2,1,0:T(4,128)S(1)}, s32[4,4,32]{2,1,0:T(4,128)}, u32[]{:S(2)}) copy-start(s32[4,4,32]{2,1,0:T(4,128)} %param.9) | copy-start | bytes 6148
  1.8 6.6 %collective-permute-start.1 = (f32[64,128]{1,0:T(8,128)S(1)}, f32[64,128]{1,0:T(8,128)S(1)}, u32[]{:S(2)}, u32[]{:S(2)}) collective-permute-start(f32[64,128]{1,0:T(8,128)S(1)} %get-tuple-element.88), channel_id=1, source_target_pairs={{2,4},{4,2},{6,8},{8,6},{10,12},{12,10},{14,16},{16,14},{18,20},{2... | collective-permute-start | bytes 98312 | tf_op jit(solution)/shard_map/ppermute | solution.py:496
  5.5 3.3 %collective-permute-start.2 = (f32[64,128]{1,0:T(8,128)S(1)}, f32[64,128]{1,0:T(8,128)S(1)}, u32[]{:S(2)}, u32[]{:S(2)}) collective-permute-start(f32[64,128]{1,0:T(8,128)S(1)} %get-tuple-element.89), channel_id=1, source_target_pairs={{0,1},{1,0},{2,3},{3,2},{4,5},{5,4},{6,7},{7,6},{8,9},{9,8},{10,11... | collective-permute-start | bytes 98312 | tf_op jit(solution)/shard_map/ppermute | solution.py:496
  6.8 2.0 %collective-permute-start = (f32[64,128]{1,0:T(8,128)S(1)}, f32[64,128]{1,0:T(8,128)S(1)}, u32[]{:S(2)}, u32[]{:S(2)}) collective-permute-start(f32[64,128]{1,0:T(8,128)S(1)} %get-tuple-element.70.after), channel_id=1, source_target_pairs={{0,2},{2,0},{4,6},{6,4},{8,10},{10,8},{12,14},{14,12},{16,18},{18,... | collective-permute-start | bytes 98312 | tf_op jit(solution)/shard_map/ppermute | solution.py:496
  6.9 1.8 %copy-start = (s32[16,16,128]{2,1,0:T(8,128)S(1)}, s32[16,16,128]{2,1,0:T(8,128)}, u32[]{:S(2)}) copy-start(s32[16,16,128]{2,1,0:T(8,128)} %param.8) | copy-start | bytes 393220
  9.5 2.9 %collective-permute-start.3 = (f32[76,128]{1,0:T(8,128)S(1)}, f32[76,128]{1,0:T(8,128)S(1)}, u32[]{:S(2)}, u32[]{:S(2)}) collective-permute-start(f32[76,128]{1,0:T(8,128)S(1)} %get-tuple-element.109), channel_id=1, source_target_pairs={{0,1},{1,0},{2,3},{3,2},{4,5},{5,4},{6,7},{7,6},{8,9},{9,8},{10,11... | collective-permute-start | bytes 116744 | tf_op jit(solution)/shard_map/ppermute | solution.py:496
  12.4 4.4 %collective-permute-start.4 = (f32[82,128]{1,0:T(8,128)S(1)}, f32[82,128]{1,0:T(8,128)S(1)}, u32[]{:S(2)}, u32[]{:S(2)}) collective-permute-start(f32[82,128]{1,0:T(8,128)S(1)} %shard_map.83), channel_id=1, source_target_pairs={{0,2},{2,0},{4,6},{6,4},{8,10},{10,8},{12,14},{14,12},{16,18},{18,... | collective-permute-start | bytes 125960 | tf_op jit(solution)/shard_map/ppermute | solution.py:501
  14.2 5.9 %collective-permute-start.5 = (f32[82,128]{1,0:T(8,128)S(1)}, f32[82,128]{1,0:T(8,128)S(1)}, u32[]{:S(2)}, u32[]{:S(2)}) collective-permute-start(f32[82,128]{1,0:T(8,128)S(1)} %shard_map.82.after), channel_id=1, source_target_pairs={{2,4},{4,2},{6,8},{8,6},{10,12},{12,10},{14,16},{16,14},{18,20},{2... | collective-permute-start | bytes 125960 | tf_op jit(solution)/shard_map/ppermute | solution.py:501
  20.9 2.9 %collective-permute-start.6 = (f32[68,128]{1,0:T(8,128)S(1)}, f32[68,128]{1,0:T(8,128)S(1)}, u32[]{:S(2)}, u32[]{:S(2)}) collective-permute-start(f32[68,128]{1,0:T(8,128)S(1)} %get-tuple-element.129), channel_id=1, source_target_pairs={{0,1},{1,0},{2,3},{3,2},{4,5},{5,4},{6,7},{7,6},{8,9},{9,8},{10,11... | collective-permute-start | bytes 104456 | tf_op jit(solution)/shard_map/ppermute | solution.py:496
  23.8 3.6 %collective-permute-start.7 = (f32[73,128]{1,0:T(8,128)S(1)}, f32[73,128]{1,0:T(8,128)S(1)}, u32[]{:S(2)}, u32[]{:S(2)}) collective-permute-start(f32[73,128]{1,0:T(8,128)S(1)} %shard_map.87), channel_id=1, source_target_pairs={{0,2},{2,0},{4,6},{6,4},{8,10},{10,8},{12,14},{14,12},{16,18},{18,... | collective-permute-start | bytes 112136 | tf_op jit(solution)/shard_map/ppermute | solution.py:501
  25.6 5.8 %collective-permute-start.8 = (f32[73,128]{1,0:T(8,128)S(1)}, f32[73,128]{1,0:T(8,128)S(1)}, u32[]{:S(2)}, u32[]{:S(2)}) collective-permute-start(f32[73,128]{1,0:T(8,128)S(1)} %shard_map.86.after), channel_id=1, source_target_pairs={{2,4},{4,2},{6,8},{8,6},{10,12},{12,10},{14,16},{16,14},{18,20},{2... | collective-permute-start | bytes 112136 | tf_op jit(solution)/shard_map/ppermute | solution.py:501
  31.7 2.6 %collective-permute-start.9 = (f32[20,128]{1,0:T(8,128)S(1)}, f32[20,128]{1,0:T(8,128)S(1)}, u32[]{:S(2)}, u32[]{:S(2)}) collective-permute-start(f32[20,128]{1,0:T(8,128)S(1)} %get-tuple-element.137), channel_id=1, source_target_pairs={{0,1},{1,0},{2,3},{3,2},{4,5},{5,4},{6,7},{7,6},{8,9},{9,8},{10,11... | collective-permute-start | bytes 30728 | tf_op jit(solution)/shard_map/ppermute | solution.py:496
  34.4 3.6 %collective-permute-start.10 = (f32[25,128]{1,0:T(8,128)S(1)}, f32[25,128]{1,0:T(8,128)S(1)}, u32[]{:S(2)}, u32[]{:S(2)}) collective-permute-start(f32[25,128]{1,0:T(8,128)S(1)} %shard_map.91), channel_id=1, source_target_pairs={{0,2},{2,0},{4,6},{6,4},{8,10},{10,8},{12,14},{14,12},{16,18},{18,... | collective-permute-start | bytes 38408 | tf_op jit(solution)/shard_map/ppermute | solution.py:501
  36.1 5.3 %collective-permute-start.11 = (f32[25,128]{1,0:T(8,128)S(1)}, f32[25,128]{1,0:T(8,128)S(1)}, u32[]{:S(2)}, u32[]{:S(2)}) collective-permute-start(f32[25,128]{1,0:T(8,128)S(1)} %shard_map.90.after), channel_id=1, source_target_pairs={{2,4},{4,2},{6,8},{8,6},{10,12},{12,10},{14,16},{16,14},{18,20},{2... | collective-permute-start | bytes 38408 | tf_op jit(solution)/shard_map/ppermute | solution.py:501
